TPU v7x, 32 devices: a whole 2x2x4 slice. The times are simulated.
32 devices in a mesh: blk: 16 (over z, x, core), grp: 2 (over y).
Axes of the slice: x: 2, y: 2, z: 4, core: 2. Of those that a mesh axis runs over, the one named last changes fastest.
Arguments:
- embeddings: bfloat16 [32768, 1024], P(('blk', 'grp')), may hold values from -6 to 6
Outputs:
- tile_max: float32 [32768, 40], P(('blk', 'grp'))
All inputs are finite; a program needn't handle non-finite values.
Results may differ from a plain program's by a relative error of at most 0.0017.
Values may be sent and summed in bfloat16 or wider, within the bound.
No kernel may reach another device: no remote copies, remote signals or barrier semaphores. Data moves between devices by JAX's collectives and lax.ppermute only.
A program may use at most 64 MiB of HBM per device.

v0:
```python
import functools

import jax
import jax.numpy as jnp
from jax import lax
from jax.experimental import pallas as pl
from jax.experimental.pallas import tpu as pltpu
from jax.sharding import PartitionSpec as P


AXES = ("blk", "grp")
TILE = 128
STEP = 256
OFFSETS = 5
VMEM_LIMIT = 16 << 20
F32, BF16 = jnp.float32, jnp.bfloat16


def unit_of(rows):
    values = rows.astype(F32)
    mean = jnp.mean(values * values, axis=-1, keepdims=True)
    return (values * lax.rsqrt(mean + 1e-06)).astype(BF16)


def scores(left, right):
    return lax.dot_general(left, right, (((1,), (1,)), ((), ())), preferred_element_type=F32)


def best(scale, left, right, right_ref, right_at=0, left_ref=None, left_at=0, same=None):
    rows, keys = left.shape[0], right.shape[0]
    for m in range(0, rows, STEP):
        for n in range(0, keys, STEP):
            s = scores(left[m : m + STEP, :], right[n : n + STEP, :])
            if same is not None and m == n:
                s = jnp.where(same, -jnp.inf, s)
            tiles = jnp.max(s.reshape(STEP // TILE, TILE, STEP), axis=1)
            at = right_at + m // TILE
            right_ref[at : at + STEP // TILE, n : n + STEP] = tiles * scale
            if left_ref is not None:
                for t in range(STEP // TILE):
                    tile = jnp.max(s[:, t * TILE : (t + 1) * TILE], axis=1)
                    at = n // TILE + t
                    left_ref[at : at + 1, left_at + m : left_at + m + STEP] = tile.reshape(1, STEP) * scale


def place(role_ref):
    turn = lax.rem(role_ref[0], 4)
    step = lax.rem(lax.div(role_ref[0], 4), 2)
    return turn, step, jnp.logical_or(turn == 1, turn == 2)


def cut_kernel(at, rows_ref, cut_ref, sem):
    copy = pltpu.make_async_copy(rows_ref.at[at : at + cut_ref.shape[0], :], cut_ref, sem)
    copy.start()
    copy.wait()


def own_kernel(scale, high_ref, low_ref, unit_ref, own_ref):
    half = low_ref.shape[0]
    unit_ref[:half, :] = unit_of(low_ref[...])
    unit_ref[half:, :] = unit_of(high_ref[...])
    same = lax.broadcasted_iota(jnp.int32, (STEP, STEP), 0) == lax.broadcasted_iota(
        jnp.int32, (STEP, STEP), 1
    )
    best(scale, unit_ref, unit_ref, own_ref, same=same)


def partner_kernel(scale, rows_ref, unit_ref, partner_ref, max_ref):
    partner_ref[...] = unit_of(rows_ref[...])
    best(scale, partner_ref, unit_ref, max_ref)


def far_kernel(
    scale, rows_ref, unit_ref, partner_ref, far_ref, own_far_ref, far_own_ref, partner_far_ref
):
    far_ref[...] = unit_of(rows_ref[...])
    best(scale, far_ref, unit_ref, own_far_ref, left_ref=far_own_ref)
    best(scale, far_ref, partner_ref, partner_far_ref)


def last_kernel(
    scale, role_ref, even_ref, odd_ref, unit_ref, low_ref, high_ref, low_own_ref, high_own_ref,
    partner_low_ref, partner_high_ref, far_ref, beside_ref, cross_ref, tiles_ref, half_ref,
):
    _, step, middle = place(role_ref)
    half = half_ref.shape[0]
    across = half // TILE
    tiles = 2 * across
    far_ref[:tiles, :half] = low_own_ref[...]
    far_ref[:tiles, half:] = high_own_ref[...]

    @pl.when(jnp.logical_not(middle))
    def _():
        beside_ref[:across, :] = partner_low_ref[...]
        beside_ref[across:, :] = partner_high_ref[...]

    @pl.when(jnp.logical_and(step == 0, middle))
    def _():
        half_ref[...] = unit_of(even_ref[...])
        best(scale, half_ref, low_ref, far_ref.at[tiles:, :half], left_ref=beside_ref.at[:across, :half])
        best(scale, half_ref, high_ref, far_ref.at[tiles:, half:], left_ref=beside_ref.at[across:, :half])

    @pl.when(jnp.logical_and(step == 1, jnp.logical_not(middle)))
    def _():
        half_ref[...] = unit_of(odd_ref[...])
        best(scale, half_ref, unit_ref, tiles_ref, left_ref=cross_ref)


def join_kernel(
    role_ref, own_ref, own_partner_ref, own_low_ref, own_high_ref, tiles_ref, far_ref, beside_ref, cross_ref, out_ref
):
    turn, step, middle = place(role_ref)
    tiles, count = own_ref.shape
    half = count // 2

    def put(slots, *values):
        slot = slots[0]
        for i in range(1, 4):
            slot = jnp.where(turn == i, slots[i], slot)
        at = pl.multiple_of(slot * tiles, tiles)
        out_ref[pl.ds(at, tiles), :] = jnp.concatenate(values[1:], axis=values[0])

    put((2, 2, 2, 2), 0, own_ref[...])
    put((4, 4, 0, 0), 0, own_partner_ref[...])
    put((3, 0, 4, 1), 0, own_low_ref[...], own_high_ref[...])
    put((0, 1, 3, 4), 0, far_ref[:tiles, :])

    @pl.when(middle)
    def _():
        put((0, 3, 1, 0), 0, beside_ref[...])

    @pl.when(jnp.logical_and(jnp.logical_not(middle), step == 0))
    def _():
        put((1, 1, 1, 3), 1, beside_ref[:, :half], cross_ref[...])

    @pl.when(jnp.logical_and(jnp.logical_not(middle), step == 1))
    def _():
        put((1, 1, 1, 3), 0, far_ref[tiles:, :], tiles_ref[...])


def call(kernel, outs, *operands, scratch=(), source=False, last=False):
    specs, placed = [], []
    for value in operands:
        if value.dtype == jnp.int32:
            specs.append(pl.BlockSpec(memory_space=pltpu.SMEM))
            placed.append(value)
            continue
        space = pltpu.HBM if source else pltpu.VMEM
        specs.append(pl.BlockSpec(memory_space=space))
        placed.append(pltpu.with_memory_space_constraint(value, space))
    return pl.pallas_call(
        kernel,
        out_shape=[jax.ShapeDtypeStruct(*o) if last else pltpu.VMEM(*o) for o in outs],
        in_specs=specs,
        out_specs=[pl.BlockSpec(memory_space=pltpu.VMEM) for _ in outs],
        scratch_shapes=list(scratch),
        compiler_params=pltpu.CompilerParams(vmem_limit_bytes=VMEM_LIMIT),
    )(*placed)


def body(embeddings):
    count, width = embeddings.shape
    blocks = lax.axis_size(AXES[0]) * lax.axis_size(AXES[1])
    columns = blocks // 4
    assert blocks % 8 == 0 and count % (2 * STEP) == 0
    scale = 1.0 / width**0.5
    tiles, half = count // TILE, count // 2

    at = lambda column, turn: column % columns * 4 + turn
    far, swap, even, odd, beside, cross = [], [], [], [], [], []
    for q in range(columns):
        far += [(at(q, 1), at(q, 0)), (at(q, 2), at(q, 3))]
        far += [(at(q, 3), at(q + 1, 1)), (at(q, 0), at(q - 1, 2))]
        swap += [(at(q, 0), at(q, 2)), (at(q, 2), at(q, 0)), (at(q, 1), at(q, 3)), (at(q, 3), at(q, 1))]
        beside += [(at(q, 0), at(q, 2)), (at(q, 3), at(q, 1))]
        if q % 2 == 0:
            even += [(at(q, 0), at(q, 1)), (at(q, 3), at(q, 2))]
            beside += [(at(q, 1), at(q, 0)), (at(q, 2), at(q, 3))]
        else:
            odd += [(at(q, 1), at(q, 0)), (at(q, 2), at(q, 3))]
            cross += [(at(q, 0), at(q - 1, 3)), (at(q, 3), at(q + 1, 0))]

    def send(value, pairs):
        return lax.ppermute(value, AXES, pairs)

    role = lax.axis_index(AXES).astype(jnp.int32).reshape(1)
    role, embeddings = lax.optimization_barrier((role, embeddings))

    def cut(at):
        (part,) = call(
            functools.partial(cut_kernel, at),
            [((half, width), BF16)],
            embeddings,
            source=True,
            scratch=[pltpu.SemaphoreType.DMA],
        )
        return part

    high = cut(half)
    high_rows = send(high, far)
    high, embeddings = lax.optimization_barrier((high, embeddings))
    low = cut(0)
    low_rows = send(low, far)
    low, embeddings = lax.optimization_barrier((low, embeddings))
    partner_rows = send(embeddings, swap)
    unit, own = call(functools.partial(own_kernel, scale), [((count, width), BF16), ((tiles, count), F32)], high, low)
    partner, own_partner = call(
        functools.partial(partner_kernel, scale), [((count, width), BF16), ((tiles, count), F32)], partner_rows, unit
    )
    high_rows, low, own_partner = lax.optimization_barrier((high_rows, low, own_partner))
    odd_rows = send(high_rows, odd)
    even_rows = send(low, even)
    far_of = lambda rows: call(
        functools.partial(far_kernel, scale),
        [((half, width), BF16), ((tiles // 2, count), F32), ((tiles, half), F32), ((tiles // 2, count), F32)],
        rows,
        unit,
        partner,
    )
    high_unit, own_high, high_own, partner_high = far_of(high_rows)
    low_unit, own_low, low_own, partner_low = far_of(low_rows)
    far_max, beside_max, cross_max, half_tiles = call(
        functools.partial(last_kernel, scale),
        [
            ((tiles + tiles // 2, count), F32),
            ((tiles, count), F32),
            ((tiles, half), F32),
            ((tiles // 2, count), F32),
        ],
        role,
        even_rows,
        odd_rows,
        unit,
        low_unit,
        high_unit,
        low_own,
        high_own,
        partner_low,
        partner_high,
        scratch=[pltpu.VMEM((half, width), BF16)],
    )
    cross_max = send(cross_max, cross)
    far_max = send(far_max, [(b, a) for a, b in far])
    beside_max = send(beside_max, beside)
    (out,) = call(
        join_kernel,
        [((OFFSETS * tiles, count), F32)],
        role,
        own,
        own_partner,
        own_low,
        own_high,
        half_tiles,
        far_max,
        beside_max,
        cross_max,
        last=True,
    )
    return jnp.transpose(out)


def solution(mesh):
    return jax.shard_map(
        body,
        mesh=mesh,
        in_specs=(P(AXES, None),),
        out_specs=P(AXES, None),
        check_vma=False,
    )
```

profile of v0, /device:TPU:0, one launch (start us, length us, event | category | flops | bytes accessed | tf_op | source)
XLA Modules:
  0.0 56.4 jit_solution(1945646086909267958)
XLA Ops:
  0.0 1.2 %shard_map.17.high_ref = bf16[512,1024]{1,0:T(8,128)(2,1)S(1)} custom-call(bf16[1024,1024]{1,0:T(8,128)(2,1)} %rows_ref.1), custom_call_target="tpu_custom_call" | custom-call | tf_op jit(solution)/shard_map/pallas_call | solution.py:151
  1.2 0.0 copy-start
  1.3 1.4 %shard_map.18.low_ref = bf16[512,1024]{1,0:T(8,128)(2,1)S(1)} custom-call(bf16[1024,1024]{1,0:T(8,128)(2,1)} %rows_ref.1), custom_call_target="tpu_custom_call" | custom-call | tf_op jit(solution)/shard_map/pallas_call | solution.py:151
  2.6 0.5 copy-done
  3.2 0.5 collective-permute-start.1
  3.6 5.6 %collective-permute-start = (bf16[512,1024]{1,0:T(8,128)(2,1)S(1)}, bf16[512,1024]{1,0:T(8,128)(2,1)S(1)}, u32[]{:S(2)}, u32[]{:S(2)}) collective-permute-start(bf16[512,1024]{1,0:T(8,128)(2,1)S(1)} %shard_map.17.high_ref), channel_id=1, source_target_pairs={{1,0},{2,3},{3,5},{0,30},{5,4},{6,7},{7,9},{4,2},{9,8},{10,11},{11... | collective-permute-start | bytes 3145736 | tf_op jit(solution)/shard_map/ppermute | solution.py:184
  9.3 1.2 %collective-permute-start.2 = (bf16[512,1024]{1,0:T(8,128)(2,1)S(1)}, bf16[512,1024]{1,0:T(8,128)(2,1)S(1)}, u32[]{:S(2)}, u32[]{:S(2)}) collective-permute-start(bf16[512,1024]{1,0:T(8,128)(2,1)S(1)} %shard_map.18.low_ref), channel_id=1, source_target_pairs={{1,0},{2,3},{3,5},{0,30},{5,4},{6,7},{7,9},{4,2},{9,8},{10,11},{11... | collective-permute-start | bytes 3145736 | tf_op jit(solution)/shard_map/ppermute | solution.py:184
  10.5 2.9 %shard_map.19 = (bf16[1024,1024]{1,0:T(8,128)(2,1)S(1)}, f32[8,1024]{1,0:T(8,128)S(1)}) custom-call(bf16[512,1024]{1,0:T(8,128)(2,1)S(1)} %shard_map.17.high_ref, bf16[512,1024]{1,0:T(8,128)(2,1)S(1)} %shard_map.18.low_ref), custom_call_target="tpu_custom_call" | custom-call | tf_op jit(solution)/shard_map/pallas_call | solution.py:151
  13.4 0.0 collective-permute-done.1.rows_ref
  13.4 2.7 %shard_map.20 = (bf16[1024,1024]{1,0:T(8,128)(2,1)S(1)}, f32[8,1024]{1,0:T(8,128)S(1)}) custom-call(bf16[1024,1024]{1,0:T(8,128)(2,1)S(1)} %collective-permute-done.1.rows_ref, bf16[1024,1024]{1,0:T(8,128)(2,1)S(1)} %get-tuple-element.37.unit_ref), custom_call_target="tpu_custom_call" | custom-call | tf_op jit(solution)/shard_map/pallas_call | solution.py:151
  16.1 5.5 %collective-permute-done.rows_ref = bf16[512,1024]{1,0:T(8,128)(2,1)S(1)} collective-permute-done((bf16[512,1024]{1,0:T(8,128)(2,1)S(1)}, bf16[512,1024]{1,0:T(8,128)(2,1)S(1)}, u32[]{:S(2)}, u32[]{:S(2)}) %collective-permute-start) | collective-permute-done | bytes 1048608 | tf_op jit(solution)/shard_map/ppermute | solution.py:184
  21.6 3.6 %collective-permute-start.3 = (bf16[512,1024]{1,0:T(8,128)(2,1)S(1)}, bf16[512,1024]{1,0:T(8,128)(2,1)S(1)}, u32[]{:S(2)}, u32[]{:S(2)}) collective-permute-start(bf16[512,1024]{1,0:T(8,128)(2,1)S(1)} %shard_map.18.low_ref), channel_id=1, source_target_pairs={{0,1},{3,2},{8,9},{11,10},{16,17},{19,18},{24,25},{27,26}} | collective-permute-start | bytes 3145736 | tf_op jit(solution)/shard_map/ppermute | solution.py:184
  25.2 0.7 %collective-permute-start.4 = (bf16[512,1024]{1,0:T(8,128)(2,1)S(1)}, bf16[512,1024]{1,0:T(8,128)(2,1)S(1)}, u32[]{:S(2)}, u32[]{:S(2)}) collective-permute-start(bf16[512,1024]{1,0:T(8,128)(2,1)S(1)} %collective-permute-done.rows_ref), channel_id=1, source_target_pairs={{5,4},{6,7},{13,12},{14,15},{21,20},{22,23},{29,28},{30,31}} | collective-permute-start | bytes 3145736 | tf_op jit(solution)/shard_map/ppermute | solution.py:184
  26.0 2.7 %shard_map.22 = (bf16[512,1024]{1,0:T(8,128)(2,1)S(1)}, f32[4,1024]{1,0:T(4,128)S(1)}, f32[8,512]{1,0:T(8,128)S(1)}, f32[4,1024]{1,0:T(4,128)S(1)}) custom-call(bf16[512,1024]{1,0:T(8,128)(2,1)S(1)} %collective-permute-done.rows_ref, bf16[1024,1024]{1,0:T(8,128)(2,1)S(1)} %get-tuple-element.37.unit_ref, bf16[1024,1024]{1,0:T(8,128)(2,1)S(1)} %get-tuple-element.40.partner_ref), custom_call_target="tpu_custom_call" | custom-call | tf_op jit(solution)/shard_map/pallas_call | solution.py:151
  28.7 8.2 %collective-permute-done.2.rows_ref = bf16[512,1024]{1,0:T(8,128)(2,1)S(1)} collective-permute-done((bf16[512,1024]{1,0:T(8,128)(2,1)S(1)}, bf16[512,1024]{1,0:T(8,128)(2,1)S(1)}, u32[]{:S(2)}, u32[]{:S(2)}) %collective-permute-start.2) | collective-permute-done | bytes 1048608 | tf_op jit(solution)/shard_map/ppermute | solution.py:184
  36.8 2.7 %shard_map.21 = (bf16[512,1024]{1,0:T(8,128)(2,1)S(1)}, f32[4,1024]{1,0:T(4,128)S(1)}, f32[8,512]{1,0:T(8,128)S(1)}, f32[4,1024]{1,0:T(4,128)S(1)}) custom-call(bf16[512,1024]{1,0:T(8,128)(2,1)S(1)} %collective-permute-done.2.rows_ref, bf16[1024,1024]{1,0:T(8,128)(2,1)S(1)} %get-tuple-element.37.unit_ref, bf16[1024,1024]{1,0:T(8,128)(2,1)S(1)} %get-tuple-element.40.partner_ref), custom_call_target="tpu_custom_call" | custom-call | tf_op jit(solution)/shard_map/pallas_call | solution.py:151
  39.5 1.0 %collective-permute-done.3.even_ref = bf16[512,1024]{1,0:T(8,128)(2,1)S(1)} collective-permute-done((bf16[512,1024]{1,0:T(8,128)(2,1)S(1)}, bf16[512,1024]{1,0:T(8,128)(2,1)S(1)}, u32[]{:S(2)}, u32[]{:S(2)}) %collective-permute-start.3) | collective-permute-done | bytes 1048608 | tf_op jit(solution)/shard_map/ppermute | solution.py:184
  40.5 0.0 collective-permute-done.4.odd_ref
  40.5 4.1 %collective-permute-start.5 = (f32[12,1024]{1,0:T(8,128)S(1)}, f32[12,1024]{1,0:T(8,128)S(1)}, u32[]{:S(2)}, u32[]{:S(2)}) collective-permute-start(f32[12,1024]{1,0:T(8,128)S(1)} %get-tuple-element.52), channel_id=1, source_target_pairs={{0,1},{3,2},{5,3},{30,0},{4,5},{7,6},{9,7},{2,4},{8,9},{11,10},{13... | collective-permute-start | bytes 147464 | tf_op jit(solution)/shard_map/ppermute | solution.py:184
  44.6 2.5 %collective-permute-start.6 = (f32[8,1024]{1,0:T(8,128)S(1)}, f32[8,1024]{1,0:T(8,128)S(1)}, u32[]{:S(2)}, u32[]{:S(2)}) collective-permute-start(f32[8,1024]{1,0:T(8,128)S(1)} %get-tuple-element.53), channel_id=1, source_target_pairs={{0,2},{3,1},{1,0},{2,3},{4,6},{7,5},{8,10},{11,9},{9,8},{10,11},{1... | collective-permute-start | bytes 98312 | tf_op jit(solution)/shard_map/ppermute | solution.py:184
  47.1 1.3 %collective-permute-start.7 = (f32[8,512]{1,0:T(8,128)S(1)}, f32[8,512]{1,0:T(8,128)S(1)}, u32[]{:S(2)}, u32[]{:S(2)}) collective-permute-start(f32[8,512]{1,0:T(8,128)S(1)} %get-tuple-element.54), channel_id=1, source_target_pairs={{4,3},{7,8},{12,11},{15,16},{20,19},{23,24},{28,27},{31,0}} | collective-permute-start | bytes 49160 | tf_op jit(solution)/shard_map/ppermute | solution.py:184
  48.4 7.4 %collective-permute-done.7.cross_ref = f32[8,512]{1,0:T(8,128)S(1)} collective-permute-done((f32[8,512]{1,0:T(8,128)S(1)}, f32[8,512]{1,0:T(8,128)S(1)}, u32[]{:S(2)}, u32[]{:S(2)}) %collective-permute-start.7) | collective-permute-done | bytes 16416 | tf_op jit(solution)/shard_map/ppermute | solution.py:184
  55.7 0.0 collective-permute-done.6.beside_ref
  55.7 0.0 collective-permute-done.5.far_ref
  55.8 0.7 %shard_map.24 = f32[40,1024]{1,0:T(8,128)} custom-call(s32[1]{0:T(128)} %bitcast.role_ref, f32[8,1024]{1,0:T(8,128)S(1)} %get-tuple-element.35.own_ref, f32[8,1024]{1,0:T(8,128)S(1)} %get-tuple-element.39.own_partner_ref, f32[4,1024]{1,0:T(4,128)S(1)} %get-tuple-element.41.own_low_ref, f32[4,1024]{1,0:T(4,128)S(1)} %get-tuple-element.43.own_high_ref, ...), custom_call_target="tpu_custom_call" | custom-call | tf_op jit(solution)/shard_map/pallas_call | solution.py:151
  (1 shorter events, 0.0 us)
Async XLA Ops:
  1.2 1.9 %copy-start = (bf16[1024,1024]{1,0:T(8,128)(2,1)S(1)}, bf16[1024,1024]{1,0:T(8,128)(2,1)}, u32[]{:S(2)}) copy-start(bf16[1024,1024]{1,0:T(8,128)(2,1)} %rows_ref.1) | copy-start | bytes 6291460
  3.2 10.2 %collective-permute-start.1 = (bf16[1024,1024]{1,0:T(8,128)(2,1)S(1)}, bf16[1024,1024]{1,0:T(8,128)(2,1)S(1)}, u32[]{:S(2)}, u32[]{:S(2)}) collective-permute-start(bf16[1024,1024]{1,0:T(8,128)(2,1)S(1)} %copy-done), channel_id=1, source_target_pairs={{0,2},{2,0},{1,3},{3,1},{4,6},{6,4},{5,7},{7,5},{8,10},{10,8},{9,1... | collective-permute-start | bytes 6291464 | tf_op jit(solution)/shard_map/ppermute | solution.py:184
  3.6 17.9 %collective-permute-start = (bf16[512,1024]{1,0:T(8,128)(2,1)S(1)}, bf16[512,1024]{1,0:T(8,128)(2,1)S(1)}, u32[]{:S(2)}, u32[]{:S(2)}) collective-permute-start(bf16[512,1024]{1,0:T(8,128)(2,1)S(1)} %shard_map.17.high_ref), channel_id=1, source_target_pairs={{1,0},{2,3},{3,5},{0,30},{5,4},{6,7},{7,9},{4,2},{9,8},{10,11},{11... | collective-permute-start | bytes 3145736 | tf_op jit(solution)/shard_map/ppermute | solution.py:184
  9.3 27.6 %collective-permute-start.2 = (bf16[512,1024]{1,0:T(8,128)(2,1)S(1)}, bf16[512,1024]{1,0:T(8,128)(2,1)S(1)}, u32[]{:S(2)}, u32[]{:S(2)}) collective-permute-start(bf16[512,1024]{1,0:T(8,128)(2,1)S(1)} %shard_map.18.low_ref), channel_id=1, source_target_pairs={{1,0},{2,3},{3,5},{0,30},{5,4},{6,7},{7,9},{4,2},{9,8},{10,11},{11... | collective-permute-start | bytes 3145736 | tf_op jit(solution)/shard_map/ppermute | solution.py:184
  21.6 18.9 %collective-permute-start.3 = (bf16[512,1024]{1,0:T(8,128)(2,1)S(1)}, bf16[512,1024]{1,0:T(8,128)(2,1)S(1)}, u32[]{:S(2)}, u32[]{:S(2)}) collective-permute-start(bf16[512,1024]{1,0:T(8,128)(2,1)S(1)} %shard_map.18.low_ref), channel_id=1, source_target_pairs={{0,1},{3,2},{8,9},{11,10},{16,17},{19,18},{24,25},{27,26}} | collective-permute-start | bytes 3145736 | tf_op jit(solution)/shard_map/ppermute | solution.py:184
  25.2 15.2 %collective-permute-start.4 = (bf16[512,1024]{1,0:T(8,128)(2,1)S(1)}, bf16[512,1024]{1,0:T(8,128)(2,1)S(1)}, u32[]{:S(2)}, u32[]{:S(2)}) collective-permute-start(bf16[512,1024]{1,0:T(8,128)(2,1)S(1)} %collective-permute-done.rows_ref), channel_id=1, source_target_pairs={{5,4},{6,7},{13,12},{14,15},{21,20},{22,23},{29,28},{30,31}} | collective-permute-start | bytes 3145736 | tf_op jit(solution)/shard_map/ppermute | solution.py:184
  40.5 15.2 %collective-permute-start.5 = (f32[12,1024]{1,0:T(8,128)S(1)}, f32[12,1024]{1,0:T(8,128)S(1)}, u32[]{:S(2)}, u32[]{:S(2)}) collective-permute-start(f32[12,1024]{1,0:T(8,128)S(1)} %get-tuple-element.52), channel_id=1, source_target_pairs={{0,1},{3,2},{5,3},{30,0},{4,5},{7,6},{9,7},{2,4},{8,9},{11,10},{13... | collective-permute-start | bytes 147464 | tf_op jit(solution)/shard_map/ppermute | solution.py:184
  44.6 11.1 %collective-permute-start.6 = (f32[8,1024]{1,0:T(8,128)S(1)}, f32[8,1024]{1,0:T(8,128)S(1)}, u32[]{:S(2)}, u32[]{:S(2)}) collective-permute-start(f32[8,1024]{1,0:T(8,128)S(1)} %get-tuple-element.53), channel_id=1, source_target_pairs={{0,2},{3,1},{1,0},{2,3},{4,6},{7,5},{8,10},{11,9},{9,8},{10,11},{1... | collective-permute-start | bytes 98312 | tf_op jit(solution)/shard_map/ppermute | solution.py:184
  47.1 8.7 %collective-permute-start.7 = (f32[8,512]{1,0:T(8,128)S(1)}, f32[8,512]{1,0:T(8,128)S(1)}, u32[]{:S(2)}, u32[]{:S(2)}) collective-permute-start(f32[8,512]{1,0:T(8,128)S(1)} %get-tuple-element.54), channel_id=1, source_target_pairs={{4,3},{7,8},{12,11},{15,16},{20,19},{23,24},{28,27},{31,0}} | collective-permute-start | bytes 49160 | tf_op jit(solution)/shard_map/ppermute | solution.py:184
where the time goes:
time: 56.7 us; the launch traced here: 56.4 us
  waiting for transfers between devices  22 us (39%)
  starting transfers between devices  19.6 us (35%)
  Pallas kernels  14.2 us (25%)
    ppermute x8, waiting for transfers between devices, send(): return lax.ppermute(value, AXES, pairs)  22 us
    ppermute x8, starting transfers between devices, send(): return lax.ppermute(value, AXES, pairs)  19.6 us
    pallas_call x8, Pallas kernels, call(): pl.pallas_call(kernel, out_shape=[jax.ShapeDtypeStruct(*o) if last else p...  14.2 us
  transfers between devices with their start and end apart: 8, of which 4 were waited for; matrix products, arithmetic and copies ran while one was open for 0% of the time, Pallas kernels for 19%

commit v1 on v0

--- a/solution.py
+++ b/solution.py
@@ -39,8 +39,8 @@
             if left_ref is not None:
                 for t in range(STEP // TILE):
                     tile = jnp.max(s[:, t * TILE : (t + 1) * TILE], axis=1)
-                    at = n // TILE + t
-                    left_ref[at : at + 1, left_at + m : left_at + m + STEP] = tile.reshape(1, STEP) * scale
+                    at = left_at + n // TILE + t
+                    left_ref[at : at + 1, m : m + STEP] = tile.reshape(1, STEP) * scale
 
 
 def place(role_ref):
@@ -78,27 +78,30 @@
     best(scale, far_ref, partner_ref, partner_far_ref)
 
 
+def low_kernel(
+    scale, rows_ref, unit_ref, partner_ref, own_high_ref, high_own_ref, partner_high_ref,
+    far_ref, own_far_ref, far_own_ref, partner_far_ref,
+):
+    half = rows_ref.shape[0]
+    across = half // TILE
+    far_kernel(scale, rows_ref, unit_ref, partner_ref, far_ref, own_far_ref, far_own_ref, partner_far_ref)
+    own_far_ref[across:, :] = own_high_ref[...]
+    far_own_ref[:, half:] = high_own_ref[...]
+    partner_far_ref[across:, :] = partner_high_ref[...]
+
+
 def last_kernel(
-    scale, role_ref, even_ref, odd_ref, unit_ref, low_ref, high_ref, low_own_ref, high_own_ref,
-    partner_low_ref, partner_high_ref, far_ref, beside_ref, cross_ref, tiles_ref, half_ref,
+    scale, role_ref, even_ref, odd_ref, unit_ref, low_ref, high_ref, rows_ref, cross_ref, tiles_ref, half_ref
 ):
     _, step, middle = place(role_ref)
     half = half_ref.shape[0]
     across = half // TILE
-    tiles = 2 * across
-    far_ref[:tiles, :half] = low_own_ref[...]
-    far_ref[:tiles, half:] = high_own_ref[...]
-
-    @pl.when(jnp.logical_not(middle))
-    def _():
-        beside_ref[:across, :] = partner_low_ref[...]
-        beside_ref[across:, :] = partner_high_ref[...]
 
     @pl.when(jnp.logical_and(step == 0, middle))
     def _():
         half_ref[...] = unit_of(even_ref[...])
-        best(scale, half_ref, low_ref, far_ref.at[tiles:, :half], left_ref=beside_ref.at[:across, :half])
-        best(scale, half_ref, high_ref, far_ref.at[tiles:, half:], left_ref=beside_ref.at[across:, :half])
+        best(scale, half_ref, low_ref, cross_ref, left_ref=rows_ref)
+        best(scale, half_ref, high_ref, cross_ref, right_at=across, left_ref=rows_ref, left_at=across)
 
     @pl.when(jnp.logical_and(step == 1, jnp.logical_not(middle)))
     def _():
@@ -107,11 +110,11 @@
 
 
 def join_kernel(
-    role_ref, own_ref, own_partner_ref, own_low_ref, own_high_ref, tiles_ref, far_ref, beside_ref, cross_ref, out_ref
+    role_ref, own_ref, own_partner_ref, own_far_ref, far_ref, beside_ref, tiles_ref, rows_ref, cross_ref, out_ref
 ):
     turn, step, middle = place(role_ref)
-    tiles, count = own_ref.shape
-    half = count // 2
+    tiles, _ = own_ref.shape
+    across = tiles // 2
 
     def put(slots, *values):
         slot = slots[0]
@@ -122,8 +125,8 @@
 
     put((2, 2, 2, 2), 0, own_ref[...])
     put((4, 4, 0, 0), 0, own_partner_ref[...])
-    put((3, 0, 4, 1), 0, own_low_ref[...], own_high_ref[...])
-    put((0, 1, 3, 4), 0, far_ref[:tiles, :])
+    put((3, 0, 4, 1), 0, own_far_ref[...])
+    put((0, 1, 3, 4), 0, far_ref[...])
 
     @pl.when(middle)
     def _():
@@ -131,11 +134,12 @@
 
     @pl.when(jnp.logical_and(jnp.logical_not(middle), step == 0))
     def _():
-        put((1, 1, 1, 3), 1, beside_ref[:, :half], cross_ref[...])
+        put((1, 1, 1, 3), 1, rows_ref[...], cross_ref[...])
 
     @pl.when(jnp.logical_and(jnp.logical_not(middle), step == 1))
     def _():
-        put((1, 1, 1, 3), 0, far_ref[tiles:, :], tiles_ref[...])
+        low = jnp.concatenate([cross_ref[:across, :], cross_ref[across:, :]], axis=1)
+        put((1, 1, 1, 3), 0, low, tiles_ref[...])
 
 
 def call(kernel, outs, *operands, scratch=(), source=False, last=False):
@@ -165,17 +169,20 @@
     assert blocks % 8 == 0 and count % (2 * STEP) == 0
     scale = 1.0 / width**0.5
     tiles, half = count // TILE, count // 2
+    across = half // TILE
 
     at = lambda column, turn: column % columns * 4 + turn
-    far, swap, even, odd, beside, cross = [], [], [], [], [], []
+    far, back, swap, even, odd, beside, rows, cross = [], [], [], [], [], [], [], []
     for q in range(columns):
         far += [(at(q, 1), at(q, 0)), (at(q, 2), at(q, 3))]
         far += [(at(q, 3), at(q + 1, 1)), (at(q, 0), at(q - 1, 2))]
         swap += [(at(q, 0), at(q, 2)), (at(q, 2), at(q, 0)), (at(q, 1), at(q, 3)), (at(q, 3), at(q, 1))]
         beside += [(at(q, 0), at(q, 2)), (at(q, 3), at(q, 1))]
+        back += [(b, a) for a, b in far[-4:]]
         if q % 2 == 0:
             even += [(at(q, 0), at(q, 1)), (at(q, 3), at(q, 2))]
-            beside += [(at(q, 1), at(q, 0)), (at(q, 2), at(q, 3))]
+            rows += [(at(q, 1), at(q, 0)), (at(q, 2), at(q, 3))]
+            cross += [(at(q, 1), at(q - 1, 3)), (at(q, 2), at(q + 1, 0))]
         else:
             odd += [(at(q, 1), at(q, 0)), (at(q, 2), at(q, 3))]
             cross += [(at(q, 0), at(q - 1, 3)), (at(q, 3), at(q + 1, 0))]
@@ -207,52 +214,53 @@
     partner, own_partner = call(
         functools.partial(partner_kernel, scale), [((count, width), BF16), ((tiles, count), F32)], partner_rows, unit
     )
-    high_rows, low, own_partner = lax.optimization_barrier((high_rows, low, own_partner))
+    high_rows, own_partner = lax.optimization_barrier((high_rows, own_partner))
     odd_rows = send(high_rows, odd)
-    even_rows = send(low, even)
-    far_of = lambda rows: call(
+    high_unit, own_high, high_own, partner_high = call(
         functools.partial(far_kernel, scale),
-        [((half, width), BF16), ((tiles // 2, count), F32), ((tiles, half), F32), ((tiles // 2, count), F32)],
-        rows,
+        [((half, width), BF16), ((across, count), F32), ((tiles, half), F32), ((across, count), F32)],
+        high_rows,
         unit,
         partner,
     )
-    high_unit, own_high, high_own, partner_high = far_of(high_rows)
-    low_unit, own_low, low_own, partner_low = far_of(low_rows)
-    far_max, beside_max, cross_max, half_tiles = call(
+    low, own_high = lax.optimization_barrier((low, own_high))
+    even_rows = send(low, even)
+    low_unit, own_far, far_own, partner_far = call(
+        functools.partial(low_kernel, scale),
+        [((half, width), BF16)] + [((tiles, count), F32)] * 3,
+        low_rows,
+        unit,
+        partner,
+        own_high,
+        high_own,
+        partner_high,
+    )
+    far_max = send(far_own, back)
+    beside_max = send(partner_far, beside)
+    rows_max, cross_max, half_tiles = call(
         functools.partial(last_kernel, scale),
-        [
-            ((tiles + tiles // 2, count), F32),
-            ((tiles, count), F32),
-            ((tiles, half), F32),
-            ((tiles // 2, count), F32),
-        ],
+        [((tiles, half), F32), ((tiles, half), F32), ((across, count), F32)],
         role,
         even_rows,
         odd_rows,
         unit,
         low_unit,
         high_unit,
-        low_own,
-        high_own,
-        partner_low,
-        partner_high,
         scratch=[pltpu.VMEM((half, width), BF16)],
     )
+    rows_max = send(rows_max, rows)
     cross_max = send(cross_max, cross)
-    far_max = send(far_max, [(b, a) for a, b in far])
-    beside_max = send(beside_max, beside)
     (out,) = call(
         join_kernel,
         [((OFFSETS * tiles, count), F32)],
         role,
         own,
         own_partner,
-        own_low,
-        own_high,
-        half_tiles,
+        own_far,
         far_max,
         beside_max,
+        half_tiles,
+        rows_max,
         cross_max,
         last=True,
     )

time: 56.7 us -> 53.2 us (0.938)
  starting transfers between devices: 19.6 us -> 16.6 us
    ppermute x8 -> x9, starting transfers between devices: 19.6 us -> 16.6 us  [send(): return lax.ppermute(value, AXES, pairs)]
    ppermute x8 -> x9, waiting for transfers between devices: 22 us -> 22 us  [send(): return lax.ppermute(value, AXES, pairs)]
  transfers between devices with their start and end apart: 8 -> 9, of which waited for: 4 -> 5; matrix products, arithmetic and copies ran while one was open for 0% -> 0% of each run, Pallas kernels for 19% -> 20%
where the time goes in v1:
time: 53.2 us; the launch traced here: 53 us
  waiting for transfers between devices  22 us (41%)
  starting transfers between devices  16.6 us (31%)
  Pallas kernels  13.7 us (26%)
    ppermute x9, waiting for transfers between devices, send(): return lax.ppermute(value, AXES, pairs)  22 us
    ppermute x9, starting transfers between devices, send(): return lax.ppermute(value, AXES, pairs)  16.6 us
    pallas_call x8, Pallas kernels, call(): pl.pallas_call(kernel, out_shape=[jax.ShapeDtypeStruct(*o) if last else p...  13.7 us
  transfers between devices with their start and end apart: 9, of which 5 were waited for; matrix products, arithmetic and copies ran while one was open for 0% of the time, Pallas kernels for 20%

profile of v1, /device:TPU:0, one launch (start us, length us, event | category | flops | bytes accessed | tf_op | source)
XLA Modules:
  0.0 53.0 jit_solution(14523386550933167636)
XLA Ops:
  0.0 1.2 %shard_map.17.high_ref = bf16[512,1024]{1,0:T(8,128)(2,1)S(1)} custom-call(bf16[1024,1024]{1,0:T(8,128)(2,1)} %rows_ref.1), custom_call_target="tpu_custom_call" | custom-call | tf_op jit(solution)/shard_map/pallas_call | solution.py:155
  1.2 0.0 copy-start
  1.3 1.4 %shard_map.18.low_ref = bf16[512,1024]{1,0:T(8,128)(2,1)S(1)} custom-call(bf16[1024,1024]{1,0:T(8,128)(2,1)} %rows_ref.1), custom_call_target="tpu_custom_call" | custom-call | tf_op jit(solution)/shard_map/pallas_call | solution.py:155
  2.6 0.5 copy-done
  3.2 0.5 collective-permute-start.1
  3.6 5.6 %collective-permute-start = (bf16[512,1024]{1,0:T(8,128)(2,1)S(1)}, bf16[512,1024]{1,0:T(8,128)(2,1)S(1)}, u32[]{:S(2)}, u32[]{:S(2)}) collective-permute-start(bf16[512,1024]{1,0:T(8,128)(2,1)S(1)} %shard_map.17.high_ref), channel_id=1, source_target_pairs={{1,0},{2,3},{3,5},{0,30},{5,4},{6,7},{7,9},{4,2},{9,8},{10,11},{11... | collective-permute-start | bytes 3145736 | tf_op jit(solution)/shard_map/ppermute | solution.py:191
  9.3 1.2 %collective-permute-start.2 = (bf16[512,1024]{1,0:T(8,128)(2,1)S(1)}, bf16[512,1024]{1,0:T(8,128)(2,1)S(1)}, u32[]{:S(2)}, u32[]{:S(2)}) collective-permute-start(bf16[512,1024]{1,0:T(8,128)(2,1)S(1)} %shard_map.18.low_ref), channel_id=1, source_target_pairs={{1,0},{2,3},{3,5},{0,30},{5,4},{6,7},{7,9},{4,2},{9,8},{10,11},{11... | collective-permute-start | bytes 3145736 | tf_op jit(solution)/shard_map/ppermute | solution.py:191
  10.5 2.8 %shard_map.19 = (bf16[1024,1024]{1,0:T(8,128)(2,1)S(1)}, f32[8,1024]{1,0:T(8,128)S(1)}) custom-call(bf16[512,1024]{1,0:T(8,128)(2,1)S(1)} %shard_map.17.high_ref, bf16[512,1024]{1,0:T(8,128)(2,1)S(1)} %shard_map.18.low_ref), custom_call_target="tpu_custom_call" | custom-call | tf_op jit(solution)/shard_map/pallas_call | solution.py:155
  13.3 0.0 collective-permute-done.1.rows_ref
  13.3 2.6 %shard_map.20 = (bf16[1024,1024]{1,0:T(8,128)(2,1)S(1)}, f32[8,1024]{1,0:T(8,128)S(1)}) custom-call(bf16[1024,1024]{1,0:T(8,128)(2,1)S(1)} %collective-permute-done.1.rows_ref, bf16[1024,1024]{1,0:T(8,128)(2,1)S(1)} %get-tuple-element.37.unit_ref), custom_call_target="tpu_custom_call" | custom-call | tf_op jit(solution)/shard_map/pallas_call | solution.py:155
  15.9 5.6 %collective-permute-done.rows_ref = bf16[512,1024]{1,0:T(8,128)(2,1)S(1)} collective-permute-done((bf16[512,1024]{1,0:T(8,128)(2,1)S(1)}, bf16[512,1024]{1,0:T(8,128)(2,1)S(1)}, u32[]{:S(2)}, u32[]{:S(2)}) %collective-permute-start) | collective-permute-done | bytes 1048608 | tf_op jit(solution)/shard_map/ppermute | solution.py:191
  21.6 0.7 %collective-permute-start.6 = (bf16[512,1024]{1,0:T(8,128)(2,1)S(1)}, bf16[512,1024]{1,0:T(8,128)(2,1)S(1)}, u32[]{:S(2)}, u32[]{:S(2)}) collective-permute-start(bf16[512,1024]{1,0:T(8,128)(2,1)S(1)} %collective-permute-done.rows_ref), channel_id=1, source_target_pairs={{5,4},{6,7},{13,12},{14,15},{21,20},{22,23},{29,28},{30,31}} | collective-permute-start | bytes 3145736 | tf_op jit(solution)/shard_map/ppermute | solution.py:191
  22.3 2.5 %shard_map.21 = (bf16[512,1024]{1,0:T(8,128)(2,1)S(1)}, f32[4,1024]{1,0:T(4,128)S(1)}, f32[8,512]{1,0:T(8,128)S(1)}, f32[4,1024]{1,0:T(4,128)S(1)}) custom-call(bf16[512,1024]{1,0:T(8,128)(2,1)S(1)} %collective-permute-done.rows_ref, bf16[1024,1024]{1,0:T(8,128)(2,1)S(1)} %get-tuple-element.37.unit_ref, bf16[1024,1024]{1,0:T(8,128)(2,1)S(1)} %get-tuple-element.40.partner_ref), custom_call_target="tpu_custom_call" | custom-call | tf_op jit(solution)/shard_map/pallas_call | solution.py:155
  24.8 3.7 %collective-permute-start.5 = (bf16[512,1024]{1,0:T(8,128)(2,1)S(1)}, bf16[512,1024]{1,0:T(8,128)(2,1)S(1)}, u32[]{:S(2)}, u32[]{:S(2)}) collective-permute-start(bf16[512,1024]{1,0:T(8,128)(2,1)S(1)} %shard_map.18.low_ref), channel_id=1, source_target_pairs={{0,1},{3,2},{8,9},{11,10},{16,17},{19,18},{24,25},{27,26}} | collective-permute-start | bytes 3145736 | tf_op jit(solution)/shard_map/ppermute | solution.py:191
  28.5 5.1 %collective-permute-done.2.rows_ref = bf16[512,1024]{1,0:T(8,128)(2,1)S(1)} collective-permute-done((bf16[512,1024]{1,0:T(8,128)(2,1)S(1)}, bf16[512,1024]{1,0:T(8,128)(2,1)S(1)}, u32[]{:S(2)}, u32[]{:S(2)}) %collective-permute-start.2) | collective-permute-done | bytes 1048608 | tf_op jit(solution)/shard_map/ppermute | solution.py:191
  33.6 2.5 %shard_map.22 = (bf16[512,1024]{1,0:T(8,128)(2,1)S(1)}, f32[8,1024]{1,0:T(8,128)S(1)}, f32[8,1024]{1,0:T(8,128)S(1)}, f32[8,1024]{1,0:T(8,128)S(1)}) custom-call(bf16[512,1024]{1,0:T(8,128)(2,1)S(1)} %collective-permute-done.2.rows_ref, bf16[1024,1024]{1,0:T(8,128)(2,1)S(1)} %get-tuple-element.37.unit_ref, ...), custom_call_target="tpu_custom_call" | custom-call | tf_op jit(solution)/shard_map/pallas_call | solution.py:155
  36.1 1.0 %collective-permute-start.3 = (f32[8,1024]{1,0:T(8,128)S(1)}, f32[8,1024]{1,0:T(8,128)S(1)}, u32[]{:S(2)}, u32[]{:S(2)}) collective-permute-start(f32[8,1024]{1,0:T(8,128)S(1)} %get-tuple-element.47), channel_id=1, source_target_pairs={{0,1},{3,2},{5,3},{30,0},{4,5},{7,6},{9,7},{2,4},{8,9},{11,10},{13... | collective-permute-start | bytes 98312 | tf_op jit(solution)/shard_map/ppermute | solution.py:191
  37.1 1.3 %collective-permute-start.4 = (f32[8,1024]{1,0:T(8,128)S(1)}, f32[8,1024]{1,0:T(8,128)S(1)}, u32[]{:S(2)}, u32[]{:S(2)}) collective-permute-start(f32[8,1024]{1,0:T(8,128)S(1)} %get-tuple-element.48), channel_id=1, source_target_pairs={{0,2},{3,1},{4,6},{7,5},{8,10},{11,9},{12,14},{15,13},{16,18},{19,... | collective-permute-start | bytes 98312 | tf_op jit(solution)/shard_map/ppermute | solution.py:191
  38.4 0.0 collective-permute-done.6.odd_ref
  38.4 2.3 %collective-permute-done.5.even_ref = bf16[512,1024]{1,0:T(8,128)(2,1)S(1)} collective-permute-done((bf16[512,1024]{1,0:T(8,128)(2,1)S(1)}, bf16[512,1024]{1,0:T(8,128)(2,1)S(1)}, u32[]{:S(2)}, u32[]{:S(2)}) %collective-permute-start.5) | collective-permute-done | bytes 1048608 | tf_op jit(solution)/shard_map/ppermute | solution.py:191
  40.7 1.3 %collective-permute-start.7 = (f32[8,512]{1,0:T(8,128)S(1)}, f32[8,512]{1,0:T(8,128)S(1)}, u32[]{:S(2)}, u32[]{:S(2)}) collective-permute-start(f32[8,512]{1,0:T(8,128)S(1)} %get-tuple-element.53), channel_id=1, source_target_pairs={{1,0},{2,3},{9,8},{10,11},{17,16},{18,19},{25,24},{26,27}} | collective-permute-start | bytes 49160 | tf_op jit(solution)/shard_map/ppermute | solution.py:191
  42.0 1.3 %collective-permute-start.8 = (f32[8,512]{1,0:T(8,128)S(1)}, f32[8,512]{1,0:T(8,128)S(1)}, u32[]{:S(2)}, u32[]{:S(2)}) collective-permute-start(f32[8,512]{1,0:T(8,128)S(1)} %get-tuple-element.54), channel_id=1, source_target_pairs={{1,31},{2,4},{4,3},{7,8},{9,7},{10,12},{12,11},{15,16},{17,15},{18... | collective-permute-start | bytes 49160 | tf_op jit(solution)/shard_map/ppermute | solution.py:191
  43.3 0.0 collective-permute-done.3.far_ref
  43.3 0.0 collective-permute-done.4.beside_ref
  43.3 4.4 %collective-permute-done.7.rows_ref = f32[8,512]{1,0:T(8,128)S(1)} collective-permute-done((f32[8,512]{1,0:T(8,128)S(1)}, f32[8,512]{1,0:T(8,128)S(1)}, u32[]{:S(2)}, u32[]{:S(2)}) %collective-permute-start.7) | collective-permute-done | bytes 16416 | tf_op jit(solution)/shard_map/ppermute | solution.py:191
  47.7 4.5 %collective-permute-done.8.cross_ref = f32[8,512]{1,0:T(8,128)S(1)} collective-permute-done((f32[8,512]{1,0:T(8,128)S(1)}, f32[8,512]{1,0:T(8,128)S(1)}, u32[]{:S(2)}, u32[]{:S(2)}) %collective-permute-start.8) | collective-permute-done | bytes 16416 | tf_op jit(solution)/shard_map/ppermute | solution.py:191
  52.3 0.7 %shard_map.24 = f32[40,1024]{1,0:T(8,128)} custom-call(s32[1]{0:T(128)} %bitcast.role_ref, f32[8,1024]{1,0:T(8,128)S(1)} %get-tuple-element.35.own_ref, f32[8,1024]{1,0:T(8,128)S(1)} %get-tuple-element.39.own_partner_ref, f32[8,1024]{1,0:T(8,128)S(1)} %get-tuple-element.46.own_far_ref, f32[8,1024]{1,0:T(8,128)S(1)} %collective-permute-done.3.far_ref, ...), custom_call_target="tpu_custom_call" | custom-call | tf_op jit(solution)/shard_map/pallas_call | solution.py:155
  (1 shorter events, 0.0 us)
Async XLA Ops:
  1.2 1.9 %copy-start = (bf16[1024,1024]{1,0:T(8,128)(2,1)S(1)}, bf16[1024,1024]{1,0:T(8,128)(2,1)}, u32[]{:S(2)}) copy-start(bf16[1024,1024]{1,0:T(8,128)(2,1)} %rows_ref.1) | copy-start | bytes 6291460
  3.2 10.2 %collective-permute-start.1 = (bf16[1024,1024]{1,0:T(8,128)(2,1)S(1)}, bf16[1024,1024]{1,0:T(8,128)(2,1)S(1)}, u32[]{:S(2)}, u32[]{:S(2)}) collective-permute-start(bf16[1024,1024]{1,0:T(8,128)(2,1)S(1)} %copy-done), channel_id=1, source_target_pairs={{0,2},{2,0},{1,3},{3,1},{4,6},{6,4},{5,7},{7,5},{8,10},{10,8},{9,1... | collective-permute-start | bytes 6291464 | tf_op jit(solution)/shard_map/ppermute | solution.py:191
  3.6 17.9 %collective-permute-start = (bf16[512,1024]{1,0:T(8,128)(2,1)S(1)}, bf16[512,1024]{1,0:T(8,128)(2,1)S(1)}, u32[]{:S(2)}, u32[]{:S(2)}) collective-permute-start(bf16[512,1024]{1,0:T(8,128)(2,1)S(1)} %shard_map.17.high_ref), channel_id=1, source_target_pairs={{1,0},{2,3},{3,5},{0,30},{5,4},{6,7},{7,9},{4,2},{9,8},{10,11},{11... | collective-permute-start | bytes 3145736 | tf_op jit(solution)/shard_map/ppermute | solution.py:191
  9.3 24.3 %collective-permute-start.2 = (bf16[512,1024]{1,0:T(8,128)(2,1)S(1)}, bf16[512,1024]{1,0:T(8,128)(2,1)S(1)}, u32[]{:S(2)}, u32[]{:S(2)}) collective-permute-start(bf16[512,1024]{1,0:T(8,128)(2,1)S(1)} %shard_map.18.low_ref), channel_id=1, source_target_pairs={{1,0},{2,3},{3,5},{0,30},{5,4},{6,7},{7,9},{4,2},{9,8},{10,11},{11... | collective-permute-start | bytes 3145736 | tf_op jit(solution)/shard_map/ppermute | solution.py:191
  21.6 16.8 %collective-permute-start.6 = (bf16[512,1024]{1,0:T(8,128)(2,1)S(1)}, bf16[512,1024]{1,0:T(8,128)(2,1)S(1)}, u32[]{:S(2)}, u32[]{:S(2)}) collective-permute-start(bf16[512,1024]{1,0:T(8,128)(2,1)S(1)} %collective-permute-done.rows_ref), channel_id=1, source_target_pairs={{5,4},{6,7},{13,12},{14,15},{21,20},{22,23},{29,28},{30,31}} | collective-permute-start | bytes 3145736 | tf_op jit(solution)/shard_map/ppermute | solution.py:191
  24.8 15.9 %collective-permute-start.5 = (bf16[512,1024]{1,0:T(8,128)(2,1)S(1)}, bf16[512,1024]{1,0:T(8,128)(2,1)S(1)}, u32[]{:S(2)}, u32[]{:S(2)}) collective-permute-start(bf16[512,1024]{1,0:T(8,128)(2,1)S(1)} %shard_map.18.low_ref), channel_id=1, source_target_pairs={{0,1},{3,2},{8,9},{11,10},{16,17},{19,18},{24,25},{27,26}} | collective-permute-start | bytes 3145736 | tf_op jit(solution)/shard_map/ppermute | solution.py:191
  36.1 7.2 %collective-permute-start.3 = (f32[8,1024]{1,0:T(8,128)S(1)}, f32[8,1024]{1,0:T(8,128)S(1)}, u32[]{:S(2)}, u32[]{:S(2)}) collective-permute-start(f32[8,1024]{1,0:T(8,128)S(1)} %get-tuple-element.47), channel_id=1, source_target_pairs={{0,1},{3,2},{5,3},{30,0},{4,5},{7,6},{9,7},{2,4},{8,9},{11,10},{13... | collective-permute-start | bytes 98312 | tf_op jit(solution)/shard_map/ppermute | solution.py:191
  37.1 6.2 %collective-permute-start.4 = (f32[8,1024]{1,0:T(8,128)S(1)}, f32[8,1024]{1,0:T(8,128)S(1)}, u32[]{:S(2)}, u32[]{:S(2)}) collective-permute-start(f32[8,1024]{1,0:T(8,128)S(1)} %get-tuple-element.48), channel_id=1, source_target_pairs={{0,2},{3,1},{4,6},{7,5},{8,10},{11,9},{12,14},{15,13},{16,18},{19,... | collective-permute-start | bytes 98312 | tf_op jit(solution)/shard_map/ppermute | solution.py:191
  40.7 7.0 %collective-permute-start.7 = (f32[8,512]{1,0:T(8,128)S(1)}, f32[8,512]{1,0:T(8,128)S(1)}, u32[]{:S(2)}, u32[]{:S(2)}) collective-permute-start(f32[8,512]{1,0:T(8,128)S(1)} %get-tuple-element.53), channel_id=1, source_target_pairs={{1,0},{2,3},{9,8},{10,11},{17,16},{18,19},{25,24},{26,27}} | collective-permute-start | bytes 49160 | tf_op jit(solution)/shard_map/ppermute | solution.py:191
  42.0 10.2 %collective-permute-start.8 = (f32[8,512]{1,0:T(8,128)S(1)}, f32[8,512]{1,0:T(8,128)S(1)}, u32[]{:S(2)}, u32[]{:S(2)}) collective-permute-start(f32[8,512]{1,0:T(8,128)S(1)} %get-tuple-element.54), channel_id=1, source_target_pairs={{1,31},{2,4},{4,3},{7,8},{9,7},{10,12},{12,11},{15,16},{17,15},{18... | collective-permute-start | bytes 49160 | tf_op jit(solution)/shard_map/ppermute | solution.py:191

commit v2 on v1

v2 whole, which is shorter than its diff:
```python
import functools

import jax
import jax.numpy as jnp
from jax import lax
from jax.experimental import pallas as pl
from jax.experimental.pallas import tpu as pltpu
from jax.sharding import PartitionSpec as P


AXES = ("blk", "grp")
TILE = 128
STEP = 256
PARTS = 2
OFFSETS = 5
VMEM_LIMIT = 16 << 20
F32, BF16 = jnp.float32, jnp.bfloat16


def unit_of(rows):
    values = rows.astype(F32)
    mean = jnp.mean(values * values, axis=-1, keepdims=True)
    return (values * lax.rsqrt(mean + 1e-06)).astype(BF16)


def scores(left, right):
    return lax.dot_general(left, right, (((1,), (1,)), ((), ())), preferred_element_type=F32)


def best(scale, left, right, right_ref, right_at=0, left_ref=None, left_at=0, left_from=0, same=None):
    rows, keys = left.shape[0], right.shape[0]
    for m in range(0, rows, STEP):
        for n in range(0, keys, STEP):
            s = scores(left[m : m + STEP, :], right[n : n + STEP, :])
            if same is not None and m == n:
                s = jnp.where(same, -jnp.inf, s)
            tiles = jnp.max(s.reshape(STEP // TILE, TILE, STEP), axis=1)
            at = right_at + m // TILE
            right_ref[at : at + STEP // TILE, n : n + STEP] = tiles * scale
            if left_ref is not None:
                for t in range(STEP // TILE):
                    tile = jnp.max(s[:, t * TILE : (t + 1) * TILE], axis=1)
                    at = left_at + n // TILE + t
                    left_ref[at : at + 1, left_from + m : left_from + m + STEP] = tile.reshape(1, STEP) * scale


def place(role_ref):
    turn = lax.rem(role_ref[0], 4)
    step = lax.rem(lax.div(role_ref[0], 4), 2)
    return turn, step, jnp.logical_or(turn == 1, turn == 2)


def own_kernel(scale, rows_ref, unit_ref, own_ref):
    unit_ref[...] = unit_of(rows_ref[...])
    same = lax.broadcasted_iota(jnp.int32, (STEP, STEP), 0) == lax.broadcasted_iota(
        jnp.int32, (STEP, STEP), 1
    )
    best(scale, unit_ref, unit_ref, own_ref, same=same)


def partner_kernel(role_ref, rows_ref, unit_ref, partner_ref, *part_refs):
    middle = place(role_ref)[2]
    size = part_refs[0].shape[0]
    half = size * len(part_refs)
    partner_ref[...] = unit_of(rows_ref[...])
    for i, part_ref in enumerate(part_refs):
        at = i * size

        @pl.when(middle)
        def _():
            part_ref[...] = partner_ref[at : at + size, :]

        @pl.when(jnp.logical_not(middle))
        def _():
            part_ref[...] = unit_ref[half + at : half + at + size, :]


def pair_kernel(scale, unit_ref, partner_ref, max_ref):
    best(scale, partner_ref, unit_ref, max_ref)


def far_kernel(scale, role_ref, rows_ref, unit_ref, partner_ref, far_ref, own_far_ref, far_max_ref):
    middle = place(role_ref)[2]
    tiles = own_far_ref.shape[0]
    far_ref[...] = unit_of(rows_ref[...])
    best(scale, far_ref, unit_ref, own_far_ref, left_ref=far_max_ref)

    @pl.when(jnp.logical_not(middle))
    def _():
        best(scale, partner_ref, far_ref, far_max_ref, right_at=tiles)


def part_kernel(scale, first, role_ref, part_ref, unit_ref, far_ref, *refs):
    _, step, middle = place(role_ref)
    rows_ref, cross_ref, tiles_ref = refs[-3:]
    count = unit_ref.shape[0]
    half, across = count // 2, count // 2 // TILE
    inside = jnp.logical_and(step == 0, middle)
    outside = jnp.logical_and(step == 1, jnp.logical_not(middle))
    at = first // TILE

    if first:
        old_rows_ref, old_cross_ref, old_tiles_ref = refs[:3]

        @pl.when(inside)
        def _():
            rows_ref[:, :first] = old_rows_ref[:, :first]
            cross_ref[:at, :] = old_cross_ref[:at, :]
            cross_ref[across : across + at, :] = old_cross_ref[across : across + at, :]

        @pl.when(outside)
        def _():
            cross_ref[:, :first] = old_cross_ref[:, :first]
            tiles_ref[:at, :] = old_tiles_ref[:at, :]

    @pl.when(inside)
    def _():
        best(scale, part_ref, far_ref.at[:half, :], cross_ref, right_at=at, left_ref=rows_ref, left_from=first)
        best(
            scale, part_ref, far_ref.at[half:, :], cross_ref, right_at=across + at,
            left_ref=rows_ref, left_at=across, left_from=first,
        )

    @pl.when(outside)
    def _():
        best(scale, part_ref, unit_ref, tiles_ref, right_at=at, left_ref=cross_ref, left_from=first)


def join_kernel(
    role_ref, own_ref, own_partner_ref, own_far_ref, far_ref, tiles_ref, rows_ref, cross_ref, out_ref
):
    turn, step, middle = place(role_ref)
    tiles, _ = own_ref.shape
    across = tiles // 2

    def put(slots, *values):
        slot = slots[0]
        for i in range(1, 4):
            slot = jnp.where(turn == i, slots[i], slot)
        at = pl.multiple_of(slot * tiles, tiles)
        out_ref[pl.ds(at, tiles), :] = jnp.concatenate(values[1:], axis=values[0])

    put((2, 2, 2, 2), 0, own_ref[...])
    put((4, 4, 0, 0), 0, own_partner_ref[...])
    put((3, 0, 4, 1), 0, own_far_ref[...])
    put((0, 1, 3, 4), 0, far_ref[:tiles, :])

    @pl.when(middle)
    def _():
        put((0, 3, 1, 0), 0, far_ref[tiles:, :])

    @pl.when(jnp.logical_and(jnp.logical_not(middle), step == 0))
    def _():
        put((1, 1, 1, 3), 1, rows_ref[...], cross_ref[...])

    @pl.when(jnp.logical_and(jnp.logical_not(middle), step == 1))
    def _():
        low = jnp.concatenate([cross_ref[:across, :], cross_ref[across:, :]], axis=1)
        put((1, 1, 1, 3), 0, low, tiles_ref[...])


def call(kernel, outs, *operands, last=False):
    specs, placed = [], []
    for value in operands:
        scalar = value.dtype == jnp.int32
        specs.append(pl.BlockSpec(memory_space=pltpu.SMEM if scalar else pltpu.VMEM))
        placed.append(value if scalar else pltpu.with_memory_space_constraint(value, pltpu.VMEM))
    return pl.pallas_call(
        kernel,
        out_shape=[jax.ShapeDtypeStruct(*o) if last else pltpu.VMEM(*o) for o in outs],
        in_specs=specs,
        out_specs=[pl.BlockSpec(memory_space=pltpu.VMEM) for _ in outs],
        compiler_params=pltpu.CompilerParams(vmem_limit_bytes=VMEM_LIMIT),
    )(*placed)


def body(embeddings):
    count, width = embeddings.shape
    blocks = lax.axis_size(AXES[0]) * lax.axis_size(AXES[1])
    columns = blocks // 4
    scale = 1.0 / width**0.5
    tiles, half = count // TILE, count // 2
    across, size = half // TILE, half // PARTS
    assert blocks % 8 == 0 and size % STEP == 0

    at = lambda column, turn: column % columns * 4 + turn
    far, swap, parts, rows, cross = [], [], [], [], []
    for q in range(columns):
        far += [(at(q, 1), at(q, 0)), (at(q, 2), at(q, 3))]
        far += [(at(q, 3), at(q + 1, 1)), (at(q, 0), at(q - 1, 2))]
        swap += [(at(q, 0), at(q, 2)), (at(q, 2), at(q, 0)), (at(q, 1), at(q, 3)), (at(q, 3), at(q, 1))]
        if q % 2 == 0:
            parts += [(at(q, 1), at(q, 2)), (at(q, 2), at(q, 1))]
            parts += [(at(q, 3), at(q + 1, 0)), (at(q, 0), at(q - 1, 3))]
            rows += [(at(q, 1), at(q, 0)), (at(q, 2), at(q, 3))]
            cross += [(at(q, 1), at(q - 1, 3)), (at(q, 2), at(q + 1, 0))]
        else:
            cross += [(at(q, 0), at(q - 1, 3)), (at(q, 3), at(q + 1, 0))]

    def send(value, pairs):
        return lax.ppermute(value, AXES, pairs)

    role = lax.axis_index(AXES).astype(jnp.int32).reshape(1)
    role, embeddings = lax.optimization_barrier((role, embeddings))
    far_rows = send(embeddings, far)
    partner_rows = send(embeddings, swap)
    unit, own = call(functools.partial(own_kernel, scale), [((count, width), BF16), ((tiles, count), F32)], embeddings)
    partner, *pieces = call(
        partner_kernel, [((count, width), BF16)] + [((size, width), BF16)] * PARTS, role, partner_rows, unit
    )
    pieces = [send(piece, parts) for piece in pieces]
    (own_partner,) = call(functools.partial(pair_kernel, scale), [((tiles, count), F32)], unit, partner)
    far_unit, own_far, far_max = call(
        functools.partial(far_kernel, scale),
        [((count, width), BF16), ((tiles, count), F32), ((2 * tiles, count), F32)],
        role,
        far_rows,
        unit,
        partner,
    )
    far_max = send(far_max, [(b, a) for a, b in far])
    done = []
    for i, piece in enumerate(pieces):
        done = call(
            functools.partial(part_kernel, scale, i * size),
            [((tiles, half), F32), ((tiles, half), F32), ((across, count), F32)],
            role,
            piece,
            unit,
            far_unit,
            *done,
        )
    rows_max, cross_max, half_tiles = done
    rows_max = send(rows_max, rows)
    cross_max = send(cross_max, cross)
    (out,) = call(
        join_kernel,
        [((OFFSETS * tiles, count), F32)],
        role,
        own,
        own_partner,
        own_far,
        far_max,
        half_tiles,
        rows_max,
        cross_max,
        last=True,
    )
    return jnp.transpose(out)


def solution(mesh):
    return jax.shard_map(
        body,
        mesh=mesh,
        in_specs=(P(AXES, None),),
        out_specs=P(AXES, None),
        check_vma=False,
    )
```

time: 53.2 us -> 52.5 us (0.987)
  starting transfers between devices: 16.6 us -> 13 us
  waiting for transfers between devices: 22 us -> 25.5 us
  Pallas kernels: 13.7 us -> 12.1 us
  local copies, waits for them, and re-layouts: 0.51 us -> 1.62 us
    ppermute x9 -> x7, starting transfers between devices: 16.6 us -> 13 us  [send(): return lax.ppermute(value, AXES, pairs)]
    ppermute x9 -> x7, waiting for transfers between devices: 22 us -> 25.5 us  [send(): return lax.ppermute(value, AXES, pairs)]
    pallas_call x8 -> x7, Pallas kernels: 13.7 us -> 12.1 us  [call(): pl.pallas_call(kernel, out_shape=[jax.ShapeDtypeStruct(*o) if last else p...]
    unnamed x2, local copies, waits for them, and re-layouts: 0.51 us -> 1.62 us
  transfers between devices with their start and end apart: 9 -> 7, of which waited for: 5 -> 4; matrix products, arithmetic and copies ran while one was open for 0% -> 0% of each run, Pallas kernels for 20% -> 22%
where the time goes in v2:
time: 52.5 us; the launch traced here: 52.3 us
  waiting for transfers between devices  25.5 us (49%)
  starting transfers between devices  13 us (25%)
  Pallas kernels  12.1 us (23%)
  local copies, waits for them, and re-layouts  1.62 us (3%)
    ppermute x7, waiting for transfers between devices, send(): return lax.ppermute(value, AXES, pairs)  25.5 us
    ppermute x7, starting transfers between devices, send(): return lax.ppermute(value, AXES, pairs)  13 us
    pallas_call x7, Pallas kernels, call(): pl.pallas_call(kernel, out_shape=[jax.ShapeDtypeStruct(*o) if last else p...  12.1 us
    unnamed x2, local copies, waits for them, and re-layouts  1.62 us
  transfers between devices with their start and end apart: 7, of which 4 were waited for; matrix products, arithmetic and copies ran while one was open for 0% of the time, Pallas kernels for 22%

profile of v2, /device:TPU:0, one launch (start us, length us, event | category | flops | bytes accessed | tf_op | source)
XLA Modules:
  0.0 52.3 jit_solution(15755780778391009832)
XLA Ops:
  0.0 0.5 collective-permute-start
  0.5 5.6 %collective-permute-start.1 = (bf16[1024,1024]{1,0:T(8,128)(2,1)}, bf16[1024,1024]{1,0:T(8,128)(2,1)S(1)}, u32[]{:S(2)}, u32[]{:S(2)}) collective-permute-start(bf16[1024,1024]{1,0:T(8,128)(2,1)} %rows_ref), channel_id=1, source_target_pairs={{1,0},{2,3},{3,5},{0,30},{5,4},{6,7},{7,9},{4,2},{9,8},{10,11},{11... | collective-permute-start | bytes 6291464 | tf_op jit(solution)/shard_map/ppermute | solution.py:201
  6.1 0.0 copy-start
  6.1 1.6 %copy-done = bf16[1024,1024]{1,0:T(8,128)(2,1)S(1)} copy-done((bf16[1024,1024]{1,0:T(8,128)(2,1)S(1)}, bf16[1024,1024]{1,0:T(8,128)(2,1)}, u32[]{:S(2)}) %copy-start) | copy-done | bytes 2097176
  7.7 2.9 %shard_map.17 = (bf16[1024,1024]{1,0:T(8,128)(2,1)S(1)}, f32[8,1024]{1,0:T(8,128)S(1)}) custom-call(bf16[1024,1024]{1,0:T(8,128)(2,1)S(1)} %copy-done), custom_call_target="tpu_custom_call" | custom-call | tf_op jit(solution)/shard_map/pallas_call | solution.py:168
  10.6 0.0 collective-permute-done.rows_ref
  10.6 0.7 %shard_map.18 = (bf16[1024,1024]{1,0:T(8,128)(2,1)S(1)}, bf16[256,1024]{1,0:T(8,128)(2,1)S(1)}, bf16[256,1024]{1,0:T(8,128)(2,1)S(1)}) custom-call(s32[1]{0:T(128)} %bitcast.role_ref, bf16[1024,1024]{1,0:T(8,128)(2,1)S(1)} %collective-permute-done.rows_ref, bf16[1024,1024]{1,0:T(8,128)(2,1)S(1)} %get-tuple-element.24.unit_ref), custom_call_target="tpu_custom_call" | custom-call | tf_op jit(solution)/shard_map/pallas_call | solution.py:168
  11.3 2.9 %collective-permute-start.4 = (bf16[256,1024]{1,0:T(8,128)(2,1)S(1)}, bf16[256,1024]{1,0:T(8,128)(2,1)S(1)}, u32[]{:S(2)}, u32[]{:S(2)}) collective-permute-start(bf16[256,1024]{1,0:T(8,128)(2,1)S(1)} %get-tuple-element.30), channel_id=1, source_target_pairs={{1,2},{2,1},{3,4},{0,31},{9,10},{10,9},{11,12},{8,7},{17,18},{18,1... | collective-permute-start | bytes 1572872 | tf_op jit(solution)/shard_map/ppermute | solution.py:201
  14.3 1.3 %collective-permute-start.3 = (bf16[256,1024]{1,0:T(8,128)(2,1)S(1)}, bf16[256,1024]{1,0:T(8,128)(2,1)S(1)}, u32[]{:S(2)}, u32[]{:S(2)}) collective-permute-start(bf16[256,1024]{1,0:T(8,128)(2,1)S(1)} %get-tuple-element.28), channel_id=1, source_target_pairs={{1,2},{2,1},{3,4},{0,31},{9,10},{10,9},{11,12},{8,7},{17,18},{18,1... | collective-permute-start | bytes 1572872 | tf_op jit(solution)/shard_map/ppermute | solution.py:201
  15.6 14.4 %collective-permute-done.1.rows_ref = bf16[1024,1024]{1,0:T(8,128)(2,1)S(1)} collective-permute-done((bf16[1024,1024]{1,0:T(8,128)(2,1)}, bf16[1024,1024]{1,0:T(8,128)(2,1)S(1)}, u32[]{:S(2)}, u32[]{:S(2)}) %collective-permute-start.1) | collective-permute-done | bytes 2097184 | tf_op jit(solution)/shard_map/ppermute | solution.py:201
  30.0 5.4 %shard_map.20 = (bf16[1024,1024]{1,0:T(8,128)(2,1)S(1)}, f32[8,1024]{1,0:T(8,128)S(1)}, f32[16,1024]{1,0:T(8,128)S(1)}) custom-call(s32[1]{0:T(128)} %bitcast.role_ref, bf16[1024,1024]{1,0:T(8,128)(2,1)S(1)} %collective-permute-done.1.rows_ref, bf16[1024,1024]{1,0:T(8,128)(2,1)S(1)} %get-tuple-element.24.unit_ref, ...), custom_call_target="tpu_custom_call" | custom-call | tf_op jit(solution)/shard_map/pallas_call | solution.py:168
  35.4 0.1 collective-permute-start.2
  35.5 0.0 collective-permute-done.4.part_ref
  35.5 5.6 %collective-permute-done.3.part_ref = bf16[256,1024]{1,0:T(8,128)(2,1)S(1)} collective-permute-done((bf16[256,1024]{1,0:T(8,128)(2,1)S(1)}, bf16[256,1024]{1,0:T(8,128)(2,1)S(1)}, u32[]{:S(2)}, u32[]{:S(2)}) %collective-permute-start.3) | collective-permute-done | bytes 524320 | tf_op jit(solution)/shard_map/ppermute | solution.py:201
  41.1 1.3 %collective-permute-start.5 = (f32[8,512]{1,0:T(8,128)S(1)}, f32[8,512]{1,0:T(8,128)S(1)}, u32[]{:S(2)}, u32[]{:S(2)}) collective-permute-start(f32[8,512]{1,0:T(8,128)S(1)} %get-tuple-element.35), channel_id=1, source_target_pairs={{1,0},{2,3},{9,8},{10,11},{17,16},{18,19},{25,24},{26,27}} | collective-permute-start | bytes 49160 | tf_op jit(solution)/shard_map/ppermute | solution.py:201
  42.4 1.3 %collective-permute-start.6 = (f32[8,512]{1,0:T(8,128)S(1)}, f32[8,512]{1,0:T(8,128)S(1)}, u32[]{:S(2)}, u32[]{:S(2)}) collective-permute-start(f32[8,512]{1,0:T(8,128)S(1)} %get-tuple-element.36), channel_id=1, source_target_pairs={{1,31},{2,4},{4,3},{7,8},{9,7},{10,12},{12,11},{15,16},{17,15},{18... | collective-permute-start | bytes 49160 | tf_op jit(solution)/shard_map/ppermute | solution.py:201
  43.7 2.4 %shard_map.19.own_partner_ref = f32[8,1024]{1,0:T(8,128)S(1)} custom-call(bf16[1024,1024]{1,0:T(8,128)(2,1)S(1)} %get-tuple-element.24.unit_ref, bf16[1024,1024]{1,0:T(8,128)(2,1)S(1)} %get-tuple-element.25.partner_ref), custom_call_target="tpu_custom_call" | custom-call | tf_op jit(solution)/shard_map/pallas_call | solution.py:168
  46.1 0.0 collective-permute-done.2.far_ref
  46.1 0.6 %collective-permute-done.5.rows_ref = f32[8,512]{1,0:T(8,128)S(1)} collective-permute-done((f32[8,512]{1,0:T(8,128)S(1)}, f32[8,512]{1,0:T(8,128)S(1)}, u32[]{:S(2)}, u32[]{:S(2)}) %collective-permute-start.5) | collective-permute-done | bytes 16416 | tf_op jit(solution)/shard_map/ppermute | solution.py:201
  46.7 4.9 %collective-permute-done.6.cross_ref = f32[8,512]{1,0:T(8,128)S(1)} collective-permute-done((f32[8,512]{1,0:T(8,128)S(1)}, f32[8,512]{1,0:T(8,128)S(1)}, u32[]{:S(2)}, u32[]{:S(2)}) %collective-permute-start.6) | collective-permute-done | bytes 16416 | tf_op jit(solution)/shard_map/ppermute | solution.py:201
  51.6 0.7 %shard_map.23 = f32[40,1024]{1,0:T(8,128)} custom-call(s32[1]{0:T(128)} %bitcast.role_ref, f32[8,1024]{1,0:T(8,128)S(1)} %get-tuple-element.23.own_ref, f32[8,1024]{1,0:T(8,128)S(1)} %shard_map.19.own_partner_ref, f32[8,1024]{1,0:T(8,128)S(1)} %get-tuple-element.26.own_far_ref, f32[16,1024]{1,0:T(8,128)S(1)} %collective-permute-done.2.far_ref, ...), custom_call_target="tpu_custom_call" | custom-call | tf_op jit(solution)/shard_map/pallas_call | solution.py:168
  (2 shorter events, 0.0 us)
Async XLA Ops:
  0.0 10.6 %collective-permute-start = (bf16[1024,1024]{1,0:T(8,128)(2,1)}, bf16[1024,1024]{1,0:T(8,128)(2,1)S(1)}, u32[]{:S(2)}, u32[]{:S(2)}) collective-permute-start(bf16[1024,1024]{1,0:T(8,128)(2,1)} %rows_ref), channel_id=1, source_target_pairs={{0,2},{2,0},{1,3},{3,1},{4,6},{6,4},{5,7},{7,5},{8,10},{10,8},{9,1... | collective-permute-start | bytes 6291464 | tf_op jit(solution)/shard_map/ppermute | solution.py:201
  0.5 29.5 %collective-permute-start.1 = (bf16[1024,1024]{1,0:T(8,128)(2,1)}, bf16[1024,1024]{1,0:T(8,128)(2,1)S(1)}, u32[]{:S(2)}, u32[]{:S(2)}) collective-permute-start(bf16[1024,1024]{1,0:T(8,128)(2,1)} %rows_ref), channel_id=1, source_target_pairs={{1,0},{2,3},{3,5},{0,30},{5,4},{6,7},{7,9},{4,2},{9,8},{10,11},{11... | collective-permute-start | bytes 6291464 | tf_op jit(solution)/shard_map/ppermute | solution.py:201
  6.1 1.6 %copy-start = (bf16[1024,1024]{1,0:T(8,128)(2,1)S(1)}, bf16[1024,1024]{1,0:T(8,128)(2,1)}, u32[]{:S(2)}) copy-start(bf16[1024,1024]{1,0:T(8,128)(2,1)} %rows_ref) | copy-start | bytes 6291460
  11.3 24.2 %collective-permute-start.4 = (bf16[256,1024]{1,0:T(8,128)(2,1)S(1)}, bf16[256,1024]{1,0:T(8,128)(2,1)S(1)}, u32[]{:S(2)}, u32[]{:S(2)}) collective-permute-start(bf16[256,1024]{1,0:T(8,128)(2,1)S(1)} %get-tuple-element.30), channel_id=1, source_target_pairs={{1,2},{2,1},{3,4},{0,31},{9,10},{10,9},{11,12},{8,7},{17,18},{18,1... | collective-permute-start | bytes 1572872 | tf_op jit(solution)/shard_map/ppermute | solution.py:201
  14.3 26.9 %collective-permute-start.3 = (bf16[256,1024]{1,0:T(8,128)(2,1)S(1)}, bf16[256,1024]{1,0:T(8,128)(2,1)S(1)}, u32[]{:S(2)}, u32[]{:S(2)}) collective-permute-start(bf16[256,1024]{1,0:T(8,128)(2,1)S(1)} %get-tuple-element.28), channel_id=1, source_target_pairs={{1,2},{2,1},{3,4},{0,31},{9,10},{10,9},{11,12},{8,7},{17,18},{18,1... | collective-permute-start | bytes 1572872 | tf_op jit(solution)/shard_map/ppermute | solution.py:201
  35.4 10.7 %collective-permute-start.2 = (f32[16,1024]{1,0:T(8,128)S(1)}, f32[16,1024]{1,0:T(8,128)S(1)}, u32[]{:S(2)}, u32[]{:S(2)}) collective-permute-start(f32[16,1024]{1,0:T(8,128)S(1)} %get-tuple-element.27), channel_id=1, source_target_pairs={{0,1},{3,2},{5,3},{30,0},{4,5},{7,6},{9,7},{2,4},{8,9},{11,10},{13... | collective-permute-start | bytes 196616 | tf_op jit(solution)/shard_map/ppermute | solution.py:201
  41.1 5.6 %collective-permute-start.5 = (f32[8,512]{1,0:T(8,128)S(1)}, f32[8,512]{1,0:T(8,128)S(1)}, u32[]{:S(2)}, u32[]{:S(2)}) collective-permute-start(f32[8,512]{1,0:T(8,128)S(1)} %get-tuple-element.35), channel_id=1, source_target_pairs={{1,0},{2,3},{9,8},{10,11},{17,16},{18,19},{25,24},{26,27}} | collective-permute-start | bytes 49160 | tf_op jit(solution)/shard_map/ppermute | solution.py:201
  42.4 9.2 %collective-permute-start.6 = (f32[8,512]{1,0:T(8,128)S(1)}, f32[8,512]{1,0:T(8,128)S(1)}, u32[]{:S(2)}, u32[]{:S(2)}) collective-permute-start(f32[8,512]{1,0:T(8,128)S(1)} %get-tuple-element.36), channel_id=1, source_target_pairs={{1,31},{2,4},{4,3},{7,8},{9,7},{10,12},{12,11},{15,16},{17,15},{18... | collective-permute-start | bytes 49160 | tf_op jit(solution)/shard_map/ppermute | solution.py:201

commit v3 on v2

--- a/solution.py
+++ b/solution.py
@@ -127,7 +127,7 @@
 
 
 def join_kernel(
-    role_ref, own_ref, own_partner_ref, own_far_ref, far_ref, tiles_ref, rows_ref, cross_ref, out_ref
+    role_ref, own_ref, own_partner_ref, own_far_ref, far_ref, tiles_ref, rows_ref, cross_ref, ends_ref, out_ref
 ):
     turn, step, middle = place(role_ref)
     tiles, _ = own_ref.shape
@@ -155,7 +155,7 @@
 
     @pl.when(jnp.logical_and(jnp.logical_not(middle), step == 1))
     def _():
-        low = jnp.concatenate([cross_ref[:across, :], cross_ref[across:, :]], axis=1)
+        low = jnp.concatenate([ends_ref[:across, :], ends_ref[across:, :]], axis=1)
         put((1, 1, 1, 3), 0, low, tiles_ref[...])
 
 
@@ -184,7 +184,7 @@
     assert blocks % 8 == 0 and size % STEP == 0
 
     at = lambda column, turn: column % columns * 4 + turn
-    far, swap, parts, rows, cross = [], [], [], [], []
+    far, swap, parts, rows, cross, ends = [], [], [], [], [], []
     for q in range(columns):
         far += [(at(q, 1), at(q, 0)), (at(q, 2), at(q, 3))]
         far += [(at(q, 3), at(q + 1, 1)), (at(q, 0), at(q - 1, 2))]
@@ -193,7 +193,7 @@
             parts += [(at(q, 1), at(q, 2)), (at(q, 2), at(q, 1))]
             parts += [(at(q, 3), at(q + 1, 0)), (at(q, 0), at(q - 1, 3))]
             rows += [(at(q, 1), at(q, 0)), (at(q, 2), at(q, 3))]
-            cross += [(at(q, 1), at(q - 1, 3)), (at(q, 2), at(q + 1, 0))]
+            ends += [(at(q, 1), at(q - 1, 3)), (at(q, 2), at(q + 1, 0))]
         else:
             cross += [(at(q, 0), at(q - 1, 3)), (at(q, 3), at(q + 1, 0))]
 
@@ -231,6 +231,7 @@
             *done,
         )
     rows_max, cross_max, half_tiles = done
+    ends_max = send(cross_max, ends)
     rows_max = send(rows_max, rows)
     cross_max = send(cross_max, cross)
     (out,) = call(
@@ -244,6 +245,7 @@
         half_tiles,
         rows_max,
         cross_max,
+        ends_max,
         last=True,
     )
     return jnp.transpose(out)

time: 52.5 us -> 52.5 us (level); the launches traced: 52.3 us -> 51.8 us
  waiting for transfers between devices: 25.5 us -> 24.3 us
  starting transfers between devices: 13 us -> 13.6 us
    ppermute x7 -> x8, waiting for transfers between devices: 25.5 us -> 24.3 us  [send(): return lax.ppermute(value, AXES, pairs)]
    ppermute x7 -> x8, starting transfers between devices: 13 us -> 13.6 us  [send(): return lax.ppermute(value, AXES, pairs)]
  transfers between devices with their start and end apart: 7 -> 8, of which waited for: 4 -> 3; matrix products, arithmetic and copies ran while one was open for 0% -> 0% of each run, Pallas kernels for 22% -> 22%
where the time goes in v3:
time: 52.5 us; the launch traced here: 51.8 us
  waiting for transfers between devices  24.3 us (46%)
  starting transfers between devices  13.6 us (26%)
  Pallas kernels  12.1 us (23%)
  local copies, waits for them, and re-layouts  1.62 us (3%)
    ppermute x8, waiting for transfers between devices, send(): return lax.ppermute(value, AXES, pairs)  24.3 us
    ppermute x8, starting transfers between devices, send(): return lax.ppermute(value, AXES, pairs)  13.6 us
    pallas_call x7, Pallas kernels, call(): pl.pallas_call(kernel, out_shape=[jax.ShapeDtypeStruct(*o) if last else p...  12.1 us
    unnamed x2, local copies, waits for them, and re-layouts  1.62 us
  transfers between devices with their start and end apart: 8, of which 3 were waited for; matrix products, arithmetic and copies ran while one was open for 0% of the time, Pallas kernels for 22%

profile of v3, /device:TPU:0, one launch (start us, length us, event | category | flops | bytes accessed | tf_op | source)
XLA Modules:
  0.0 51.8 jit_solution(4950300045802083054)
XLA Ops:
  0.0 0.5 collective-permute-start
  0.5 5.6 %collective-permute-start.1 = (bf16[1024,1024]{1,0:T(8,128)(2,1)}, bf16[1024,1024]{1,0:T(8,128)(2,1)S(1)}, u32[]{:S(2)}, u32[]{:S(2)}) collective-permute-start(bf16[1024,1024]{1,0:T(8,128)(2,1)} %rows_ref), channel_id=1, source_target_pairs={{1,0},{2,3},{3,5},{0,30},{5,4},{6,7},{7,9},{4,2},{9,8},{10,11},{11... | collective-permute-start | bytes 6291464 | tf_op jit(solution)/shard_map/ppermute | solution.py:201
  6.1 0.0 copy-start
  6.1 1.6 %copy-done = bf16[1024,1024]{1,0:T(8,128)(2,1)S(1)} copy-done((bf16[1024,1024]{1,0:T(8,128)(2,1)S(1)}, bf16[1024,1024]{1,0:T(8,128)(2,1)}, u32[]{:S(2)}) %copy-start) | copy-done | bytes 2097176
  7.7 2.9 %shard_map.17 = (bf16[1024,1024]{1,0:T(8,128)(2,1)S(1)}, f32[8,1024]{1,0:T(8,128)S(1)}) custom-call(bf16[1024,1024]{1,0:T(8,128)(2,1)S(1)} %copy-done), custom_call_target="tpu_custom_call" | custom-call | tf_op jit(solution)/shard_map/pallas_call | solution.py:168
  10.6 0.0 collective-permute-done.rows_ref
  10.6 0.7 %shard_map.18 = (bf16[1024,1024]{1,0:T(8,128)(2,1)S(1)}, bf16[256,1024]{1,0:T(8,128)(2,1)S(1)}, bf16[256,1024]{1,0:T(8,128)(2,1)S(1)}) custom-call(s32[1]{0:T(128)} %bitcast.role_ref, bf16[1024,1024]{1,0:T(8,128)(2,1)S(1)} %collective-permute-done.rows_ref, bf16[1024,1024]{1,0:T(8,128)(2,1)S(1)} %get-tuple-element.24.unit_ref), custom_call_target="tpu_custom_call" | custom-call | tf_op jit(solution)/shard_map/pallas_call | solution.py:168
  11.3 2.9 %collective-permute-start.4 = (bf16[256,1024]{1,0:T(8,128)(2,1)S(1)}, bf16[256,1024]{1,0:T(8,128)(2,1)S(1)}, u32[]{:S(2)}, u32[]{:S(2)}) collective-permute-start(bf16[256,1024]{1,0:T(8,128)(2,1)S(1)} %get-tuple-element.30), channel_id=1, source_target_pairs={{1,2},{2,1},{3,4},{0,31},{9,10},{10,9},{11,12},{8,7},{17,18},{18,1... | collective-permute-start | bytes 1572872 | tf_op jit(solution)/shard_map/ppermute | solution.py:201
  14.3 1.3 %collective-permute-start.3 = (bf16[256,1024]{1,0:T(8,128)(2,1)S(1)}, bf16[256,1024]{1,0:T(8,128)(2,1)S(1)}, u32[]{:S(2)}, u32[]{:S(2)}) collective-permute-start(bf16[256,1024]{1,0:T(8,128)(2,1)S(1)} %get-tuple-element.28), channel_id=1, source_target_pairs={{1,2},{2,1},{3,4},{0,31},{9,10},{10,9},{11,12},{8,7},{17,18},{18,1... | collective-permute-start | bytes 1572872 | tf_op jit(solution)/shard_map/ppermute | solution.py:201
  15.6 14.4 %collective-permute-done.1.rows_ref = bf16[1024,1024]{1,0:T(8,128)(2,1)S(1)} collective-permute-done((bf16[1024,1024]{1,0:T(8,128)(2,1)}, bf16[1024,1024]{1,0:T(8,128)(2,1)S(1)}, u32[]{:S(2)}, u32[]{:S(2)}) %collective-permute-start.1) | collective-permute-done | bytes 2097184 | tf_op jit(solution)/shard_map/ppermute | solution.py:201
  30.0 5.4 %shard_map.20 = (bf16[1024,1024]{1,0:T(8,128)(2,1)S(1)}, f32[8,1024]{1,0:T(8,128)S(1)}, f32[16,1024]{1,0:T(8,128)S(1)}) custom-call(s32[1]{0:T(128)} %bitcast.role_ref, bf16[1024,1024]{1,0:T(8,128)(2,1)S(1)} %collective-permute-done.1.rows_ref, bf16[1024,1024]{1,0:T(8,128)(2,1)S(1)} %get-tuple-element.24.unit_ref, ...), custom_call_target="tpu_custom_call" | custom-call | tf_op jit(solution)/shard_map/pallas_call | solution.py:168
  35.4 0.1 collective-permute-start.2
  35.5 0.0 collective-permute-done.4.part_ref
  35.5 5.6 %collective-permute-done.3.part_ref = bf16[256,1024]{1,0:T(8,128)(2,1)S(1)} collective-permute-done((bf16[256,1024]{1,0:T(8,128)(2,1)S(1)}, bf16[256,1024]{1,0:T(8,128)(2,1)S(1)}, u32[]{:S(2)}, u32[]{:S(2)}) %collective-permute-start.3) | collective-permute-done | bytes 524320 | tf_op jit(solution)/shard_map/ppermute | solution.py:201
  41.1 1.3 %collective-permute-start.5 = (f32[8,512]{1,0:T(8,128)S(1)}, f32[8,512]{1,0:T(8,128)S(1)}, u32[]{:S(2)}, u32[]{:S(2)}) collective-permute-start(f32[8,512]{1,0:T(8,128)S(1)} %get-tuple-element.35), channel_id=1, source_target_pairs={{1,0},{2,3},{9,8},{10,11},{17,16},{18,19},{25,24},{26,27}} | collective-permute-start | bytes 49160 | tf_op jit(solution)/shard_map/ppermute | solution.py:201
  42.4 1.3 %collective-permute-start.6 = (f32[8,512]{1,0:T(8,128)S(1)}, f32[8,512]{1,0:T(8,128)S(1)}, u32[]{:S(2)}, u32[]{:S(2)}) collective-permute-start(f32[8,512]{1,0:T(8,128)S(1)} %get-tuple-element.36), channel_id=1, source_target_pairs={{4,3},{7,8},{12,11},{15,16},{20,19},{23,24},{28,27},{31,0}} | collective-permute-start | bytes 49160 | tf_op jit(solution)/shard_map/ppermute | solution.py:201
  43.7 0.7 %collective-permute-start.7 = (f32[8,512]{1,0:T(8,128)S(1)}, f32[8,512]{1,0:T(8,128)S(1)}, u32[]{:S(2)}, u32[]{:S(2)}) collective-permute-start(f32[8,512]{1,0:T(8,128)S(1)} %get-tuple-element.36), channel_id=1, source_target_pairs={{1,31},{2,4},{9,7},{10,12},{17,15},{18,20},{25,23},{26,28}} | collective-permute-start | bytes 49160 | tf_op jit(solution)/shard_map/ppermute | solution.py:201
  44.4 2.4 %shard_map.19.own_partner_ref = f32[8,1024]{1,0:T(8,128)S(1)} custom-call(bf16[1024,1024]{1,0:T(8,128)(2,1)S(1)} %get-tuple-element.24.unit_ref, bf16[1024,1024]{1,0:T(8,128)(2,1)S(1)} %get-tuple-element.25.partner_ref), custom_call_target="tpu_custom_call" | custom-call | tf_op jit(solution)/shard_map/pallas_call | solution.py:168
  46.8 0.0 collective-permute-done.2.far_ref
  46.8 0.0 collective-permute-done.5.rows_ref
  46.8 4.3 %collective-permute-done.6.cross_ref = f32[8,512]{1,0:T(8,128)S(1)} collective-permute-done((f32[8,512]{1,0:T(8,128)S(1)}, f32[8,512]{1,0:T(8,128)S(1)}, u32[]{:S(2)}, u32[]{:S(2)}) %collective-permute-start.6) | collective-permute-done | bytes 16416 | tf_op jit(solution)/shard_map/ppermute | solution.py:201
  51.1 0.0 collective-permute-done.7.ends_ref
  51.1 0.7 %shard_map.23 = f32[40,1024]{1,0:T(8,128)} custom-call(s32[1]{0:T(128)} %bitcast.role_ref, f32[8,1024]{1,0:T(8,128)S(1)} %get-tuple-element.23.own_ref, f32[8,1024]{1,0:T(8,128)S(1)} %shard_map.19.own_partner_ref, f32[8,1024]{1,0:T(8,128)S(1)} %get-tuple-element.26.own_far_ref, f32[16,1024]{1,0:T(8,128)S(1)} %collective-permute-done.2.far_ref, ...), custom_call_target="tpu_custom_call" | custom-call | tf_op jit(solution)/shard_map/pallas_call | solution.py:168
  (2 shorter events, 0.0 us)
Async XLA Ops:
  0.0 10.6 %collective-permute-start = (bf16[1024,1024]{1,0:T(8,128)(2,1)}, bf16[1024,1024]{1,0:T(8,128)(2,1)S(1)}, u32[]{:S(2)}, u32[]{:S(2)}) collective-permute-start(bf16[1024,1024]{1,0:T(8,128)(2,1)} %rows_ref), channel_id=1, source_target_pairs={{0,2},{2,0},{1,3},{3,1},{4,6},{6,4},{5,7},{7,5},{8,10},{10,8},{9,1... | collective-permute-start | bytes 6291464 | tf_op jit(solution)/shard_map/ppermute | solution.py:201
  0.5 29.5 %collective-permute-start.1 = (bf16[1024,1024]{1,0:T(8,128)(2,1)}, bf16[1024,1024]{1,0:T(8,128)(2,1)S(1)}, u32[]{:S(2)}, u32[]{:S(2)}) collective-permute-start(bf16[1024,1024]{1,0:T(8,128)(2,1)} %rows_ref), channel_id=1, source_target_pairs={{1,0},{2,3},{3,5},{0,30},{5,4},{6,7},{7,9},{4,2},{9,8},{10,11},{11... | collective-permute-start | bytes 6291464 | tf_op jit(solution)/shard_map/ppermute | solution.py:201
  6.1 1.6 %copy-start = (bf16[1024,1024]{1,0:T(8,128)(2,1)S(1)}, bf16[1024,1024]{1,0:T(8,128)(2,1)}, u32[]{:S(2)}) copy-start(bf16[1024,1024]{1,0:T(8,128)(2,1)} %rows_ref) | copy-start | bytes 6291460
  11.3 24.2 %collective-permute-start.4 = (bf16[256,1024]{1,0:T(8,128)(2,1)S(1)}, bf16[256,1024]{1,0:T(8,128)(2,1)S(1)}, u32[]{:S(2)}, u32[]{:S(2)}) collective-permute-start(bf16[256,1024]{1,0:T(8,128)(2,1)S(1)} %get-tuple-element.30), channel_id=1, source_target_pairs={{1,2},{2,1},{3,4},{0,31},{9,10},{10,9},{11,12},{8,7},{17,18},{18,1... | collective-permute-start | bytes 1572872 | tf_op jit(solution)/shard_map/ppermute | solution.py:201
  14.3 26.9 %collective-permute-start.3 = (bf16[256,1024]{1,0:T(8,128)(2,1)S(1)}, bf16[256,1024]{1,0:T(8,128)(2,1)S(1)}, u32[]{:S(2)}, u32[]{:S(2)}) collective-permute-start(bf16[256,1024]{1,0:T(8,128)(2,1)S(1)} %get-tuple-element.28), channel_id=1, source_target_pairs={{1,2},{2,1},{3,4},{0,31},{9,10},{10,9},{11,12},{8,7},{17,18},{18,1... | collective-permute-start | bytes 1572872 | tf_op jit(solution)/shard_map/ppermute | solution.py:201
  35.4 11.4 %collective-permute-start.2 = (f32[16,1024]{1,0:T(8,128)S(1)}, f32[16,1024]{1,0:T(8,128)S(1)}, u32[]{:S(2)}, u32[]{:S(2)}) collective-permute-start(f32[16,1024]{1,0:T(8,128)S(1)} %get-tuple-element.27), channel_id=1, source_target_pairs={{0,1},{3,2},{5,3},{30,0},{4,5},{7,6},{9,7},{2,4},{8,9},{11,10},{13... | collective-permute-start | bytes 196616 | tf_op jit(solution)/shard_map/ppermute | solution.py:201
  41.1 5.7 %collective-permute-start.5 = (f32[8,512]{1,0:T(8,128)S(1)}, f32[8,512]{1,0:T(8,128)S(1)}, u32[]{:S(2)}, u32[]{:S(2)}) collective-permute-start(f32[8,512]{1,0:T(8,128)S(1)} %get-tuple-element.35), channel_id=1, source_target_pairs={{1,0},{2,3},{9,8},{10,11},{17,16},{18,19},{25,24},{26,27}} | collective-permute-start | bytes 49160 | tf_op jit(solution)/shard_map/ppermute | solution.py:201
  42.4 8.7 %collective-permute-start.6 = (f32[8,512]{1,0:T(8,128)S(1)}, f32[8,512]{1,0:T(8,128)S(1)}, u32[]{:S(2)}, u32[]{:S(2)}) collective-permute-start(f32[8,512]{1,0:T(8,128)S(1)} %get-tuple-element.36), channel_id=1, source_target_pairs={{4,3},{7,8},{12,11},{15,16},{20,19},{23,24},{28,27},{31,0}} | collective-permute-start | bytes 49160 | tf_op jit(solution)/shard_map/ppermute | solution.py:201
  43.7 7.4 %collective-permute-start.7 = (f32[8,512]{1,0:T(8,128)S(1)}, f32[8,512]{1,0:T(8,128)S(1)}, u32[]{:S(2)}, u32[]{:S(2)}) collective-permute-start(f32[8,512]{1,0:T(8,128)S(1)} %get-tuple-element.36), channel_id=1, source_target_pairs={{1,31},{2,4},{9,7},{10,12},{17,15},{18,20},{25,23},{26,28}} | collective-permute-start | bytes 49160 | tf_op jit(solution)/shard_map/ppermute | solution.py:201

commit v4 on v3

--- a/solution.py
+++ b/solution.py
@@ -50,29 +50,23 @@
     return turn, step, jnp.logical_or(turn == 1, turn == 2)
 
 
-def own_kernel(scale, rows_ref, unit_ref, own_ref):
+def own_kernel(scale, rows_ref, unit_ref, own_ref, *part_refs):
     unit_ref[...] = unit_of(rows_ref[...])
+    size = part_refs[0].shape[0]
+    for i, part_ref in enumerate(part_refs):
+        at = (len(part_refs) + i) * size
+        part_ref[...] = unit_ref[at : at + size, :]
     same = lax.broadcasted_iota(jnp.int32, (STEP, STEP), 0) == lax.broadcasted_iota(
         jnp.int32, (STEP, STEP), 1
     )
     best(scale, unit_ref, unit_ref, own_ref, same=same)
 
 
-def partner_kernel(role_ref, rows_ref, unit_ref, partner_ref, *part_refs):
-    middle = place(role_ref)[2]
+def partner_kernel(rows_ref, partner_ref, *part_refs):
+    partner_ref[...] = unit_of(rows_ref[...])
     size = part_refs[0].shape[0]
-    half = size * len(part_refs)
-    partner_ref[...] = unit_of(rows_ref[...])
     for i, part_ref in enumerate(part_refs):
-        at = i * size
-
-        @pl.when(middle)
-        def _():
-            part_ref[...] = partner_ref[at : at + size, :]
-
-        @pl.when(jnp.logical_not(middle))
-        def _():
-            part_ref[...] = unit_ref[half + at : half + at + size, :]
+        part_ref[...] = partner_ref[i * size : (i + 1) * size, :]
 
 
 def pair_kernel(scale, unit_ref, partner_ref, max_ref):
@@ -90,39 +84,37 @@
         best(scale, partner_ref, far_ref, far_max_ref, right_at=tiles)
 
 
-def part_kernel(scale, first, role_ref, part_ref, unit_ref, far_ref, *refs):
+def even_kernel(first, scale, role_ref, part_ref, far_ref, *refs):
     _, step, middle = place(role_ref)
-    rows_ref, cross_ref, tiles_ref = refs[-3:]
-    count = unit_ref.shape[0]
-    half, across = count // 2, count // 2 // TILE
-    inside = jnp.logical_and(step == 0, middle)
-    outside = jnp.logical_and(step == 1, jnp.logical_not(middle))
+    rows_ref, ends_ref = refs[-2:]
+    half = far_ref.shape[0] // 2
+    at, across = first // TILE, half // TILE
+
+    @pl.when(jnp.logical_and(step == 0, middle))
+    def _():
+        if first:
+            old_rows_ref, old_ends_ref = refs[:2]
+            rows_ref[:, :first] = old_rows_ref[:, :first]
+            ends_ref[:at, :] = old_ends_ref[:at, :]
+            ends_ref[across : across + at, :] = old_ends_ref[across : across + at, :]
+        best(scale, part_ref, far_ref.at[:half, :], ends_ref, right_at=at, left_ref=rows_ref, left_from=first)
+        best(
+            scale, part_ref, far_ref.at[half:, :], ends_ref, right_at=across + at,
+            left_ref=rows_ref, left_at=across, left_from=first,
+        )
+
+
+def odd_kernel(first, scale, role_ref, part_ref, unit_ref, *refs):
+    _, step, middle = place(role_ref)
+    cross_ref, tiles_ref = refs[-2:]
     at = first // TILE
 
-    if first:
-        old_rows_ref, old_cross_ref, old_tiles_ref = refs[:3]
-
-        @pl.when(inside)
-        def _():
-            rows_ref[:, :first] = old_rows_ref[:, :first]
-            cross_ref[:at, :] = old_cross_ref[:at, :]
-            cross_ref[across : across + at, :] = old_cross_ref[across : across + at, :]
-
-        @pl.when(outside)
-        def _():
+    @pl.when(jnp.logical_and(step == 1, jnp.logical_not(middle)))
+    def _():
+        if first:
+            old_cross_ref, old_tiles_ref = refs[:2]
             cross_ref[:, :first] = old_cross_ref[:, :first]
             tiles_ref[:at, :] = old_tiles_ref[:at, :]
-
-    @pl.when(inside)
-    def _():
-        best(scale, part_ref, far_ref.at[:half, :], cross_ref, right_at=at, left_ref=rows_ref, left_from=first)
-        best(
-            scale, part_ref, far_ref.at[half:, :], cross_ref, right_at=across + at,
-            left_ref=rows_ref, left_at=across, left_from=first,
-        )
-
-    @pl.when(outside)
-    def _():
         best(scale, part_ref, unit_ref, tiles_ref, right_at=at, left_ref=cross_ref, left_from=first)
 
 
@@ -184,14 +176,14 @@
     assert blocks % 8 == 0 and size % STEP == 0
 
     at = lambda column, turn: column % columns * 4 + turn
-    far, swap, parts, rows, cross, ends = [], [], [], [], [], []
+    far, swap, even, odd, rows, cross, ends = [], [], [], [], [], [], []
     for q in range(columns):
         far += [(at(q, 1), at(q, 0)), (at(q, 2), at(q, 3))]
         far += [(at(q, 3), at(q + 1, 1)), (at(q, 0), at(q - 1, 2))]
         swap += [(at(q, 0), at(q, 2)), (at(q, 2), at(q, 0)), (at(q, 1), at(q, 3)), (at(q, 3), at(q, 1))]
         if q % 2 == 0:
-            parts += [(at(q, 1), at(q, 2)), (at(q, 2), at(q, 1))]
-            parts += [(at(q, 3), at(q + 1, 0)), (at(q, 0), at(q - 1, 3))]
+            even += [(at(q, 1), at(q, 2)), (at(q, 2), at(q, 1))]
+            odd += [(at(q, 3), at(q + 1, 0)), (at(q, 0), at(q - 1, 3))]
             rows += [(at(q, 1), at(q, 0)), (at(q, 2), at(q, 3))]
             ends += [(at(q, 1), at(q - 1, 3)), (at(q, 2), at(q + 1, 0))]
         else:
@@ -204,11 +196,15 @@
     role, embeddings = lax.optimization_barrier((role, embeddings))
     far_rows = send(embeddings, far)
     partner_rows = send(embeddings, swap)
-    unit, own = call(functools.partial(own_kernel, scale), [((count, width), BF16), ((tiles, count), F32)], embeddings)
-    partner, *pieces = call(
-        partner_kernel, [((count, width), BF16)] + [((size, width), BF16)] * PARTS, role, partner_rows, unit
-    )
-    pieces = [send(piece, parts) for piece in pieces]
+    piece = ((size, width), BF16)
+    unit, own, *odd_parts = call(
+        functools.partial(own_kernel, scale),
+        [((count, width), BF16), ((tiles, count), F32)] + [piece] * PARTS,
+        embeddings,
+    )
+    odd_parts = [send(part, odd) for part in odd_parts]
+    partner, *even_parts = call(partner_kernel, [((count, width), BF16)] + [piece] * PARTS, partner_rows)
+    even_parts = [send(part, even) for part in even_parts]
     (own_partner,) = call(functools.partial(pair_kernel, scale), [((tiles, count), F32)], unit, partner)
     far_unit, own_far, far_max = call(
         functools.partial(far_kernel, scale),
@@ -219,20 +215,19 @@
         partner,
     )
     far_max = send(far_max, [(b, a) for a, b in far])
+    column = ((tiles, half), F32)
     done = []
-    for i, piece in enumerate(pieces):
+    for i, part in enumerate(even_parts):
+        done = call(functools.partial(even_kernel, i * size, scale), [column, column], role, part, far_unit, *done)
+    rows_max, ends_max = done
+    ends_max = send(ends_max, ends)
+    rows_max = send(rows_max, rows)
+    done = []
+    for i, part in enumerate(odd_parts):
         done = call(
-            functools.partial(part_kernel, scale, i * size),
-            [((tiles, half), F32), ((tiles, half), F32), ((across, count), F32)],
-            role,
-            piece,
-            unit,
-            far_unit,
-            *done,
+            functools.partial(odd_kernel, i * size, scale), [column, ((across, count), F32)], role, part, unit, *done
         )
-    rows_max, cross_max, half_tiles = done
-    ends_max = send(cross_max, ends)
-    rows_max = send(rows_max, rows)
+    cross_max, half_tiles = done
     cross_max = send(cross_max, cross)
     (out,) = call(
         join_kernel,

time: 52.5 us -> 52.7 us (level)
  the two profiles are of different devices: /device:TPU:0 before, /device:TPU:4 now
where the time goes in v4:
time: 52.7 us; the launch traced here: 52.5 us
  starting transfers between devices  22.2 us (42%)
  waiting for transfers between devices  16.9 us (32%)
  Pallas kernels  11.5 us (22%)
  local copies, waits for them, and re-layouts  1.61 us (3%)
    ppermute x10, starting transfers between devices, send(): return lax.ppermute(value, AXES, pairs)  22.2 us
    ppermute x10, waiting for transfers between devices, send(): return lax.ppermute(value, AXES, pairs)  16.9 us
    pallas_call x9, Pallas kernels, call(): pl.pallas_call(kernel, out_shape=[jax.ShapeDtypeStruct(*o) if last else p...  11.5 us
    unnamed x2, local copies, waits for them, and re-layouts  1.61 us
  transfers between devices with their start and end apart: 10, of which 2 were waited for; matrix products, arithmetic and copies ran while one was open for 0% of the time, Pallas kernels for 21%

profile of v4, /device:TPU:4, one launch (start us, length us, event | category | flops | bytes accessed | tf_op | source)
XLA Modules:
  0.0 52.5 jit_solution(7536014750133126824)
XLA Ops:
  0.0 0.0 collective-permute-start
  0.0 0.0 collective-permute-start.1
  0.0 0.0 copy-start
  0.0 1.6 %copy-done = bf16[1024,1024]{1,0:T(8,128)(2,1)S(1)} copy-done((bf16[1024,1024]{1,0:T(8,128)(2,1)S(1)}, bf16[1024,1024]{1,0:T(8,128)(2,1)}, u32[]{:S(2)}) %copy-start) | copy-done | bytes 2097176
  1.6 2.9 %shard_map.17 = (bf16[1024,1024]{1,0:T(8,128)(2,1)S(1)}, f32[8,1024]{1,0:T(8,128)S(1)}, bf16[256,1024]{1,0:T(8,128)(2,1)S(1)}, bf16[256,1024]{1,0:T(8,128)(2,1)S(1)}) custom-call(bf16[1024,1024]{1,0:T(8,128)(2,1)S(1)} %copy-done), custom_call_target="tpu_custom_call" | custom-call | tf_op jit(solution)/shard_map/pallas_call | solution.py:160
  4.6 0.7 %collective-permute-start.4 = (bf16[256,1024]{1,0:T(8,128)(2,1)S(1)}, bf16[256,1024]{1,0:T(8,128)(2,1)S(1)}, u32[]{:S(2)}, u32[]{:S(2)}) collective-permute-start(bf16[256,1024]{1,0:T(8,128)(2,1)S(1)} %get-tuple-element.33), channel_id=1, source_target_pairs={{3,4},{0,31},{11,12},{8,7},{19,20},{16,15},{27,28},{24,23}} | collective-permute-start | bytes 1572872 | tf_op jit(solution)/shard_map/ppermute | solution.py:193
  5.3 0.7 %collective-permute-start.3 = (bf16[256,1024]{1,0:T(8,128)(2,1)S(1)}, bf16[256,1024]{1,0:T(8,128)(2,1)S(1)}, u32[]{:S(2)}, u32[]{:S(2)}) collective-permute-start(bf16[256,1024]{1,0:T(8,128)(2,1)S(1)} %get-tuple-element.32), channel_id=1, source_target_pairs={{3,4},{0,31},{11,12},{8,7},{19,20},{16,15},{27,28},{24,23}} | collective-permute-start | bytes 1572872 | tf_op jit(solution)/shard_map/ppermute | solution.py:193
  6.0 0.0 collective-permute-done.rows_ref
  6.0 0.7 %shard_map.18 = (bf16[1024,1024]{1,0:T(8,128)(2,1)S(1)}, bf16[256,1024]{1,0:T(8,128)(2,1)S(1)}, bf16[256,1024]{1,0:T(8,128)(2,1)S(1)}) custom-call(bf16[1024,1024]{1,0:T(8,128)(2,1)S(1)} %collective-permute-done.rows_ref), custom_call_target="tpu_custom_call" | custom-call | tf_op jit(solution)/shard_map/pallas_call | solution.py:160
  6.7 3.8 %collective-permute-start.6 = (bf16[256,1024]{1,0:T(8,128)(2,1)S(1)}, bf16[256,1024]{1,0:T(8,128)(2,1)S(1)}, u32[]{:S(2)}, u32[]{:S(2)}) collective-permute-start(bf16[256,1024]{1,0:T(8,128)(2,1)S(1)} %get-tuple-element.39), channel_id=1, source_target_pairs={{1,2},{2,1},{9,10},{10,9},{17,18},{18,17},{25,26},{26,25}} | collective-permute-start | bytes 1572872 | tf_op jit(solution)/shard_map/ppermute | solution.py:193
  10.4 1.9 %collective-permute-start.5 = (bf16[256,1024]{1,0:T(8,128)(2,1)S(1)}, bf16[256,1024]{1,0:T(8,128)(2,1)S(1)}, u32[]{:S(2)}, u32[]{:S(2)}) collective-permute-start(bf16[256,1024]{1,0:T(8,128)(2,1)S(1)} %get-tuple-element.37), channel_id=1, source_target_pairs={{1,2},{2,1},{9,10},{10,9},{17,18},{18,17},{25,26},{26,25}} | collective-permute-start | bytes 1572872 | tf_op jit(solution)/shard_map/ppermute | solution.py:193
  12.4 16.2 %collective-permute-done.1.rows_ref = bf16[1024,1024]{1,0:T(8,128)(2,1)S(1)} collective-permute-done((bf16[1024,1024]{1,0:T(8,128)(2,1)}, bf16[1024,1024]{1,0:T(8,128)(2,1)S(1)}, u32[]{:S(2)}, u32[]{:S(2)}) %collective-permute-start.1) | collective-permute-done | bytes 2097184 | tf_op jit(solution)/shard_map/ppermute | solution.py:193
  28.6 3.0 %shard_map.20 = (bf16[1024,1024]{1,0:T(8,128)(2,1)S(1)}, f32[8,1024]{1,0:T(8,128)S(1)}, f32[16,1024]{1,0:T(8,128)S(1)}) custom-call(s32[1]{0:T(128)} %bitcast.role_ref, bf16[1024,1024]{1,0:T(8,128)(2,1)S(1)} %collective-permute-done.1.rows_ref, bf16[1024,1024]{1,0:T(8,128)(2,1)S(1)} %get-tuple-element.28.unit_ref, ...), custom_call_target="tpu_custom_call" | custom-call | tf_op jit(solution)/shard_map/pallas_call | solution.py:160
  31.6 3.8 %collective-permute-start.2 = (f32[16,1024]{1,0:T(8,128)S(1)}, f32[16,1024]{1,0:T(8,128)S(1)}, u32[]{:S(2)}, u32[]{:S(2)}) collective-permute-start(f32[16,1024]{1,0:T(8,128)S(1)} %get-tuple-element.31), channel_id=1, source_target_pairs={{0,1},{3,2},{5,3},{30,0},{4,5},{7,6},{9,7},{2,4},{8,9},{11,10},{13... | collective-permute-start | bytes 196616 | tf_op jit(solution)/shard_map/ppermute | solution.py:193
  35.4 0.0 collective-permute-done.4.part_ref
  35.4 0.0 collective-permute-done.3.part_ref
  35.4 0.7 %collective-permute-start.8 = (f32[8,512]{1,0:T(8,128)S(1)}, f32[8,512]{1,0:T(8,128)S(1)}, u32[]{:S(2)}, u32[]{:S(2)}) collective-permute-start(f32[8,512]{1,0:T(8,128)S(1)} %get-tuple-element.43), channel_id=1, source_target_pairs={{4,3},{7,8},{12,11},{15,16},{20,19},{23,24},{28,27},{31,0}} | collective-permute-start | bytes 49160 | tf_op jit(solution)/shard_map/ppermute | solution.py:193
  36.1 0.0 collective-permute-done.6.part_ref
  36.1 0.9 %shard_map.23 = (f32[8,512]{1,0:T(8,128)S(1)}, f32[8,512]{1,0:T(8,128)S(1)}) custom-call(s32[1]{0:T(128)} %bitcast.role_ref, bf16[256,1024]{1,0:T(8,128)(2,1)S(1)} %collective-permute-done.6.part_ref, bf16[1024,1024]{1,0:T(8,128)(2,1)S(1)} %get-tuple-element.38.far_ref), custom_call_target="tpu_custom_call" | custom-call | tf_op jit(solution)/shard_map/pallas_call | solution.py:160
  37.0 0.7 %collective-permute-done.5.part_ref = bf16[256,1024]{1,0:T(8,128)(2,1)S(1)} collective-permute-done((bf16[256,1024]{1,0:T(8,128)(2,1)S(1)}, bf16[256,1024]{1,0:T(8,128)(2,1)S(1)}, u32[]{:S(2)}, u32[]{:S(2)}) %collective-permute-start.5) | collective-permute-done | bytes 524320 | tf_op jit(solution)/shard_map/ppermute | solution.py:193
  37.7 0.9 %shard_map.24 = (f32[8,512]{1,0:T(8,128)S(1)}, f32[8,512]{1,0:T(8,128)S(1)}) custom-call(s32[1]{0:T(128)} %bitcast.role_ref, bf16[256,1024]{1,0:T(8,128)(2,1)S(1)} %collective-permute-done.5.part_ref, bf16[1024,1024]{1,0:T(8,128)(2,1)S(1)} %get-tuple-element.38.far_ref, f32[8,512]{1,0:T(8,128)S(1)} %get-tuple-element.40.refs_0_, ...), custom_call_target="tpu_custom_call" | custom-call | tf_op jit(solution)/shard_map/pallas_call | solution.py:160
  38.6 5.0 %collective-permute-start.7 = (f32[8,512]{1,0:T(8,128)S(1)}, f32[8,512]{1,0:T(8,128)S(1)}, u32[]{:S(2)}, u32[]{:S(2)}) collective-permute-start(f32[8,512]{1,0:T(8,128)S(1)} %get-tuple-element.42), channel_id=1, source_target_pairs={{1,0},{2,3},{9,8},{10,11},{17,16},{18,19},{25,24},{26,27}} | collective-permute-start | bytes 49160 | tf_op jit(solution)/shard_map/ppermute | solution.py:193
  43.6 5.7 %collective-permute-start.9 = (f32[8,512]{1,0:T(8,128)S(1)}, f32[8,512]{1,0:T(8,128)S(1)}, u32[]{:S(2)}, u32[]{:S(2)}) collective-permute-start(f32[8,512]{1,0:T(8,128)S(1)} %get-tuple-element.44), channel_id=1, source_target_pairs={{1,31},{2,4},{9,7},{10,12},{17,15},{18,20},{25,23},{26,28}} | collective-permute-start | bytes 49160 | tf_op jit(solution)/shard_map/ppermute | solution.py:193
  49.3 2.4 %shard_map.19.own_partner_ref = f32[8,1024]{1,0:T(8,128)S(1)} custom-call(bf16[1024,1024]{1,0:T(8,128)(2,1)S(1)} %get-tuple-element.28.unit_ref, bf16[1024,1024]{1,0:T(8,128)(2,1)S(1)} %get-tuple-element.29.partner_ref), custom_call_target="tpu_custom_call" | custom-call | tf_op jit(solution)/shard_map/pallas_call | solution.py:160
  51.7 0.0 collective-permute-done.8.cross_ref
  51.7 0.0 collective-permute-done.2.far_ref
  51.7 0.0 collective-permute-done.7.rows_ref
  51.7 0.0 collective-permute-done.9.ends_ref
  51.7 0.7 %shard_map.25 = f32[40,1024]{1,0:T(8,128)} custom-call(s32[1]{0:T(128)} %bitcast.role_ref, f32[8,1024]{1,0:T(8,128)S(1)} %get-tuple-element.27.own_ref, f32[8,1024]{1,0:T(8,128)S(1)} %shard_map.19.own_partner_ref, f32[8,1024]{1,0:T(8,128)S(1)} %get-tuple-element.30.own_far_ref, f32[16,1024]{1,0:T(8,128)S(1)} %collective-permute-done.2.far_ref, ...), custom_call_target="tpu_custom_call" | custom-call | tf_op jit(solution)/shard_map/pallas_call | solution.py:160
  (2 shorter events, 0.0 us)
Async XLA Ops:
  0.0 6.0 %collective-permute-start = (bf16[1024,1024]{1,0:T(8,128)(2,1)}, bf16[1024,1024]{1,0:T(8,128)(2,1)S(1)}, u32[]{:S(2)}, u32[]{:S(2)}) collective-permute-start(bf16[1024,1024]{1,0:T(8,128)(2,1)} %rows_ref), channel_id=1, source_target_pairs={{0,2},{2,0},{1,3},{3,1},{4,6},{6,4},{5,7},{7,5},{8,10},{10,8},{9,1... | collective-permute-start | bytes 6291464 | tf_op jit(solution)/shard_map/ppermute | solution.py:193
  0.0 28.6 %collective-permute-start.1 = (bf16[1024,1024]{1,0:T(8,128)(2,1)}, bf16[1024,1024]{1,0:T(8,128)(2,1)S(1)}, u32[]{:S(2)}, u32[]{:S(2)}) collective-permute-start(bf16[1024,1024]{1,0:T(8,128)(2,1)} %rows_ref), channel_id=1, source_target_pairs={{1,0},{2,3},{3,5},{0,30},{5,4},{6,7},{7,9},{4,2},{9,8},{10,11},{11... | collective-permute-start | bytes 6291464 | tf_op jit(solution)/shard_map/ppermute | solution.py:193
  0.0 1.6 %copy-start = (bf16[1024,1024]{1,0:T(8,128)(2,1)S(1)}, bf16[1024,1024]{1,0:T(8,128)(2,1)}, u32[]{:S(2)}) copy-start(bf16[1024,1024]{1,0:T(8,128)(2,1)} %rows_ref) | copy-start | bytes 6291460
  4.6 30.8 %collective-permute-start.4 = (bf16[256,1024]{1,0:T(8,128)(2,1)S(1)}, bf16[256,1024]{1,0:T(8,128)(2,1)S(1)}, u32[]{:S(2)}, u32[]{:S(2)}) collective-permute-start(bf16[256,1024]{1,0:T(8,128)(2,1)S(1)} %get-tuple-element.33), channel_id=1, source_target_pairs={{3,4},{0,31},{11,12},{8,7},{19,20},{16,15},{27,28},{24,23}} | collective-permute-start | bytes 1572872 | tf_op jit(solution)/shard_map/ppermute | solution.py:193
  5.3 30.1 %collective-permute-start.3 = (bf16[256,1024]{1,0:T(8,128)(2,1)S(1)}, bf16[256,1024]{1,0:T(8,128)(2,1)S(1)}, u32[]{:S(2)}, u32[]{:S(2)}) collective-permute-start(bf16[256,1024]{1,0:T(8,128)(2,1)S(1)} %get-tuple-element.32), channel_id=1, source_target_pairs={{3,4},{0,31},{11,12},{8,7},{19,20},{16,15},{27,28},{24,23}} | collective-permute-start | bytes 1572872 | tf_op jit(solution)/shard_map/ppermute | solution.py:193
  6.7 29.4 %collective-permute-start.6 = (bf16[256,1024]{1,0:T(8,128)(2,1)S(1)}, bf16[256,1024]{1,0:T(8,128)(2,1)S(1)}, u32[]{:S(2)}, u32[]{:S(2)}) collective-permute-start(bf16[256,1024]{1,0:T(8,128)(2,1)S(1)} %get-tuple-element.39), channel_id=1, source_target_pairs={{1,2},{2,1},{9,10},{10,9},{17,18},{18,17},{25,26},{26,25}} | collective-permute-start | bytes 1572872 | tf_op jit(solution)/shard_map/ppermute | solution.py:193
  10.4 27.3 %collective-permute-start.5 = (bf16[256,1024]{1,0:T(8,128)(2,1)S(1)}, bf16[256,1024]{1,0:T(8,128)(2,1)S(1)}, u32[]{:S(2)}, u32[]{:S(2)}) collective-permute-start(bf16[256,1024]{1,0:T(8,128)(2,1)S(1)} %get-tuple-element.37), channel_id=1, source_target_pairs={{1,2},{2,1},{9,10},{10,9},{17,18},{18,17},{25,26},{26,25}} | collective-permute-start | bytes 1572872 | tf_op jit(solution)/shard_map/ppermute | solution.py:193
  31.6 20.1 %collective-permute-start.2 = (f32[16,1024]{1,0:T(8,128)S(1)}, f32[16,1024]{1,0:T(8,128)S(1)}, u32[]{:S(2)}, u32[]{:S(2)}) collective-permute-start(f32[16,1024]{1,0:T(8,128)S(1)} %get-tuple-element.31), channel_id=1, source_target_pairs={{0,1},{3,2},{5,3},{30,0},{4,5},{7,6},{9,7},{2,4},{8,9},{11,10},{13... | collective-permute-start | bytes 196616 | tf_op jit(solution)/shard_map/ppermute | solution.py:193
  35.4 16.3 %collective-permute-start.8 = (f32[8,512]{1,0:T(8,128)S(1)}, f32[8,512]{1,0:T(8,128)S(1)}, u32[]{:S(2)}, u32[]{:S(2)}) collective-permute-start(f32[8,512]{1,0:T(8,128)S(1)} %get-tuple-element.43), channel_id=1, source_target_pairs={{4,3},{7,8},{12,11},{15,16},{20,19},{23,24},{28,27},{31,0}} | collective-permute-start | bytes 49160 | tf_op jit(solution)/shard_map/ppermute | solution.py:193
  38.6 13.1 %collective-permute-start.7 = (f32[8,512]{1,0:T(8,128)S(1)}, f32[8,512]{1,0:T(8,128)S(1)}, u32[]{:S(2)}, u32[]{:S(2)}) collective-permute-start(f32[8,512]{1,0:T(8,128)S(1)} %get-tuple-element.42), channel_id=1, source_target_pairs={{1,0},{2,3},{9,8},{10,11},{17,16},{18,19},{25,24},{26,27}} | collective-permute-start | bytes 49160 | tf_op jit(solution)/shard_map/ppermute | solution.py:193
  43.6 8.1 %collective-permute-start.9 = (f32[8,512]{1,0:T(8,128)S(1)}, f32[8,512]{1,0:T(8,128)S(1)}, u32[]{:S(2)}, u32[]{:S(2)}) collective-permute-start(f32[8,512]{1,0:T(8,128)S(1)} %get-tuple-element.44), channel_id=1, source_target_pairs={{1,31},{2,4},{9,7},{10,12},{17,15},{18,20},{25,23},{26,28}} | collective-permute-start | bytes 49160 | tf_op jit(solution)/shard_map/ppermute | solution.py:193

commit v5 on v4

--- a/solution.py
+++ b/solution.py
@@ -187,7 +187,11 @@
             rows += [(at(q, 1), at(q, 0)), (at(q, 2), at(q, 3))]
             ends += [(at(q, 1), at(q - 1, 3)), (at(q, 2), at(q + 1, 0))]
         else:
-            cross += [(at(q, 0), at(q - 1, 3)), (at(q, 3), at(q + 1, 0))]
+            for ring in (
+                (at(q, 0), at(q - 1, 3), at(q - 1, 1), at(q, 2)),
+                (at(q, 3), at(q + 1, 0), at(q + 1, 2), at(q, 1)),
+            ):
+                cross += [(ring[i], ring[(i + 1) % 4]) for i in range(4)]
 
     def send(value, pairs):
         return lax.ppermute(value, AXES, pairs)

time: 52.7 us -> 51.6 us (0.979)
  starting transfers between devices: 22.2 us -> 20.6 us
  waiting for transfers between devices: 16.9 us -> 17.5 us
    ppermute x10, starting transfers between devices: 22.2 us -> 20.6 us  [send(): return lax.ppermute(value, AXES, pairs)]
    ppermute x10, waiting for transfers between devices: 16.9 us -> 17.5 us  [send(): return lax.ppermute(value, AXES, pairs)]
where the time goes in v5:
time: 51.6 us; the launch traced here: 51.4 us
  starting transfers between devices  20.6 us (40%)
  waiting for transfers between devices  17.5 us (34%)
  Pallas kernels  11.5 us (22%)
  local copies, waits for them, and re-layouts  1.61 us (3%)
    ppermute x10, starting transfers between devices, send(): return lax.ppermute(value, AXES, pairs)  20.6 us
    ppermute x10, waiting for transfers between devices, send(): return lax.ppermute(value, AXES, pairs)  17.5 us
    pallas_call x9, Pallas kernels, call(): pl.pallas_call(kernel, out_shape=[jax.ShapeDtypeStruct(*o) if last else p...  11.5 us
    unnamed x2, local copies, waits for them, and re-layouts  1.61 us
  transfers between devices with their start and end apart: 10, of which 2 were waited for; matrix products, arithmetic and copies ran while one was open for 0% of the time, Pallas kernels for 21%

profile of v5, /device:TPU:4, one launch (start us, length us, event | category | flops | bytes accessed | tf_op | source)
XLA Modules:
  0.0 51.4 jit_solution(901427684599600900)
XLA Ops:
  0.0 0.0 collective-permute-start
  0.0 0.0 collective-permute-start.1
  0.0 0.0 copy-start
  0.0 1.6 %copy-done = bf16[1024,1024]{1,0:T(8,128)(2,1)S(1)} copy-done((bf16[1024,1024]{1,0:T(8,128)(2,1)S(1)}, bf16[1024,1024]{1,0:T(8,128)(2,1)}, u32[]{:S(2)}) %copy-start) | copy-done | bytes 2097176
  1.6 2.9 %shard_map.17 = (bf16[1024,1024]{1,0:T(8,128)(2,1)S(1)}, f32[8,1024]{1,0:T(8,128)S(1)}, bf16[256,1024]{1,0:T(8,128)(2,1)S(1)}, bf16[256,1024]{1,0:T(8,128)(2,1)S(1)}) custom-call(bf16[1024,1024]{1,0:T(8,128)(2,1)S(1)} %copy-done), custom_call_target="tpu_custom_call" | custom-call | tf_op jit(solution)/shard_map/pallas_call | solution.py:160
  4.6 0.7 %collective-permute-start.4 = (bf16[256,1024]{1,0:T(8,128)(2,1)S(1)}, bf16[256,1024]{1,0:T(8,128)(2,1)S(1)}, u32[]{:S(2)}, u32[]{:S(2)}) collective-permute-start(bf16[256,1024]{1,0:T(8,128)(2,1)S(1)} %get-tuple-element.33), channel_id=1, source_target_pairs={{3,4},{0,31},{11,12},{8,7},{19,20},{16,15},{27,28},{24,23}} | collective-permute-start | bytes 1572872 | tf_op jit(solution)/shard_map/ppermute | solution.py:197
  5.3 0.7 %collective-permute-start.3 = (bf16[256,1024]{1,0:T(8,128)(2,1)S(1)}, bf16[256,1024]{1,0:T(8,128)(2,1)S(1)}, u32[]{:S(2)}, u32[]{:S(2)}) collective-permute-start(bf16[256,1024]{1,0:T(8,128)(2,1)S(1)} %get-tuple-element.32), channel_id=1, source_target_pairs={{3,4},{0,31},{11,12},{8,7},{19,20},{16,15},{27,28},{24,23}} | collective-permute-start | bytes 1572872 | tf_op jit(solution)/shard_map/ppermute | solution.py:197
  6.0 0.0 collective-permute-done.rows_ref
  6.0 0.7 %shard_map.18 = (bf16[1024,1024]{1,0:T(8,128)(2,1)S(1)}, bf16[256,1024]{1,0:T(8,128)(2,1)S(1)}, bf16[256,1024]{1,0:T(8,128)(2,1)S(1)}) custom-call(bf16[1024,1024]{1,0:T(8,128)(2,1)S(1)} %collective-permute-done.rows_ref), custom_call_target="tpu_custom_call" | custom-call | tf_op jit(solution)/shard_map/pallas_call | solution.py:160
  6.7 3.8 %collective-permute-start.6 = (bf16[256,1024]{1,0:T(8,128)(2,1)S(1)}, bf16[256,1024]{1,0:T(8,128)(2,1)S(1)}, u32[]{:S(2)}, u32[]{:S(2)}) collective-permute-start(bf16[256,1024]{1,0:T(8,128)(2,1)S(1)} %get-tuple-element.39), channel_id=1, source_target_pairs={{1,2},{2,1},{9,10},{10,9},{17,18},{18,17},{25,26},{26,25}} | collective-permute-start | bytes 1572872 | tf_op jit(solution)/shard_map/ppermute | solution.py:197
  10.4 1.9 %collective-permute-start.5 = (bf16[256,1024]{1,0:T(8,128)(2,1)S(1)}, bf16[256,1024]{1,0:T(8,128)(2,1)S(1)}, u32[]{:S(2)}, u32[]{:S(2)}) collective-permute-start(bf16[256,1024]{1,0:T(8,128)(2,1)S(1)} %get-tuple-element.37), channel_id=1, source_target_pairs={{1,2},{2,1},{9,10},{10,9},{17,18},{18,17},{25,26},{26,25}} | collective-permute-start | bytes 1572872 | tf_op jit(solution)/shard_map/ppermute | solution.py:197
  12.4 16.2 %collective-permute-done.1.rows_ref = bf16[1024,1024]{1,0:T(8,128)(2,1)S(1)} collective-permute-done((bf16[1024,1024]{1,0:T(8,128)(2,1)}, bf16[1024,1024]{1,0:T(8,128)(2,1)S(1)}, u32[]{:S(2)}, u32[]{:S(2)}) %collective-permute-start.1) | collective-permute-done | bytes 2097184 | tf_op jit(solution)/shard_map/ppermute | solution.py:197
  28.6 3.0 %shard_map.20 = (bf16[1024,1024]{1,0:T(8,128)(2,1)S(1)}, f32[8,1024]{1,0:T(8,128)S(1)}, f32[16,1024]{1,0:T(8,128)S(1)}) custom-call(s32[1]{0:T(128)} %bitcast.role_ref, bf16[1024,1024]{1,0:T(8,128)(2,1)S(1)} %collective-permute-done.1.rows_ref, bf16[1024,1024]{1,0:T(8,128)(2,1)S(1)} %get-tuple-element.28.unit_ref, ...), custom_call_target="tpu_custom_call" | custom-call | tf_op jit(solution)/shard_map/pallas_call | solution.py:160
  31.6 3.8 %collective-permute-start.2 = (f32[16,1024]{1,0:T(8,128)S(1)}, f32[16,1024]{1,0:T(8,128)S(1)}, u32[]{:S(2)}, u32[]{:S(2)}) collective-permute-start(f32[16,1024]{1,0:T(8,128)S(1)} %get-tuple-element.31), channel_id=1, source_target_pairs={{0,1},{3,2},{5,3},{30,0},{4,5},{7,6},{9,7},{2,4},{8,9},{11,10},{13... | collective-permute-start | bytes 196616 | tf_op jit(solution)/shard_map/ppermute | solution.py:197
  35.4 0.0 collective-permute-done.4.part_ref
  35.4 0.0 collective-permute-done.3.part_ref
  35.4 0.1 collective-permute-start.8
  35.5 0.0 collective-permute-done.6.part_ref
  35.5 0.9 %shard_map.23 = (f32[8,512]{1,0:T(8,128)S(1)}, f32[8,512]{1,0:T(8,128)S(1)}) custom-call(s32[1]{0:T(128)} %bitcast.role_ref, bf16[256,1024]{1,0:T(8,128)(2,1)S(1)} %collective-permute-done.6.part_ref, bf16[1024,1024]{1,0:T(8,128)(2,1)S(1)} %get-tuple-element.38.far_ref), custom_call_target="tpu_custom_call" | custom-call | tf_op jit(solution)/shard_map/pallas_call | solution.py:160
  36.4 1.3 %collective-permute-done.5.part_ref = bf16[256,1024]{1,0:T(8,128)(2,1)S(1)} collective-permute-done((bf16[256,1024]{1,0:T(8,128)(2,1)S(1)}, bf16[256,1024]{1,0:T(8,128)(2,1)S(1)}, u32[]{:S(2)}, u32[]{:S(2)}) %collective-permute-start.5) | collective-permute-done | bytes 524320 | tf_op jit(solution)/shard_map/ppermute | solution.py:197
  37.7 0.9 %shard_map.24 = (f32[8,512]{1,0:T(8,128)S(1)}, f32[8,512]{1,0:T(8,128)S(1)}) custom-call(s32[1]{0:T(128)} %bitcast.role_ref, bf16[256,1024]{1,0:T(8,128)(2,1)S(1)} %collective-permute-done.5.part_ref, bf16[1024,1024]{1,0:T(8,128)(2,1)S(1)} %get-tuple-element.38.far_ref, f32[8,512]{1,0:T(8,128)S(1)} %get-tuple-element.40.refs_0_, ...), custom_call_target="tpu_custom_call" | custom-call | tf_op jit(solution)/shard_map/pallas_call | solution.py:160
  38.6 3.8 %collective-permute-start.7 = (f32[8,512]{1,0:T(8,128)S(1)}, f32[8,512]{1,0:T(8,128)S(1)}, u32[]{:S(2)}, u32[]{:S(2)}) collective-permute-start(f32[8,512]{1,0:T(8,128)S(1)} %get-tuple-element.42), channel_id=1, source_target_pairs={{1,0},{2,3},{9,8},{10,11},{17,16},{18,19},{25,24},{26,27}} | collective-permute-start | bytes 49160 | tf_op jit(solution)/shard_map/ppermute | solution.py:197
  42.5 5.8 %collective-permute-start.9 = (f32[8,512]{1,0:T(8,128)S(1)}, f32[8,512]{1,0:T(8,128)S(1)}, u32[]{:S(2)}, u32[]{:S(2)}) collective-permute-start(f32[8,512]{1,0:T(8,128)S(1)} %get-tuple-element.44), channel_id=1, source_target_pairs={{1,31},{2,4},{9,7},{10,12},{17,15},{18,20},{25,23},{26,28}} | collective-permute-start | bytes 49160 | tf_op jit(solution)/shard_map/ppermute | solution.py:197
  48.3 2.4 %shard_map.19.own_partner_ref = f32[8,1024]{1,0:T(8,128)S(1)} custom-call(bf16[1024,1024]{1,0:T(8,128)(2,1)S(1)} %get-tuple-element.28.unit_ref, bf16[1024,1024]{1,0:T(8,128)(2,1)S(1)} %get-tuple-element.29.partner_ref), custom_call_target="tpu_custom_call" | custom-call | tf_op jit(solution)/shard_map/pallas_call | solution.py:160
  50.6 0.0 collective-permute-done.8.cross_ref
  50.7 0.0 collective-permute-done.2.far_ref
  50.7 0.0 collective-permute-done.7.rows_ref
  50.7 0.0 collective-permute-done.9.ends_ref
  50.7 0.7 %shard_map.25 = f32[40,1024]{1,0:T(8,128)} custom-call(s32[1]{0:T(128)} %bitcast.role_ref, f32[8,1024]{1,0:T(8,128)S(1)} %get-tuple-element.27.own_ref, f32[8,1024]{1,0:T(8,128)S(1)} %shard_map.19.own_partner_ref, f32[8,1024]{1,0:T(8,128)S(1)} %get-tuple-element.30.own_far_ref, f32[16,1024]{1,0:T(8,128)S(1)} %collective-permute-done.2.far_ref, ...), custom_call_target="tpu_custom_call" | custom-call | tf_op jit(solution)/shard_map/pallas_call | solution.py:160
  (2 shorter events, 0.0 us)
Async XLA Ops:
  0.0 6.0 %collective-permute-start = (bf16[1024,1024]{1,0:T(8,128)(2,1)}, bf16[1024,1024]{1,0:T(8,128)(2,1)S(1)}, u32[]{:S(2)}, u32[]{:S(2)}) collective-permute-start(bf16[1024,1024]{1,0:T(8,128)(2,1)} %rows_ref), channel_id=1, source_target_pairs={{0,2},{2,0},{1,3},{3,1},{4,6},{6,4},{5,7},{7,5},{8,10},{10,8},{9,1... | collective-permute-start | bytes 6291464 | tf_op jit(solution)/shard_map/ppermute | solution.py:197
  0.0 28.6 %collective-permute-start.1 = (bf16[1024,1024]{1,0:T(8,128)(2,1)}, bf16[1024,1024]{1,0:T(8,128)(2,1)S(1)}, u32[]{:S(2)}, u32[]{:S(2)}) collective-permute-start(bf16[1024,1024]{1,0:T(8,128)(2,1)} %rows_ref), channel_id=1, source_target_pairs={{1,0},{2,3},{3,5},{0,30},{5,4},{6,7},{7,9},{4,2},{9,8},{10,11},{11... | collective-permute-start | bytes 6291464 | tf_op jit(solution)/shard_map/ppermute | solution.py:197
  0.0 1.6 %copy-start = (bf16[1024,1024]{1,0:T(8,128)(2,1)S(1)}, bf16[1024,1024]{1,0:T(8,128)(2,1)}, u32[]{:S(2)}) copy-start(bf16[1024,1024]{1,0:T(8,128)(2,1)} %rows_ref) | copy-start | bytes 6291460
  4.6 30.8 %collective-permute-start.4 = (bf16[256,1024]{1,0:T(8,128)(2,1)S(1)}, bf16[256,1024]{1,0:T(8,128)(2,1)S(1)}, u32[]{:S(2)}, u32[]{:S(2)}) collective-permute-start(bf16[256,1024]{1,0:T(8,128)(2,1)S(1)} %get-tuple-element.33), channel_id=1, source_target_pairs={{3,4},{0,31},{11,12},{8,7},{19,20},{16,15},{27,28},{24,23}} | collective-permute-start | bytes 1572872 | tf_op jit(solution)/shard_map/ppermute | solution.py:197
  5.3 30.1 %collective-permute-start.3 = (bf16[256,1024]{1,0:T(8,128)(2,1)S(1)}, bf16[256,1024]{1,0:T(8,128)(2,1)S(1)}, u32[]{:S(2)}, u32[]{:S(2)}) collective-permute-start(bf16[256,1024]{1,0:T(8,128)(2,1)S(1)} %get-tuple-element.32), channel_id=1, source_target_pairs={{3,4},{0,31},{11,12},{8,7},{19,20},{16,15},{27,28},{24,23}} | collective-permute-start | bytes 1572872 | tf_op jit(solution)/shard_map/ppermute | solution.py:197
  6.7 28.8 %collective-permute-start.6 = (bf16[256,1024]{1,0:T(8,128)(2,1)S(1)}, bf16[256,1024]{1,0:T(8,128)(2,1)S(1)}, u32[]{:S(2)}, u32[]{:S(2)}) collective-permute-start(bf16[256,1024]{1,0:T(8,128)(2,1)S(1)} %get-tuple-element.39), channel_id=1, source_target_pairs={{1,2},{2,1},{9,10},{10,9},{17,18},{18,17},{25,26},{26,25}} | collective-permute-start | bytes 1572872 | tf_op jit(solution)/shard_map/ppermute | solution.py:197
  10.4 27.3 %collective-permute-start.5 = (bf16[256,1024]{1,0:T(8,128)(2,1)S(1)}, bf16[256,1024]{1,0:T(8,128)(2,1)S(1)}, u32[]{:S(2)}, u32[]{:S(2)}) collective-permute-start(bf16[256,1024]{1,0:T(8,128)(2,1)S(1)} %get-tuple-element.37), channel_id=1, source_target_pairs={{1,2},{2,1},{9,10},{10,9},{17,18},{18,17},{25,26},{26,25}} | collective-permute-start | bytes 1572872 | tf_op jit(solution)/shard_map/ppermute | solution.py:197
  31.6 19.0 %collective-permute-start.2 = (f32[16,1024]{1,0:T(8,128)S(1)}, f32[16,1024]{1,0:T(8,128)S(1)}, u32[]{:S(2)}, u32[]{:S(2)}) collective-permute-start(f32[16,1024]{1,0:T(8,128)S(1)} %get-tuple-element.31), channel_id=1, source_target_pairs={{0,1},{3,2},{5,3},{30,0},{4,5},{7,6},{9,7},{2,4},{8,9},{11,10},{13... | collective-permute-start | bytes 196616 | tf_op jit(solution)/shard_map/ppermute | solution.py:197
  35.4 15.2 %collective-permute-start.8 = (f32[8,512]{1,0:T(8,128)S(1)}, f32[8,512]{1,0:T(8,128)S(1)}, u32[]{:S(2)}, u32[]{:S(2)}) collective-permute-start(f32[8,512]{1,0:T(8,128)S(1)} %get-tuple-element.43), channel_id=1, source_target_pairs={{4,3},{3,1},{1,6},{6,4},{7,8},{8,10},{10,5},{5,7},{12,11},{11,9},{... | collective-permute-start | bytes 49160 | tf_op jit(solution)/shard_map/ppermute | solution.py:197
  38.6 12.1 %collective-permute-start.7 = (f32[8,512]{1,0:T(8,128)S(1)}, f32[8,512]{1,0:T(8,128)S(1)}, u32[]{:S(2)}, u32[]{:S(2)}) collective-permute-start(f32[8,512]{1,0:T(8,128)S(1)} %get-tuple-element.42), channel_id=1, source_target_pairs={{1,0},{2,3},{9,8},{10,11},{17,16},{18,19},{25,24},{26,27}} | collective-permute-start | bytes 49160 | tf_op jit(solution)/shard_map/ppermute | solution.py:197
  42.5 8.2 %collective-permute-start.9 = (f32[8,512]{1,0:T(8,128)S(1)}, f32[8,512]{1,0:T(8,128)S(1)}, u32[]{:S(2)}, u32[]{:S(2)}) collective-permute-start(f32[8,512]{1,0:T(8,128)S(1)} %get-tuple-element.44), channel_id=1, source_target_pairs={{1,31},{2,4},{9,7},{10,12},{17,15},{18,20},{25,23},{26,28}} | collective-permute-start | bytes 49160 | tf_op jit(solution)/shard_map/ppermute | solution.py:197

commit v6 on v5

--- a/solution.py
+++ b/solution.py
@@ -46,7 +46,7 @@
 
 def place(role_ref):
     turn = lax.rem(role_ref[0], 4)
-    step = lax.rem(lax.div(role_ref[0], 4), 2)
+    step = 1 - lax.rem(lax.div(role_ref[0], 4), 2)
     return turn, step, jnp.logical_or(turn == 1, turn == 2)
 
 
@@ -166,6 +166,10 @@
     )(*placed)
 
 
+def ring_pairs(ring):
+    return list(zip(ring, ring[1:] + ring[:1]))
+
+
 def body(embeddings):
     count, width = embeddings.shape
     blocks = lax.axis_size(AXES[0]) * lax.axis_size(AXES[1])
@@ -181,17 +185,22 @@
         far += [(at(q, 1), at(q, 0)), (at(q, 2), at(q, 3))]
         far += [(at(q, 3), at(q + 1, 1)), (at(q, 0), at(q - 1, 2))]
         swap += [(at(q, 0), at(q, 2)), (at(q, 2), at(q, 0)), (at(q, 1), at(q, 3)), (at(q, 3), at(q, 1))]
-        if q % 2 == 0:
+        if q % 2 == 1:
             even += [(at(q, 1), at(q, 2)), (at(q, 2), at(q, 1))]
             odd += [(at(q, 3), at(q + 1, 0)), (at(q, 0), at(q - 1, 3))]
             rows += [(at(q, 1), at(q, 0)), (at(q, 2), at(q, 3))]
-            ends += [(at(q, 1), at(q - 1, 3)), (at(q, 2), at(q + 1, 0))]
+            for ring in (
+                (at(q, 1), at(q - 1, 3), at(q - 1, 1)),
+                (at(q, 2), at(q + 1, 0), at(q + 1, 2)),
+                (at(q, 0), at(q, 3)),
+            ):
+                ends += ring_pairs(ring)
         else:
             for ring in (
                 (at(q, 0), at(q - 1, 3), at(q - 1, 1), at(q, 2)),
                 (at(q, 3), at(q + 1, 0), at(q + 1, 2), at(q, 1)),
             ):
-                cross += [(ring[i], ring[(i + 1) % 4]) for i in range(4)]
+                cross += ring_pairs(ring)
 
     def send(value, pairs):
         return lax.ppermute(value, AXES, pairs)

time: 51.6 us -> 51.2 us (level)
  the two profiles are of different devices: /device:TPU:4 before, /device:TPU:0 now
where the time goes in v6:
time: 51.2 us; the launch traced here: 50.9 us
  waiting for transfers between devices  23.8 us (46%)
  Pallas kernels  14.1 us (28%)
  starting transfers between devices  11.2 us (22%)
  local copies, waits for them, and re-layouts  1.62 us (3%)
    ppermute x10, waiting for transfers between devices, send(): return lax.ppermute(value, AXES, pairs)  23.8 us
    pallas_call x9, Pallas kernels, call(): pl.pallas_call(kernel, out_shape=[jax.ShapeDtypeStruct(*o) if last else p...  14.1 us
    ppermute x10, starting transfers between devices, send(): return lax.ppermute(value, AXES, pairs)  11.2 us
    unnamed x2, local copies, waits for them, and re-layouts  1.62 us
  transfers between devices with their start and end apart: 10, of which 4 were waited for; matrix products, arithmetic and copies ran while one was open for 0% of the time, Pallas kernels for 26%

profile of v6, /device:TPU:0, one launch (start us, length us, event | category | flops | bytes accessed | tf_op | source)
XLA Modules:
  0.0 50.9 jit_solution(11159314905541768194)
XLA Ops:
  0.0 0.5 collective-permute-start
  0.5 5.6 %collective-permute-start.1 = (bf16[1024,1024]{1,0:T(8,128)(2,1)}, bf16[1024,1024]{1,0:T(8,128)(2,1)S(1)}, u32[]{:S(2)}, u32[]{:S(2)}) collective-permute-start(bf16[1024,1024]{1,0:T(8,128)(2,1)} %rows_ref), channel_id=1, source_target_pairs={{1,0},{2,3},{3,5},{0,30},{5,4},{6,7},{7,9},{4,2},{9,8},{10,11},{11... | collective-permute-start | bytes 6291464 | tf_op jit(solution)/shard_map/ppermute | solution.py:206
  6.1 0.0 copy-start
  6.1 1.6 %copy-done = bf16[1024,1024]{1,0:T(8,128)(2,1)S(1)} copy-done((bf16[1024,1024]{1,0:T(8,128)(2,1)S(1)}, bf16[1024,1024]{1,0:T(8,128)(2,1)}, u32[]{:S(2)}) %copy-start) | copy-done | bytes 2097176
  7.7 2.9 %shard_map.17 = (bf16[1024,1024]{1,0:T(8,128)(2,1)S(1)}, f32[8,1024]{1,0:T(8,128)S(1)}, bf16[256,1024]{1,0:T(8,128)(2,1)S(1)}, bf16[256,1024]{1,0:T(8,128)(2,1)S(1)}) custom-call(bf16[1024,1024]{1,0:T(8,128)(2,1)S(1)} %copy-done), custom_call_target="tpu_custom_call" | custom-call | tf_op jit(solution)/shard_map/pallas_call | solution.py:160
  10.7 1.3 %collective-permute-start.4 = (bf16[256,1024]{1,0:T(8,128)(2,1)S(1)}, bf16[256,1024]{1,0:T(8,128)(2,1)S(1)}, u32[]{:S(2)}, u32[]{:S(2)}) collective-permute-start(bf16[256,1024]{1,0:T(8,128)(2,1)S(1)} %get-tuple-element.33), channel_id=1, source_target_pairs={{7,8},{4,3},{15,16},{12,11},{23,24},{20,19},{31,0},{28,27}} | collective-permute-start | bytes 1572872 | tf_op jit(solution)/shard_map/ppermute | solution.py:206
  12.0 1.3 %collective-permute-start.3 = (bf16[256,1024]{1,0:T(8,128)(2,1)S(1)}, bf16[256,1024]{1,0:T(8,128)(2,1)S(1)}, u32[]{:S(2)}, u32[]{:S(2)}) collective-permute-start(bf16[256,1024]{1,0:T(8,128)(2,1)S(1)} %get-tuple-element.32), channel_id=1, source_target_pairs={{7,8},{4,3},{15,16},{12,11},{23,24},{20,19},{31,0},{28,27}} | collective-permute-start | bytes 1572872 | tf_op jit(solution)/shard_map/ppermute | solution.py:206
  13.3 0.0 collective-permute-done.rows_ref
  13.3 0.7 %shard_map.18 = (bf16[1024,1024]{1,0:T(8,128)(2,1)S(1)}, bf16[256,1024]{1,0:T(8,128)(2,1)S(1)}, bf16[256,1024]{1,0:T(8,128)(2,1)S(1)}) custom-call(bf16[1024,1024]{1,0:T(8,128)(2,1)S(1)} %collective-permute-done.rows_ref), custom_call_target="tpu_custom_call" | custom-call | tf_op jit(solution)/shard_map/pallas_call | solution.py:160
  14.0 0.7 %collective-permute-start.6 = (bf16[256,1024]{1,0:T(8,128)(2,1)S(1)}, bf16[256,1024]{1,0:T(8,128)(2,1)S(1)}, u32[]{:S(2)}, u32[]{:S(2)}) collective-permute-start(bf16[256,1024]{1,0:T(8,128)(2,1)S(1)} %get-tuple-element.39), channel_id=1, source_target_pairs={{5,6},{6,5},{13,14},{14,13},{21,22},{22,21},{29,30},{30,29}} | collective-permute-start | bytes 1572872 | tf_op jit(solution)/shard_map/ppermute | solution.py:206
  14.7 0.7 %collective-permute-start.5 = (bf16[256,1024]{1,0:T(8,128)(2,1)S(1)}, bf16[256,1024]{1,0:T(8,128)(2,1)S(1)}, u32[]{:S(2)}, u32[]{:S(2)}) collective-permute-start(bf16[256,1024]{1,0:T(8,128)(2,1)S(1)} %get-tuple-element.37), channel_id=1, source_target_pairs={{5,6},{6,5},{13,14},{14,13},{21,22},{22,21},{29,30},{30,29}} | collective-permute-start | bytes 1572872 | tf_op jit(solution)/shard_map/ppermute | solution.py:206
  15.4 14.6 %collective-permute-done.1.rows_ref = bf16[1024,1024]{1,0:T(8,128)(2,1)S(1)} collective-permute-done((bf16[1024,1024]{1,0:T(8,128)(2,1)}, bf16[1024,1024]{1,0:T(8,128)(2,1)S(1)}, u32[]{:S(2)}, u32[]{:S(2)}) %collective-permute-start.1) | collective-permute-done | bytes 2097184 | tf_op jit(solution)/shard_map/ppermute | solution.py:206
  30.0 5.4 %shard_map.20 = (bf16[1024,1024]{1,0:T(8,128)(2,1)S(1)}, f32[8,1024]{1,0:T(8,128)S(1)}, f32[16,1024]{1,0:T(8,128)S(1)}) custom-call(s32[1]{0:T(128)} %bitcast.role_ref, bf16[1024,1024]{1,0:T(8,128)(2,1)S(1)} %collective-permute-done.1.rows_ref, bf16[1024,1024]{1,0:T(8,128)(2,1)S(1)} %get-tuple-element.28.unit_ref, ...), custom_call_target="tpu_custom_call" | custom-call | tf_op jit(solution)/shard_map/pallas_call | solution.py:160
  35.4 0.1 collective-permute-start.2
  35.5 1.1 %collective-permute-done.4.part_ref = bf16[256,1024]{1,0:T(8,128)(2,1)S(1)} collective-permute-done((bf16[256,1024]{1,0:T(8,128)(2,1)S(1)}, bf16[256,1024]{1,0:T(8,128)(2,1)S(1)}, u32[]{:S(2)}, u32[]{:S(2)}) %collective-permute-start.4) | collective-permute-done | bytes 524320 | tf_op jit(solution)/shard_map/ppermute | solution.py:206
  36.6 0.9 %shard_map.21 = (f32[8,512]{1,0:T(8,128)S(1)}, f32[4,1024]{1,0:T(4,128)S(1)}) custom-call(s32[1]{0:T(128)} %bitcast.role_ref, bf16[256,1024]{1,0:T(8,128)(2,1)S(1)} %collective-permute-done.4.part_ref, bf16[1024,1024]{1,0:T(8,128)(2,1)S(1)} %get-tuple-element.28.unit_ref), custom_call_target="tpu_custom_call" | custom-call | tf_op jit(solution)/shard_map/pallas_call | solution.py:160
  37.5 4.9 %collective-permute-done.3.part_ref = bf16[256,1024]{1,0:T(8,128)(2,1)S(1)} collective-permute-done((bf16[256,1024]{1,0:T(8,128)(2,1)S(1)}, bf16[256,1024]{1,0:T(8,128)(2,1)S(1)}, u32[]{:S(2)}, u32[]{:S(2)}) %collective-permute-start.3) | collective-permute-done | bytes 524320 | tf_op jit(solution)/shard_map/ppermute | solution.py:206
  42.4 0.9 %shard_map.22 = (f32[8,512]{1,0:T(8,128)S(1)}, f32[4,1024]{1,0:T(4,128)S(1)}) custom-call(s32[1]{0:T(128)} %bitcast.role_ref, bf16[256,1024]{1,0:T(8,128)(2,1)S(1)} %collective-permute-done.3.part_ref, bf16[1024,1024]{1,0:T(8,128)(2,1)S(1)} %get-tuple-element.28.unit_ref, f32[8,512]{1,0:T(8,128)S(1)} %get-tuple-element.34.refs_0_, ...), custom_call_target="tpu_custom_call" | custom-call | tf_op jit(solution)/shard_map/pallas_call | solution.py:160
  43.3 0.1 collective-permute-start.8
  43.4 0.0 collective-permute-done.6.part_ref
  43.4 0.0 collective-permute-done.5.part_ref
  43.4 0.2 shard_map.24
  43.6 0.7 %collective-permute-start.7 = (f32[8,512]{1,0:T(8,128)S(1)}, f32[8,512]{1,0:T(8,128)S(1)}, u32[]{:S(2)}, u32[]{:S(2)}) collective-permute-start(f32[8,512]{1,0:T(8,128)S(1)} %get-tuple-element.42), channel_id=1, source_target_pairs={{5,4},{6,7},{13,12},{14,15},{21,20},{22,23},{29,28},{30,31}} | collective-permute-start | bytes 49160 | tf_op jit(solution)/shard_map/ppermute | solution.py:206
  44.3 0.3 collective-permute-start.9
  44.6 2.4 %shard_map.19.own_partner_ref = f32[8,1024]{1,0:T(8,128)S(1)} custom-call(bf16[1024,1024]{1,0:T(8,128)(2,1)S(1)} %get-tuple-element.28.unit_ref, bf16[1024,1024]{1,0:T(8,128)(2,1)S(1)} %get-tuple-element.29.partner_ref), custom_call_target="tpu_custom_call" | custom-call | tf_op jit(solution)/shard_map/pallas_call | solution.py:160
  47.0 0.0 collective-permute-done.8.cross_ref
  47.0 0.0 collective-permute-done.2.far_ref
  47.0 0.0 collective-permute-done.7.rows_ref
  47.0 3.2 %collective-permute-done.9.ends_ref = f32[8,512]{1,0:T(8,128)S(1)} collective-permute-done((f32[8,512]{1,0:T(8,128)S(1)}, f32[8,512]{1,0:T(8,128)S(1)}, u32[]{:S(2)}, u32[]{:S(2)}) %collective-permute-start.9) | collective-permute-done | bytes 16416 | tf_op jit(solution)/shard_map/ppermute | solution.py:206
  50.2 0.7 %shard_map.25 = f32[40,1024]{1,0:T(8,128)} custom-call(s32[1]{0:T(128)} %bitcast.role_ref, f32[8,1024]{1,0:T(8,128)S(1)} %get-tuple-element.27.own_ref, f32[8,1024]{1,0:T(8,128)S(1)} %shard_map.19.own_partner_ref, f32[8,1024]{1,0:T(8,128)S(1)} %get-tuple-element.30.own_far_ref, f32[16,1024]{1,0:T(8,128)S(1)} %collective-permute-done.2.far_ref, ...), custom_call_target="tpu_custom_call" | custom-call | tf_op jit(solution)/shard_map/pallas_call | solution.py:160
  (1 shorter events, 0.0 us)
Async XLA Ops:
  0.0 13.3 %collective-permute-start = (bf16[1024,1024]{1,0:T(8,128)(2,1)}, bf16[1024,1024]{1,0:T(8,128)(2,1)S(1)}, u32[]{:S(2)}, u32[]{:S(2)}) collective-permute-start(bf16[1024,1024]{1,0:T(8,128)(2,1)} %rows_ref), channel_id=1, source_target_pairs={{0,2},{2,0},{1,3},{3,1},{4,6},{6,4},{5,7},{7,5},{8,10},{10,8},{9,1... | collective-permute-start | bytes 6291464 | tf_op jit(solution)/shard_map/ppermute | solution.py:206
  0.5 29.5 %collective-permute-start.1 = (bf16[1024,1024]{1,0:T(8,128)(2,1)}, bf16[1024,1024]{1,0:T(8,128)(2,1)S(1)}, u32[]{:S(2)}, u32[]{:S(2)}) collective-permute-start(bf16[1024,1024]{1,0:T(8,128)(2,1)} %rows_ref), channel_id=1, source_target_pairs={{1,0},{2,3},{3,5},{0,30},{5,4},{6,7},{7,9},{4,2},{9,8},{10,11},{11... | collective-permute-start | bytes 6291464 | tf_op jit(solution)/shard_map/ppermute | solution.py:206
  6.1 1.6 %copy-start = (bf16[1024,1024]{1,0:T(8,128)(2,1)S(1)}, bf16[1024,1024]{1,0:T(8,128)(2,1)}, u32[]{:S(2)}) copy-start(bf16[1024,1024]{1,0:T(8,128)(2,1)} %rows_ref) | copy-start | bytes 6291460
  10.7 25.9 %collective-permute-start.4 = (bf16[256,1024]{1,0:T(8,128)(2,1)S(1)}, bf16[256,1024]{1,0:T(8,128)(2,1)S(1)}, u32[]{:S(2)}, u32[]{:S(2)}) collective-permute-start(bf16[256,1024]{1,0:T(8,128)(2,1)S(1)} %get-tuple-element.33), channel_id=1, source_target_pairs={{7,8},{4,3},{15,16},{12,11},{23,24},{20,19},{31,0},{28,27}} | collective-permute-start | bytes 1572872 | tf_op jit(solution)/shard_map/ppermute | solution.py:206
  12.0 30.4 %collective-permute-start.3 = (bf16[256,1024]{1,0:T(8,128)(2,1)S(1)}, bf16[256,1024]{1,0:T(8,128)(2,1)S(1)}, u32[]{:S(2)}, u32[]{:S(2)}) collective-permute-start(bf16[256,1024]{1,0:T(8,128)(2,1)S(1)} %get-tuple-element.32), channel_id=1, source_target_pairs={{7,8},{4,3},{15,16},{12,11},{23,24},{20,19},{31,0},{28,27}} | collective-permute-start | bytes 1572872 | tf_op jit(solution)/shard_map/ppermute | solution.py:206
  14.0 29.4 %collective-permute-start.6 = (bf16[256,1024]{1,0:T(8,128)(2,1)S(1)}, bf16[256,1024]{1,0:T(8,128)(2,1)S(1)}, u32[]{:S(2)}, u32[]{:S(2)}) collective-permute-start(bf16[256,1024]{1,0:T(8,128)(2,1)S(1)} %get-tuple-element.39), channel_id=1, source_target_pairs={{5,6},{6,5},{13,14},{14,13},{21,22},{22,21},{29,30},{30,29}} | collective-permute-start | bytes 1572872 | tf_op jit(solution)/shard_map/ppermute | solution.py:206
  14.7 28.7 %collective-permute-start.5 = (bf16[256,1024]{1,0:T(8,128)(2,1)S(1)}, bf16[256,1024]{1,0:T(8,128)(2,1)S(1)}, u32[]{:S(2)}, u32[]{:S(2)}) collective-permute-start(bf16[256,1024]{1,0:T(8,128)(2,1)S(1)} %get-tuple-element.37), channel_id=1, source_target_pairs={{5,6},{6,5},{13,14},{14,13},{21,22},{22,21},{29,30},{30,29}} | collective-permute-start | bytes 1572872 | tf_op jit(solution)/shard_map/ppermute | solution.py:206
  35.4 11.6 %collective-permute-start.2 = (f32[16,1024]{1,0:T(8,128)S(1)}, f32[16,1024]{1,0:T(8,128)S(1)}, u32[]{:S(2)}, u32[]{:S(2)}) collective-permute-start(f32[16,1024]{1,0:T(8,128)S(1)} %get-tuple-element.31), channel_id=1, source_target_pairs={{0,1},{3,2},{5,3},{30,0},{4,5},{7,6},{9,7},{2,4},{8,9},{11,10},{13... | collective-permute-start | bytes 196616 | tf_op jit(solution)/shard_map/ppermute | solution.py:206
  43.3 3.7 %collective-permute-start.8 = (f32[8,512]{1,0:T(8,128)S(1)}, f32[8,512]{1,0:T(8,128)S(1)}, u32[]{:S(2)}, u32[]{:S(2)}) collective-permute-start(f32[8,512]{1,0:T(8,128)S(1)} %get-tuple-element.43), channel_id=1, source_target_pairs={{0,31},{31,29},{29,2},{2,0},{3,4},{4,6},{6,1},{1,3},{8,7},{7,5},{5... | collective-permute-start | bytes 49160 | tf_op jit(solution)/shard_map/ppermute | solution.py:206
  43.6 3.4 %collective-permute-start.7 = (f32[8,512]{1,0:T(8,128)S(1)}, f32[8,512]{1,0:T(8,128)S(1)}, u32[]{:S(2)}, u32[]{:S(2)}) collective-permute-start(f32[8,512]{1,0:T(8,128)S(1)} %get-tuple-element.42), channel_id=1, source_target_pairs={{5,4},{6,7},{13,12},{14,15},{21,20},{22,23},{29,28},{30,31}} | collective-permute-start | bytes 49160 | tf_op jit(solution)/shard_map/ppermute | solution.py:206
  44.3 5.9 %collective-permute-start.9 = (f32[8,512]{1,0:T(8,128)S(1)}, f32[8,512]{1,0:T(8,128)S(1)}, u32[]{:S(2)}, u32[]{:S(2)}) collective-permute-start(f32[8,512]{1,0:T(8,128)S(1)} %get-tuple-element.44), channel_id=1, source_target_pairs={{5,3},{3,1},{1,5},{6,8},{8,10},{10,6},{4,7},{7,4},{13,11},{11,9},{... | collective-permute-start | bytes 49160 | tf_op jit(solution)/shard_map/ppermute | solution.py:206

commit v7 on v4

--- a/solution.py
+++ b/solution.py
@@ -11,7 +11,7 @@
 AXES = ("blk", "grp")
 TILE = 128
 STEP = 256
-PARTS = 2
+PARTS = 1
 OFFSETS = 5
 VMEM_LIMIT = 16 << 20
 F32, BF16 = jnp.float32, jnp.bfloat16
@@ -46,7 +46,7 @@
 
 def place(role_ref):
     turn = lax.rem(role_ref[0], 4)
-    step = lax.rem(lax.div(role_ref[0], 4), 2)
+    step = 1 - lax.rem(lax.div(role_ref[0], 4), 2)
     return turn, step, jnp.logical_or(turn == 1, turn == 2)
 
 
@@ -181,13 +181,20 @@
         far += [(at(q, 1), at(q, 0)), (at(q, 2), at(q, 3))]
         far += [(at(q, 3), at(q + 1, 1)), (at(q, 0), at(q - 1, 2))]
         swap += [(at(q, 0), at(q, 2)), (at(q, 2), at(q, 0)), (at(q, 1), at(q, 3)), (at(q, 3), at(q, 1))]
-        if q % 2 == 0:
+        beside = q ^ 1
+        if q % 2 == 1:
             even += [(at(q, 1), at(q, 2)), (at(q, 2), at(q, 1))]
             odd += [(at(q, 3), at(q + 1, 0)), (at(q, 0), at(q - 1, 3))]
             rows += [(at(q, 1), at(q, 0)), (at(q, 2), at(q, 3))]
             ends += [(at(q, 1), at(q - 1, 3)), (at(q, 2), at(q + 1, 0))]
+            ends += [(at(q, 0), at(q, 3)), (at(q, 3), at(q, 0))]
+            cross += [(at(q, 3), at(q, 1)), (at(q, 0), at(q, 2))]
+            cross += [(at(q, 1), at(beside, 1)), (at(q, 2), at(beside, 2))]
         else:
             cross += [(at(q, 0), at(q - 1, 3)), (at(q, 3), at(q + 1, 0))]
+            cross += [(at(q, 1), at(q, 3)), (at(q, 2), at(q, 0))]
+            ends += [(at(q, 3), at(q, 1)), (at(q, 0), at(q, 2))]
+            ends += [(at(q, 1), at(beside, 1)), (at(q, 2), at(beside, 2))]
 
     def send(value, pairs):
         return lax.ppermute(value, AXES, pairs)

time: 52.7 us -> 51.3 us (0.973)
  the two profiles are of different devices: /device:TPU:4 before, /device:TPU:0 now
where the time goes in v7:
time: 51.3 us; the launch traced here: 51.1 us
  waiting for transfers between devices  26.3 us (51%)
  Pallas kernels  13.6 us (27%)
  starting transfers between devices  9.45 us (18%)
  local copies, waits for them, and re-layouts  1.62 us (3%)
    ppermute x8, waiting for transfers between devices, send(): return lax.ppermute(value, AXES, pairs)  26.3 us
    pallas_call x7, Pallas kernels, call(): pl.pallas_call(kernel, out_shape=[jax.ShapeDtypeStruct(*o) if last else p...  13.6 us
    ppermute x8, starting transfers between devices, send(): return lax.ppermute(value, AXES, pairs)  9.45 us
    unnamed x2, local copies, waits for them, and re-layouts  1.62 us
  transfers between devices with their start and end apart: 8, of which 3 were waited for; matrix products, arithmetic and copies ran while one was open for 0% of the time, Pallas kernels for 25%

profile of v7, /device:TPU:0, one launch (start us, length us, event | category | flops | bytes accessed | tf_op | source)
XLA Modules:
  0.0 51.1 jit_solution(2815578225991703596)
XLA Ops:
  0.0 0.5 collective-permute-start
  0.5 5.6 %collective-permute-start.1 = (bf16[1024,1024]{1,0:T(8,128)(2,1)}, bf16[1024,1024]{1,0:T(8,128)(2,1)S(1)}, u32[]{:S(2)}, u32[]{:S(2)}) collective-permute-start(bf16[1024,1024]{1,0:T(8,128)(2,1)} %rows_ref), channel_id=1, source_target_pairs={{1,0},{2,3},{3,5},{0,30},{5,4},{6,7},{7,9},{4,2},{9,8},{10,11},{11... | collective-permute-start | bytes 6291464 | tf_op jit(solution)/shard_map/ppermute | solution.py:200
  6.1 0.0 copy-start
  6.1 1.6 %copy-done = bf16[1024,1024]{1,0:T(8,128)(2,1)S(1)} copy-done((bf16[1024,1024]{1,0:T(8,128)(2,1)S(1)}, bf16[1024,1024]{1,0:T(8,128)(2,1)}, u32[]{:S(2)}) %copy-start) | copy-done | bytes 2097176
  7.7 3.0 %shard_map.17 = (bf16[1024,1024]{1,0:T(8,128)(2,1)S(1)}, f32[8,1024]{1,0:T(8,128)S(1)}, bf16[512,1024]{1,0:T(8,128)(2,1)S(1)}) custom-call(bf16[1024,1024]{1,0:T(8,128)(2,1)S(1)} %copy-done), custom_call_target="tpu_custom_call" | custom-call | tf_op jit(solution)/shard_map/pallas_call | solution.py:160
  10.7 1.3 %collective-permute-start.3 = (bf16[512,1024]{1,0:T(8,128)(2,1)S(1)}, bf16[512,1024]{1,0:T(8,128)(2,1)S(1)}, u32[]{:S(2)}, u32[]{:S(2)}) collective-permute-start(bf16[512,1024]{1,0:T(8,128)(2,1)S(1)} %get-tuple-element.26), channel_id=1, source_target_pairs={{7,8},{4,3},{15,16},{12,11},{23,24},{20,19},{31,0},{28,27}} | collective-permute-start | bytes 3145736 | tf_op jit(solution)/shard_map/ppermute | solution.py:200
  12.0 0.0 collective-permute-done.rows_ref
  12.0 0.7 %shard_map.18 = (bf16[1024,1024]{1,0:T(8,128)(2,1)S(1)}, bf16[512,1024]{1,0:T(8,128)(2,1)S(1)}) custom-call(bf16[1024,1024]{1,0:T(8,128)(2,1)S(1)} %collective-permute-done.rows_ref), custom_call_target="tpu_custom_call" | custom-call | tf_op jit(solution)/shard_map/pallas_call | solution.py:160
  12.7 0.7 %collective-permute-start.4 = (bf16[512,1024]{1,0:T(8,128)(2,1)S(1)}, bf16[512,1024]{1,0:T(8,128)(2,1)S(1)}, u32[]{:S(2)}, u32[]{:S(2)}) collective-permute-start(bf16[512,1024]{1,0:T(8,128)(2,1)S(1)} %get-tuple-element.28), channel_id=1, source_target_pairs={{5,6},{6,5},{13,14},{14,13},{21,22},{22,21},{29,30},{30,29}} | collective-permute-start | bytes 3145736 | tf_op jit(solution)/shard_map/ppermute | solution.py:200
  13.4 16.6 %collective-permute-done.1.rows_ref = bf16[1024,1024]{1,0:T(8,128)(2,1)S(1)} collective-permute-done((bf16[1024,1024]{1,0:T(8,128)(2,1)}, bf16[1024,1024]{1,0:T(8,128)(2,1)S(1)}, u32[]{:S(2)}, u32[]{:S(2)}) %collective-permute-start.1) | collective-permute-done | bytes 2097184 | tf_op jit(solution)/shard_map/ppermute | solution.py:200
  30.0 5.4 %shard_map.20 = (bf16[1024,1024]{1,0:T(8,128)(2,1)S(1)}, f32[8,1024]{1,0:T(8,128)S(1)}, f32[16,1024]{1,0:T(8,128)S(1)}) custom-call(s32[1]{0:T(128)} %bitcast.role_ref, bf16[1024,1024]{1,0:T(8,128)(2,1)S(1)} %collective-permute-done.1.rows_ref, bf16[1024,1024]{1,0:T(8,128)(2,1)S(1)} %get-tuple-element.22.unit_ref, ...), custom_call_target="tpu_custom_call" | custom-call | tf_op jit(solution)/shard_map/pallas_call | solution.py:160
  35.4 0.1 collective-permute-start.2
  35.5 6.7 %collective-permute-done.3.part_ref = bf16[512,1024]{1,0:T(8,128)(2,1)S(1)} collective-permute-done((bf16[512,1024]{1,0:T(8,128)(2,1)S(1)}, bf16[512,1024]{1,0:T(8,128)(2,1)S(1)}, u32[]{:S(2)}, u32[]{:S(2)}) %collective-permute-start.3) | collective-permute-done | bytes 1048608 | tf_op jit(solution)/shard_map/ppermute | solution.py:200
  42.2 1.5 %shard_map.21 = (f32[8,512]{1,0:T(8,128)S(1)}, f32[4,1024]{1,0:T(4,128)S(1)}) custom-call(s32[1]{0:T(128)} %bitcast.role_ref, bf16[512,1024]{1,0:T(8,128)(2,1)S(1)} %collective-permute-done.3.part_ref, bf16[1024,1024]{1,0:T(8,128)(2,1)S(1)} %get-tuple-element.22.unit_ref), custom_call_target="tpu_custom_call" | custom-call | tf_op jit(solution)/shard_map/pallas_call | solution.py:160
  43.7 0.1 collective-permute-start.6
  43.8 0.0 collective-permute-done.4.part_ref
  43.8 0.7 %collective-permute-start.5 = (f32[8,512]{1,0:T(8,128)S(1)}, f32[8,512]{1,0:T(8,128)S(1)}, u32[]{:S(2)}, u32[]{:S(2)}) collective-permute-start(f32[8,512]{1,0:T(8,128)S(1)} %get-tuple-element.30), channel_id=1, source_target_pairs={{5,4},{6,7},{13,12},{14,15},{21,20},{22,23},{29,28},{30,31}} | collective-permute-start | bytes 49160 | tf_op jit(solution)/shard_map/ppermute | solution.py:200
  44.5 0.5 %collective-permute-start.7 = (f32[8,512]{1,0:T(8,128)S(1)}, f32[8,512]{1,0:T(8,128)S(1)}, u32[]{:S(2)}, u32[]{:S(2)}) collective-permute-start(f32[8,512]{1,0:T(8,128)S(1)} %get-tuple-element.32), channel_id=1, source_target_pairs={{3,1},{0,2},{1,5},{2,6},{5,3},{6,8},{4,7},{7,4},{11,9},{8,10},{9,1... | collective-permute-start | bytes 49160 | tf_op jit(solution)/shard_map/ppermute | solution.py:200
  45.0 2.4 %shard_map.19.own_partner_ref = f32[8,1024]{1,0:T(8,128)S(1)} custom-call(bf16[1024,1024]{1,0:T(8,128)(2,1)S(1)} %get-tuple-element.22.unit_ref, bf16[1024,1024]{1,0:T(8,128)(2,1)S(1)} %get-tuple-element.23.partner_ref), custom_call_target="tpu_custom_call" | custom-call | tf_op jit(solution)/shard_map/pallas_call | solution.py:160
  47.4 0.0 collective-permute-done.6.cross_ref
  47.4 0.0 collective-permute-done.2.far_ref
  47.4 0.0 collective-permute-done.5.rows_ref
  47.4 3.0 %collective-permute-done.7.ends_ref = f32[8,512]{1,0:T(8,128)S(1)} collective-permute-done((f32[8,512]{1,0:T(8,128)S(1)}, f32[8,512]{1,0:T(8,128)S(1)}, u32[]{:S(2)}, u32[]{:S(2)}) %collective-permute-start.7) | collective-permute-done | bytes 16416 | tf_op jit(solution)/shard_map/ppermute | solution.py:200
  50.4 0.7 %shard_map.23 = f32[40,1024]{1,0:T(8,128)} custom-call(s32[1]{0:T(128)} %bitcast.role_ref, f32[8,1024]{1,0:T(8,128)S(1)} %get-tuple-element.21.own_ref, f32[8,1024]{1,0:T(8,128)S(1)} %shard_map.19.own_partner_ref, f32[8,1024]{1,0:T(8,128)S(1)} %get-tuple-element.24.own_far_ref, f32[16,1024]{1,0:T(8,128)S(1)} %collective-permute-done.2.far_ref, ...), custom_call_target="tpu_custom_call" | custom-call | tf_op jit(solution)/shard_map/pallas_call | solution.py:160
  (1 shorter events, 0.0 us)
Async XLA Ops:
  0.0 12.0 %collective-permute-start = (bf16[1024,1024]{1,0:T(8,128)(2,1)}, bf16[1024,1024]{1,0:T(8,128)(2,1)S(1)}, u32[]{:S(2)}, u32[]{:S(2)}) collective-permute-start(bf16[1024,1024]{1,0:T(8,128)(2,1)} %rows_ref), channel_id=1, source_target_pairs={{0,2},{2,0},{1,3},{3,1},{4,6},{6,4},{5,7},{7,5},{8,10},{10,8},{9,1... | collective-permute-start | bytes 6291464 | tf_op jit(solution)/shard_map/ppermute | solution.py:200
  0.5 29.5 %collective-permute-start.1 = (bf16[1024,1024]{1,0:T(8,128)(2,1)}, bf16[1024,1024]{1,0:T(8,128)(2,1)S(1)}, u32[]{:S(2)}, u32[]{:S(2)}) collective-permute-start(bf16[1024,1024]{1,0:T(8,128)(2,1)} %rows_ref), channel_id=1, source_target_pairs={{1,0},{2,3},{3,5},{0,30},{5,4},{6,7},{7,9},{4,2},{9,8},{10,11},{11... | collective-permute-start | bytes 6291464 | tf_op jit(solution)/shard_map/ppermute | solution.py:200
  6.1 1.6 %copy-start = (bf16[1024,1024]{1,0:T(8,128)(2,1)S(1)}, bf16[1024,1024]{1,0:T(8,128)(2,1)}, u32[]{:S(2)}) copy-start(bf16[1024,1024]{1,0:T(8,128)(2,1)} %rows_ref) | copy-start | bytes 6291460
  10.7 31.5 %collective-permute-start.3 = (bf16[512,1024]{1,0:T(8,128)(2,1)S(1)}, bf16[512,1024]{1,0:T(8,128)(2,1)S(1)}, u32[]{:S(2)}, u32[]{:S(2)}) collective-permute-start(bf16[512,1024]{1,0:T(8,128)(2,1)S(1)} %get-tuple-element.26), channel_id=1, source_target_pairs={{7,8},{4,3},{15,16},{12,11},{23,24},{20,19},{31,0},{28,27}} | collective-permute-start | bytes 3145736 | tf_op jit(solution)/shard_map/ppermute | solution.py:200
  12.7 31.1 %collective-permute-start.4 = (bf16[512,1024]{1,0:T(8,128)(2,1)S(1)}, bf16[512,1024]{1,0:T(8,128)(2,1)S(1)}, u32[]{:S(2)}, u32[]{:S(2)}) collective-permute-start(bf16[512,1024]{1,0:T(8,128)(2,1)S(1)} %get-tuple-element.28), channel_id=1, source_target_pairs={{5,6},{6,5},{13,14},{14,13},{21,22},{22,21},{29,30},{30,29}} | collective-permute-start | bytes 3145736 | tf_op jit(solution)/shard_map/ppermute | solution.py:200
  35.4 12.0 %collective-permute-start.2 = (f32[16,1024]{1,0:T(8,128)S(1)}, f32[16,1024]{1,0:T(8,128)S(1)}, u32[]{:S(2)}, u32[]{:S(2)}) collective-permute-start(f32[16,1024]{1,0:T(8,128)S(1)} %get-tuple-element.25), channel_id=1, source_target_pairs={{0,1},{3,2},{5,3},{30,0},{4,5},{7,6},{9,7},{2,4},{8,9},{11,10},{13... | collective-permute-start | bytes 196616 | tf_op jit(solution)/shard_map/ppermute | solution.py:200
  43.7 3.7 %collective-permute-start.6 = (f32[8,512]{1,0:T(8,128)S(1)}, f32[8,512]{1,0:T(8,128)S(1)}, u32[]{:S(2)}, u32[]{:S(2)}) collective-permute-start(f32[8,512]{1,0:T(8,128)S(1)} %get-tuple-element.31), channel_id=1, source_target_pairs={{0,31},{3,4},{1,3},{2,0},{7,5},{4,6},{5,1},{6,2},{8,7},{11,12},{9,... | collective-permute-start | bytes 49160 | tf_op jit(solution)/shard_map/ppermute | solution.py:200
  43.8 3.6 %collective-permute-start.5 = (f32[8,512]{1,0:T(8,128)S(1)}, f32[8,512]{1,0:T(8,128)S(1)}, u32[]{:S(2)}, u32[]{:S(2)}) collective-permute-start(f32[8,512]{1,0:T(8,128)S(1)} %get-tuple-element.30), channel_id=1, source_target_pairs={{5,4},{6,7},{13,12},{14,15},{21,20},{22,23},{29,28},{30,31}} | collective-permute-start | bytes 49160 | tf_op jit(solution)/shard_map/ppermute | solution.py:200
  44.5 5.9 %collective-permute-start.7 = (f32[8,512]{1,0:T(8,128)S(1)}, f32[8,512]{1,0:T(8,128)S(1)}, u32[]{:S(2)}, u32[]{:S(2)}) collective-permute-start(f32[8,512]{1,0:T(8,128)S(1)} %get-tuple-element.32), channel_id=1, source_target_pairs={{3,1},{0,2},{1,5},{2,6},{5,3},{6,8},{4,7},{7,4},{11,9},{8,10},{9,1... | collective-permute-start | bytes 49160 | tf_op jit(solution)/shard_map/ppermute | solution.py:200

commit v8 on v7

--- a/solution.py
+++ b/solution.py
@@ -11,7 +11,7 @@
 AXES = ("blk", "grp")
 TILE = 128
 STEP = 256
-PARTS = 1
+PARTS = 2
 OFFSETS = 5
 VMEM_LIMIT = 16 << 20
 F32, BF16 = jnp.float32, jnp.bfloat16
@@ -54,19 +54,15 @@
     unit_ref[...] = unit_of(rows_ref[...])
     size = part_refs[0].shape[0]
     for i, part_ref in enumerate(part_refs):
-        at = (len(part_refs) + i) * size
-        part_ref[...] = unit_ref[at : at + size, :]
+        part_ref[...] = unit_ref[i * size : (i + 1) * size, :]
     same = lax.broadcasted_iota(jnp.int32, (STEP, STEP), 0) == lax.broadcasted_iota(
         jnp.int32, (STEP, STEP), 1
     )
     best(scale, unit_ref, unit_ref, own_ref, same=same)
 
 
-def partner_kernel(rows_ref, partner_ref, *part_refs):
+def partner_kernel(rows_ref, partner_ref):
     partner_ref[...] = unit_of(rows_ref[...])
-    size = part_refs[0].shape[0]
-    for i, part_ref in enumerate(part_refs):
-        part_ref[...] = partner_ref[i * size : (i + 1) * size, :]
 
 
 def pair_kernel(scale, unit_ref, partner_ref, max_ref):
@@ -183,7 +179,7 @@
         swap += [(at(q, 0), at(q, 2)), (at(q, 2), at(q, 0)), (at(q, 1), at(q, 3)), (at(q, 3), at(q, 1))]
         beside = q ^ 1
         if q % 2 == 1:
-            even += [(at(q, 1), at(q, 2)), (at(q, 2), at(q, 1))]
+            even += [(at(q, 3), at(q, 2)), (at(q, 0), at(q, 1))]
             odd += [(at(q, 3), at(q + 1, 0)), (at(q, 0), at(q - 1, 3))]
             rows += [(at(q, 1), at(q, 0)), (at(q, 2), at(q, 3))]
             ends += [(at(q, 1), at(q - 1, 3)), (at(q, 2), at(q + 1, 0))]
@@ -204,15 +200,16 @@
     far_rows = send(embeddings, far)
     partner_rows = send(embeddings, swap)
     piece = ((size, width), BF16)
-    unit, own, *odd_parts = call(
+    unit, own, *pieces = call(
         functools.partial(own_kernel, scale),
-        [((count, width), BF16), ((tiles, count), F32)] + [piece] * PARTS,
+        [((count, width), BF16), ((tiles, count), F32)] + [piece] * (2 * PARTS),
         embeddings,
     )
-    odd_parts = [send(part, odd) for part in odd_parts]
-    partner, *even_parts = call(partner_kernel, [((count, width), BF16)] + [piece] * PARTS, partner_rows)
-    even_parts = [send(part, even) for part in even_parts]
+    (partner,) = call(partner_kernel, [((count, width), BF16)], partner_rows)
     (own_partner,) = call(functools.partial(pair_kernel, scale), [((tiles, count), F32)], unit, partner)
+    pieces, own_partner = lax.optimization_barrier((pieces, own_partner))
+    odd_parts = [send(part, odd) for part in pieces[PARTS:]]
+    even_parts = [send(part, even) for part in pieces[:PARTS]]
     far_unit, own_far, far_max = call(
         functools.partial(far_kernel, scale),
         [((count, width), BF16), ((tiles, count), F32), ((2 * tiles, count), F32)],

time: 51.3 us -> 54.6 us (1.064)
  starting transfers between devices: 9.45 us -> 14.9 us
  waiting for transfers between devices: 26.3 us -> 23.9 us
    ppermute x8 -> x10, starting transfers between devices: 9.45 us -> 14.9 us  [send(): return lax.ppermute(value, AXES, pairs)]
    ppermute x8 -> x10, waiting for transfers between devices: 26.3 us -> 23.9 us  [send(): return lax.ppermute(value, AXES, pairs)]
    pallas_call x7 -> x9, Pallas kernels: 13.6 us -> 13.9 us  [call(): pl.pallas_call(kernel, out_shape=[jax.ShapeDtypeStruct(*o) if last else p...]
  transfers between devices with their start and end apart: 8 -> 10, of which waited for: 3 -> 5; matrix products, arithmetic and copies ran while one was open for 0% -> 0% of each run, Pallas kernels for 25% -> 24%
where the time goes in v8:
time: 54.6 us; the launch traced here: 54.4 us
  waiting for transfers between devices  23.9 us (44%)
  starting transfers between devices  14.9 us (27%)
  Pallas kernels  13.9 us (25%)
  local copies, waits for them, and re-layouts  1.62 us (3%)
    ppermute x10, waiting for transfers between devices, send(): return lax.ppermute(value, AXES, pairs)  23.9 us
    ppermute x10, starting transfers between devices, send(): return lax.ppermute(value, AXES, pairs)  14.9 us
    pallas_call x9, Pallas kernels, call(): pl.pallas_call(kernel, out_shape=[jax.ShapeDtypeStruct(*o) if last else p...  13.9 us
    unnamed x2, local copies, waits for them, and re-layouts  1.62 us
  transfers between devices with their start and end apart: 10, of which 5 were waited for; matrix products, arithmetic and copies ran while one was open for 0% of the time, Pallas kernels for 24%

profile of v8, /device:TPU:0, one launch (start us, length us, event | category | flops | bytes accessed | tf_op | source)
XLA Modules:
  0.0 54.4 jit_solution(10106192993663722504)
XLA Ops:
  0.0 0.5 collective-permute-start
  0.5 5.6 %collective-permute-start.1 = (bf16[1024,1024]{1,0:T(8,128)(2,1)}, bf16[1024,1024]{1,0:T(8,128)(2,1)S(1)}, u32[]{:S(2)}, u32[]{:S(2)}) collective-permute-start(bf16[1024,1024]{1,0:T(8,128)(2,1)} %rows_ref), channel_id=1, source_target_pairs={{1,0},{2,3},{3,5},{0,30},{5,4},{6,7},{7,9},{4,2},{9,8},{10,11},{11... | collective-permute-start | bytes 6291464 | tf_op jit(solution)/shard_map/ppermute | solution.py:196
  6.1 0.0 copy-start
  6.1 1.6 %copy-done = bf16[1024,1024]{1,0:T(8,128)(2,1)S(1)} copy-done((bf16[1024,1024]{1,0:T(8,128)(2,1)S(1)}, bf16[1024,1024]{1,0:T(8,128)(2,1)}, u32[]{:S(2)}) %copy-start) | copy-done | bytes 2097176
  7.7 2.9 %shard_map.17 = (bf16[1024,1024]{1,0:T(8,128)(2,1)S(1)}, f32[8,1024]{1,0:T(8,128)S(1)}, bf16[256,1024]{1,0:T(8,128)(2,1)S(1)}, bf16[256,1024]{1,0:T(8,128)(2,1)S...) custom-call(bf16[1024,1024]{1,0:T(8,128)(2,1)S(1)} %copy-done), custom_call_target="tpu_custom_call" | custom-call | tf_op jit(solution)/shard_map/pallas_call | solution.py:156
  10.7 0.0 collective-permute-done.rows_ref
  10.7 0.7 %shard_map.18.partner_ref = bf16[1024,1024]{1,0:T(8,128)(2,1)S(1)} custom-call(bf16[1024,1024]{1,0:T(8,128)(2,1)S(1)} %collective-permute-done.rows_ref), custom_call_target="tpu_custom_call" | custom-call | tf_op jit(solution)/shard_map/pallas_call | solution.py:156
  11.4 2.4 %shard_map.19.own_partner_ref = f32[8,1024]{1,0:T(8,128)S(1)} custom-call(bf16[1024,1024]{1,0:T(8,128)(2,1)S(1)} %get-tuple-element.36.unit_ref, bf16[1024,1024]{1,0:T(8,128)(2,1)S(1)} %shard_map.18.partner_ref), custom_call_target="tpu_custom_call" | custom-call | tf_op jit(solution)/shard_map/pallas_call | solution.py:156
  13.7 1.3 %collective-permute-start.4 = (bf16[256,1024]{1,0:T(8,128)(2,1)S(1)}, bf16[256,1024]{1,0:T(8,128)(2,1)S(1)}, u32[]{:S(2)}, u32[]{:S(2)}) collective-permute-start(bf16[256,1024]{1,0:T(8,128)(2,1)S(1)} %get-tuple-element.41), channel_id=1, source_target_pairs={{7,8},{4,3},{15,16},{12,11},{23,24},{20,19},{31,0},{28,27}} | collective-permute-start | bytes 1572872 | tf_op jit(solution)/shard_map/ppermute | solution.py:196
  15.0 1.3 %collective-permute-start.3 = (bf16[256,1024]{1,0:T(8,128)(2,1)S(1)}, bf16[256,1024]{1,0:T(8,128)(2,1)S(1)}, u32[]{:S(2)}, u32[]{:S(2)}) collective-permute-start(bf16[256,1024]{1,0:T(8,128)(2,1)S(1)} %get-tuple-element.40), channel_id=1, source_target_pairs={{7,8},{4,3},{15,16},{12,11},{23,24},{20,19},{31,0},{28,27}} | collective-permute-start | bytes 1572872 | tf_op jit(solution)/shard_map/ppermute | solution.py:196
  16.3 0.7 %collective-permute-start.6 = (bf16[256,1024]{1,0:T(8,128)(2,1)S(1)}, bf16[256,1024]{1,0:T(8,128)(2,1)S(1)}, u32[]{:S(2)}, u32[]{:S(2)}) collective-permute-start(bf16[256,1024]{1,0:T(8,128)(2,1)S(1)} %get-tuple-element.47), channel_id=1, source_target_pairs={{7,6},{4,5},{15,14},{12,13},{23,22},{20,21},{31,30},{28,29}} | collective-permute-start | bytes 1572872 | tf_op jit(solution)/shard_map/ppermute | solution.py:196
  17.0 0.7 %collective-permute-start.5 = (bf16[256,1024]{1,0:T(8,128)(2,1)S(1)}, bf16[256,1024]{1,0:T(8,128)(2,1)S(1)}, u32[]{:S(2)}, u32[]{:S(2)}) collective-permute-start(bf16[256,1024]{1,0:T(8,128)(2,1)S(1)} %get-tuple-element.45), channel_id=1, source_target_pairs={{7,6},{4,5},{15,14},{12,13},{23,22},{20,21},{31,30},{28,29}} | collective-permute-start | bytes 1572872 | tf_op jit(solution)/shard_map/ppermute | solution.py:196
  17.7 12.2 %collective-permute-done.1.rows_ref = bf16[1024,1024]{1,0:T(8,128)(2,1)S(1)} collective-permute-done((bf16[1024,1024]{1,0:T(8,128)(2,1)}, bf16[1024,1024]{1,0:T(8,128)(2,1)S(1)}, u32[]{:S(2)}, u32[]{:S(2)}) %collective-permute-start.1) | collective-permute-done | bytes 2097184 | tf_op jit(solution)/shard_map/ppermute | solution.py:196
  30.0 5.4 %shard_map.20 = (bf16[1024,1024]{1,0:T(8,128)(2,1)S(1)}, f32[8,1024]{1,0:T(8,128)S(1)}, f32[16,1024]{1,0:T(8,128)S(1)}) custom-call(s32[1]{0:T(128)} %bitcast.role_ref, bf16[1024,1024]{1,0:T(8,128)(2,1)S(1)} %collective-permute-done.1.rows_ref, bf16[1024,1024]{1,0:T(8,128)(2,1)S(1)} %get-tuple-element.36.unit_ref, bf16[1024,1024]{1,0:T(8,128)(2,1)S(1)} %shard_map.18.partner_ref), custom_call_target="tpu_custom_call" | custom-call | tf_op jit(solution)/shard_map/pallas_call | solution.py:156
  35.4 0.1 collective-permute-start.2
  35.5 1.1 %collective-permute-done.4.part_ref = bf16[256,1024]{1,0:T(8,128)(2,1)S(1)} collective-permute-done((bf16[256,1024]{1,0:T(8,128)(2,1)S(1)}, bf16[256,1024]{1,0:T(8,128)(2,1)S(1)}, u32[]{:S(2)}, u32[]{:S(2)}) %collective-permute-start.4) | collective-permute-done | bytes 524320 | tf_op jit(solution)/shard_map/ppermute | solution.py:196
  36.6 0.9 %shard_map.21 = (f32[8,512]{1,0:T(8,128)S(1)}, f32[4,1024]{1,0:T(4,128)S(1)}) custom-call(s32[1]{0:T(128)} %bitcast.role_ref, bf16[256,1024]{1,0:T(8,128)(2,1)S(1)} %collective-permute-done.4.part_ref, bf16[1024,1024]{1,0:T(8,128)(2,1)S(1)} %get-tuple-element.36.unit_ref), custom_call_target="tpu_custom_call" | custom-call | tf_op jit(solution)/shard_map/pallas_call | solution.py:156
  37.5 4.7 %collective-permute-done.3.part_ref = bf16[256,1024]{1,0:T(8,128)(2,1)S(1)} collective-permute-done((bf16[256,1024]{1,0:T(8,128)(2,1)S(1)}, bf16[256,1024]{1,0:T(8,128)(2,1)S(1)}, u32[]{:S(2)}, u32[]{:S(2)}) %collective-permute-start.3) | collective-permute-done | bytes 524320 | tf_op jit(solution)/shard_map/ppermute | solution.py:196
  42.2 0.9 %shard_map.22 = (f32[8,512]{1,0:T(8,128)S(1)}, f32[4,1024]{1,0:T(4,128)S(1)}) custom-call(s32[1]{0:T(128)} %bitcast.role_ref, bf16[256,1024]{1,0:T(8,128)(2,1)S(1)} %collective-permute-done.3.part_ref, bf16[1024,1024]{1,0:T(8,128)(2,1)S(1)} %get-tuple-element.36.unit_ref, f32[8,512]{1,0:T(8,128)S(1)} %get-tuple-element.42.refs_0_, ...), custom_call_target="tpu_custom_call" | custom-call | tf_op jit(solution)/shard_map/pallas_call | solution.py:156
  43.1 4.0 %collective-permute-start.8 = (f32[8,512]{1,0:T(8,128)S(1)}, f32[8,512]{1,0:T(8,128)S(1)}, u32[]{:S(2)}, u32[]{:S(2)}) collective-permute-start(f32[8,512]{1,0:T(8,128)S(1)} %get-tuple-element.51), channel_id=1, source_target_pairs={{0,31},{3,4},{1,3},{2,0},{7,5},{4,6},{5,1},{6,2},{8,7},{11,12},{9,... | collective-permute-start | bytes 49160 | tf_op jit(solution)/shard_map/ppermute | solution.py:196
  47.2 0.0 collective-permute-done.6.part_ref
  47.2 0.0 collective-permute-done.5.part_ref
  47.2 0.7 %collective-permute-start.7 = (f32[8,512]{1,0:T(8,128)S(1)}, f32[8,512]{1,0:T(8,128)S(1)}, u32[]{:S(2)}, u32[]{:S(2)}) collective-permute-start(f32[8,512]{1,0:T(8,128)S(1)} %get-tuple-element.50), channel_id=1, source_target_pairs={{5,4},{6,7},{13,12},{14,15},{21,20},{22,23},{29,28},{30,31}} | collective-permute-start | bytes 49160 | tf_op jit(solution)/shard_map/ppermute | solution.py:196
  47.8 0.1 collective-permute-start.9
  47.9 0.0 collective-permute-done.2.far_ref
  47.9 0.7 %collective-permute-done.8.cross_ref = f32[8,512]{1,0:T(8,128)S(1)} collective-permute-done((f32[8,512]{1,0:T(8,128)S(1)}, f32[8,512]{1,0:T(8,128)S(1)}, u32[]{:S(2)}, u32[]{:S(2)}) %collective-permute-start.8) | collective-permute-done | bytes 16416 | tf_op jit(solution)/shard_map/ppermute | solution.py:196
  48.6 0.0 collective-permute-done.7.rows_ref
  48.6 5.2 %collective-permute-done.9.ends_ref = f32[8,512]{1,0:T(8,128)S(1)} collective-permute-done((f32[8,512]{1,0:T(8,128)S(1)}, f32[8,512]{1,0:T(8,128)S(1)}, u32[]{:S(2)}, u32[]{:S(2)}) %collective-permute-start.9) | collective-permute-done | bytes 16416 | tf_op jit(solution)/shard_map/ppermute | solution.py:196
  53.8 0.7 %shard_map.25 = f32[40,1024]{1,0:T(8,128)} custom-call(s32[1]{0:T(128)} %bitcast.role_ref, f32[8,1024]{1,0:T(8,128)S(1)} %get-tuple-element.31.own_ref, f32[8,1024]{1,0:T(8,128)S(1)} %shard_map.19.own_partner_ref, f32[8,1024]{1,0:T(8,128)S(1)} %get-tuple-element.38.own_far_ref, f32[16,1024]{1,0:T(8,128)S(1)} %collective-permute-done.2.far_ref, ...), custom_call_target="tpu_custom_call" | custom-call | tf_op jit(solution)/shard_map/pallas_call | solution.py:156
  (2 shorter events, 0.0 us)
Async XLA Ops:
  0.0 10.7 %collective-permute-start = (bf16[1024,1024]{1,0:T(8,128)(2,1)}, bf16[1024,1024]{1,0:T(8,128)(2,1)S(1)}, u32[]{:S(2)}, u32[]{:S(2)}) collective-permute-start(bf16[1024,1024]{1,0:T(8,128)(2,1)} %rows_ref), channel_id=1, source_target_pairs={{0,2},{2,0},{1,3},{3,1},{4,6},{6,4},{5,7},{7,5},{8,10},{10,8},{9,1... | collective-permute-start | bytes 6291464 | tf_op jit(solution)/shard_map/ppermute | solution.py:196
  0.5 29.5 %collective-permute-start.1 = (bf16[1024,1024]{1,0:T(8,128)(2,1)}, bf16[1024,1024]{1,0:T(8,128)(2,1)S(1)}, u32[]{:S(2)}, u32[]{:S(2)}) collective-permute-start(bf16[1024,1024]{1,0:T(8,128)(2,1)} %rows_ref), channel_id=1, source_target_pairs={{1,0},{2,3},{3,5},{0,30},{5,4},{6,7},{7,9},{4,2},{9,8},{10,11},{11... | collective-permute-start | bytes 6291464 | tf_op jit(solution)/shard_map/ppermute | solution.py:196
  6.1 1.6 %copy-start = (bf16[1024,1024]{1,0:T(8,128)(2,1)S(1)}, bf16[1024,1024]{1,0:T(8,128)(2,1)}, u32[]{:S(2)}) copy-start(bf16[1024,1024]{1,0:T(8,128)(2,1)} %rows_ref) | copy-start | bytes 6291460
  13.7 22.9 %collective-permute-start.4 = (bf16[256,1024]{1,0:T(8,128)(2,1)S(1)}, bf16[256,1024]{1,0:T(8,128)(2,1)S(1)}, u32[]{:S(2)}, u32[]{:S(2)}) collective-permute-start(bf16[256,1024]{1,0:T(8,128)(2,1)S(1)} %get-tuple-element.41), channel_id=1, source_target_pairs={{7,8},{4,3},{15,16},{12,11},{23,24},{20,19},{31,0},{28,27}} | collective-permute-start | bytes 1572872 | tf_op jit(solution)/shard_map/ppermute | solution.py:196
  15.0 27.2 %collective-permute-start.3 = (bf16[256,1024]{1,0:T(8,128)(2,1)S(1)}, bf16[256,1024]{1,0:T(8,128)(2,1)S(1)}, u32[]{:S(2)}, u32[]{:S(2)}) collective-permute-start(bf16[256,1024]{1,0:T(8,128)(2,1)S(1)} %get-tuple-element.40), channel_id=1, source_target_pairs={{7,8},{4,3},{15,16},{12,11},{23,24},{20,19},{31,0},{28,27}} | collective-permute-start | bytes 1572872 | tf_op jit(solution)/shard_map/ppermute | solution.py:196
  16.3 30.8 %collective-permute-start.6 = (bf16[256,1024]{1,0:T(8,128)(2,1)S(1)}, bf16[256,1024]{1,0:T(8,128)(2,1)S(1)}, u32[]{:S(2)}, u32[]{:S(2)}) collective-permute-start(bf16[256,1024]{1,0:T(8,128)(2,1)S(1)} %get-tuple-element.47), channel_id=1, source_target_pairs={{7,6},{4,5},{15,14},{12,13},{23,22},{20,21},{31,30},{28,29}} | collective-permute-start | bytes 1572872 | tf_op jit(solution)/shard_map/ppermute | solution.py:196
  17.0 30.1 %collective-permute-start.5 = (bf16[256,1024]{1,0:T(8,128)(2,1)S(1)}, bf16[256,1024]{1,0:T(8,128)(2,1)S(1)}, u32[]{:S(2)}, u32[]{:S(2)}) collective-permute-start(bf16[256,1024]{1,0:T(8,128)(2,1)S(1)} %get-tuple-element.45), channel_id=1, source_target_pairs={{7,6},{4,5},{15,14},{12,13},{23,22},{20,21},{31,30},{28,29}} | collective-permute-start | bytes 1572872 | tf_op jit(solution)/shard_map/ppermute | solution.py:196
  35.4 12.5 %collective-permute-start.2 = (f32[16,1024]{1,0:T(8,128)S(1)}, f32[16,1024]{1,0:T(8,128)S(1)}, u32[]{:S(2)}, u32[]{:S(2)}) collective-permute-start(f32[16,1024]{1,0:T(8,128)S(1)} %get-tuple-element.39), channel_id=1, source_target_pairs={{0,1},{3,2},{5,3},{30,0},{4,5},{7,6},{9,7},{2,4},{8,9},{11,10},{13... | collective-permute-start | bytes 196616 | tf_op jit(solution)/shard_map/ppermute | solution.py:196
  43.1 5.5 %collective-permute-start.8 = (f32[8,512]{1,0:T(8,128)S(1)}, f32[8,512]{1,0:T(8,128)S(1)}, u32[]{:S(2)}, u32[]{:S(2)}) collective-permute-start(f32[8,512]{1,0:T(8,128)S(1)} %get-tuple-element.51), channel_id=1, source_target_pairs={{0,31},{3,4},{1,3},{2,0},{7,5},{4,6},{5,1},{6,2},{8,7},{11,12},{9,... | collective-permute-start | bytes 49160 | tf_op jit(solution)/shard_map/ppermute | solution.py:196
  47.2 1.4 %collective-permute-start.7 = (f32[8,512]{1,0:T(8,128)S(1)}, f32[8,512]{1,0:T(8,128)S(1)}, u32[]{:S(2)}, u32[]{:S(2)}) collective-permute-start(f32[8,512]{1,0:T(8,128)S(1)} %get-tuple-element.50), channel_id=1, source_target_pairs={{5,4},{6,7},{13,12},{14,15},{21,20},{22,23},{29,28},{30,31}} | collective-permute-start | bytes 49160 | tf_op jit(solution)/shard_map/ppermute | solution.py:196
  47.8 5.9 %collective-permute-start.9 = (f32[8,512]{1,0:T(8,128)S(1)}, f32[8,512]{1,0:T(8,128)S(1)}, u32[]{:S(2)}, u32[]{:S(2)}) collective-permute-start(f32[8,512]{1,0:T(8,128)S(1)} %get-tuple-element.52), channel_id=1, source_target_pairs={{3,1},{0,2},{1,5},{2,6},{5,3},{6,8},{4,7},{7,4},{11,9},{8,10},{9,1... | collective-permute-start | bytes 49160 | tf_op jit(solution)/shard_map/ppermute | solution.py:196

commit v9 on v7

--- a/solution.py
+++ b/solution.py
@@ -11,7 +11,7 @@
 AXES = ("blk", "grp")
 TILE = 128
 STEP = 256
-PARTS = 1
+PARTS = 2
 OFFSETS = 5
 VMEM_LIMIT = 16 << 20
 F32, BF16 = jnp.float32, jnp.bfloat16
@@ -73,15 +73,14 @@
     best(scale, partner_ref, unit_ref, max_ref)
 
 
-def far_kernel(scale, role_ref, rows_ref, unit_ref, partner_ref, far_ref, own_far_ref, far_max_ref):
+def far_kernel(scale, role_ref, rows_ref, unit_ref, partner_ref, far_ref, own_far_ref, far_max_ref, beside_ref):
     middle = place(role_ref)[2]
-    tiles = own_far_ref.shape[0]
     far_ref[...] = unit_of(rows_ref[...])
     best(scale, far_ref, unit_ref, own_far_ref, left_ref=far_max_ref)
 
     @pl.when(jnp.logical_not(middle))
     def _():
-        best(scale, partner_ref, far_ref, far_max_ref, right_at=tiles)
+        best(scale, far_ref, partner_ref, beside_ref)
 
 
 def even_kernel(first, scale, role_ref, part_ref, far_ref, *refs):
@@ -119,7 +118,8 @@
 
 
 def join_kernel(
-    role_ref, own_ref, own_partner_ref, own_far_ref, far_ref, tiles_ref, rows_ref, cross_ref, ends_ref, out_ref
+    role_ref, own_ref, own_partner_ref, own_far_ref, far_ref, beside_ref, tiles_ref, rows_ref, cross_ref,
+    ends_ref, out_ref
 ):
     turn, step, middle = place(role_ref)
     tiles, _ = own_ref.shape
@@ -135,11 +135,11 @@
     put((2, 2, 2, 2), 0, own_ref[...])
     put((4, 4, 0, 0), 0, own_partner_ref[...])
     put((3, 0, 4, 1), 0, own_far_ref[...])
-    put((0, 1, 3, 4), 0, far_ref[:tiles, :])
+    put((0, 1, 3, 4), 0, far_ref[...])
 
     @pl.when(middle)
     def _():
-        put((0, 3, 1, 0), 0, far_ref[tiles:, :])
+        put((0, 3, 1, 0), 0, beside_ref[...])
 
     @pl.when(jnp.logical_and(jnp.logical_not(middle), step == 0))
     def _():
@@ -187,7 +187,7 @@
             odd += [(at(q, 3), at(q + 1, 0)), (at(q, 0), at(q - 1, 3))]
             rows += [(at(q, 1), at(q, 0)), (at(q, 2), at(q, 3))]
             ends += [(at(q, 1), at(q - 1, 3)), (at(q, 2), at(q + 1, 0))]
-            ends += [(at(q, 0), at(q, 3)), (at(q, 3), at(q, 0))]
+            ends += [(at(q, 0), at(q, 0)), (at(q, 3), at(q, 3))]
             cross += [(at(q, 3), at(q, 1)), (at(q, 0), at(q, 2))]
             cross += [(at(q, 1), at(beside, 1)), (at(q, 2), at(beside, 2))]
         else:
@@ -213,15 +213,16 @@
     partner, *even_parts = call(partner_kernel, [((count, width), BF16)] + [piece] * PARTS, partner_rows)
     even_parts = [send(part, even) for part in even_parts]
     (own_partner,) = call(functools.partial(pair_kernel, scale), [((tiles, count), F32)], unit, partner)
-    far_unit, own_far, far_max = call(
+    far_unit, own_far, far_max, beside_max = call(
         functools.partial(far_kernel, scale),
-        [((count, width), BF16), ((tiles, count), F32), ((2 * tiles, count), F32)],
+        [((count, width), BF16)] + [((tiles, count), F32)] * 3,
         role,
         far_rows,
         unit,
         partner,
     )
     far_max = send(far_max, [(b, a) for a, b in far])
+    beside_max = send(beside_max, swap)
     column = ((tiles, half), F32)
     done = []
     for i, part in enumerate(even_parts):
@@ -244,6 +245,7 @@
         own_partner,
         own_far,
         far_max,
+        beside_max,
         half_tiles,
         rows_max,
         cross_max,

time: 51.3 us -> 53.7 us (1.047)
  the two profiles are of different devices: /device:TPU:0 before, /device:TPU:3 now
where the time goes in v9:
time: 53.7 us; the launch traced here: 53.5 us
  starting transfers between devices  26.2 us (49%)
  waiting for transfers between devices  13.9 us (26%)
  Pallas kernels  11.6 us (22%)
  local copies, waits for them, and re-layouts  1.62 us (3%)
    ppermute x11, starting transfers between devices, send(): return lax.ppermute(value, AXES, pairs)  26.2 us
    ppermute x11, waiting for transfers between devices, send(): return lax.ppermute(value, AXES, pairs)  13.9 us
    pallas_call x9, Pallas kernels, call(): pl.pallas_call(kernel, out_shape=[jax.ShapeDtypeStruct(*o) if last else p...  11.6 us
    unnamed x2, local copies, waits for them, and re-layouts  1.62 us
  transfers between devices with their start and end apart: 11, of which 2 were waited for; matrix products, arithmetic and copies ran while one was open for 0% of the time, Pallas kernels for 20%

profile of v9, /device:TPU:3, one launch (start us, length us, event | category | flops | bytes accessed | tf_op | source)
XLA Modules:
  0.0 53.5 jit_solution(4486329803773450625)
XLA Ops:
  0.0 0.7 %collective-permute-start = (bf16[1024,1024]{1,0:T(8,128)(2,1)}, bf16[1024,1024]{1,0:T(8,128)(2,1)S(1)}, u32[]{:S(2)}, u32[]{:S(2)}) collective-permute-start(bf16[1024,1024]{1,0:T(8,128)(2,1)} %rows_ref), channel_id=1, source_target_pairs={{0,2},{2,0},{1,3},{3,1},{4,6},{6,4},{5,7},{7,5},{8,10},{10,8},{9,1... | collective-permute-start | bytes 6291464 | tf_op jit(solution)/shard_map/ppermute | solution.py:200
  0.7 1.2 %collective-permute-start.1 = (bf16[1024,1024]{1,0:T(8,128)(2,1)}, bf16[1024,1024]{1,0:T(8,128)(2,1)S(1)}, u32[]{:S(2)}, u32[]{:S(2)}) collective-permute-start(bf16[1024,1024]{1,0:T(8,128)(2,1)} %rows_ref), channel_id=1, source_target_pairs={{1,0},{2,3},{3,5},{0,30},{5,4},{6,7},{7,9},{4,2},{9,8},{10,11},{11... | collective-permute-start | bytes 6291464 | tf_op jit(solution)/shard_map/ppermute | solution.py:200
  1.9 0.0 copy-start
  1.9 1.6 %copy-done = bf16[1024,1024]{1,0:T(8,128)(2,1)S(1)} copy-done((bf16[1024,1024]{1,0:T(8,128)(2,1)S(1)}, bf16[1024,1024]{1,0:T(8,128)(2,1)}, u32[]{:S(2)}) %copy-start) | copy-done | bytes 2097176
  3.5 2.9 %shard_map.17 = (bf16[1024,1024]{1,0:T(8,128)(2,1)S(1)}, f32[8,1024]{1,0:T(8,128)S(1)}, bf16[256,1024]{1,0:T(8,128)(2,1)S(1)}, bf16[256,1024]{1,0:T(8,128)(2,1)S(1)}) custom-call(bf16[1024,1024]{1,0:T(8,128)(2,1)S(1)} %copy-done), custom_call_target="tpu_custom_call" | custom-call | tf_op jit(solution)/shard_map/pallas_call | solution.py:160
  6.5 0.7 %collective-permute-start.5 = (bf16[256,1024]{1,0:T(8,128)(2,1)S(1)}, bf16[256,1024]{1,0:T(8,128)(2,1)S(1)}, u32[]{:S(2)}, u32[]{:S(2)}) collective-permute-start(bf16[256,1024]{1,0:T(8,128)(2,1)S(1)} %get-tuple-element.35), channel_id=1, source_target_pairs={{7,8},{4,3},{15,16},{12,11},{23,24},{20,19},{31,0},{28,27}} | collective-permute-start | bytes 1572872 | tf_op jit(solution)/shard_map/ppermute | solution.py:200
  7.2 0.7 %collective-permute-start.4 = (bf16[256,1024]{1,0:T(8,128)(2,1)S(1)}, bf16[256,1024]{1,0:T(8,128)(2,1)S(1)}, u32[]{:S(2)}, u32[]{:S(2)}) collective-permute-start(bf16[256,1024]{1,0:T(8,128)(2,1)S(1)} %get-tuple-element.34), channel_id=1, source_target_pairs={{7,8},{4,3},{15,16},{12,11},{23,24},{20,19},{31,0},{28,27}} | collective-permute-start | bytes 1572872 | tf_op jit(solution)/shard_map/ppermute | solution.py:200
  7.9 0.0 collective-permute-done.rows_ref
  7.9 0.7 %shard_map.18 = (bf16[1024,1024]{1,0:T(8,128)(2,1)S(1)}, bf16[256,1024]{1,0:T(8,128)(2,1)S(1)}, bf16[256,1024]{1,0:T(8,128)(2,1)S(1)}) custom-call(bf16[1024,1024]{1,0:T(8,128)(2,1)S(1)} %collective-permute-done.rows_ref), custom_call_target="tpu_custom_call" | custom-call | tf_op jit(solution)/shard_map/pallas_call | solution.py:160
  8.6 2.3 %collective-permute-start.7 = (bf16[256,1024]{1,0:T(8,128)(2,1)S(1)}, bf16[256,1024]{1,0:T(8,128)(2,1)S(1)}, u32[]{:S(2)}, u32[]{:S(2)}) collective-permute-start(bf16[256,1024]{1,0:T(8,128)(2,1)S(1)} %get-tuple-element.41), channel_id=1, source_target_pairs={{5,6},{6,5},{13,14},{14,13},{21,22},{22,21},{29,30},{30,29}} | collective-permute-start | bytes 1572872 | tf_op jit(solution)/shard_map/ppermute | solution.py:200
  10.9 3.3 %collective-permute-start.6 = (bf16[256,1024]{1,0:T(8,128)(2,1)S(1)}, bf16[256,1024]{1,0:T(8,128)(2,1)S(1)}, u32[]{:S(2)}, u32[]{:S(2)}) collective-permute-start(bf16[256,1024]{1,0:T(8,128)(2,1)S(1)} %get-tuple-element.39), channel_id=1, source_target_pairs={{5,6},{6,5},{13,14},{14,13},{21,22},{22,21},{29,30},{30,29}} | collective-permute-start | bytes 1572872 | tf_op jit(solution)/shard_map/ppermute | solution.py:200
  14.2 13.1 %collective-permute-done.1.rows_ref = bf16[1024,1024]{1,0:T(8,128)(2,1)S(1)} collective-permute-done((bf16[1024,1024]{1,0:T(8,128)(2,1)}, bf16[1024,1024]{1,0:T(8,128)(2,1)S(1)}, u32[]{:S(2)}, u32[]{:S(2)}) %collective-permute-start.1) | collective-permute-done | bytes 2097184 | tf_op jit(solution)/shard_map/ppermute | solution.py:200
  27.2 3.1 %shard_map.20 = (bf16[1024,1024]{1,0:T(8,128)(2,1)S(1)}, f32[8,1024]{1,0:T(8,128)S(1)}, f32[8,1024]{1,0:T(8,128)S(1)}, f32[8,1024]{1,0:T(8,128)S(1)}) custom-call(s32[1]{0:T(128)} %bitcast.role_ref, bf16[1024,1024]{1,0:T(8,128)(2,1)S(1)} %collective-permute-done.1.rows_ref, bf16[1024,1024]{1,0:T(8,128)(2,1)S(1)} %get-tuple-element.29.unit_ref, ...), custom_call_target="tpu_custom_call" | custom-call | tf_op jit(solution)/shard_map/pallas_call | solution.py:160
  30.3 3.3 %collective-permute-start.2 = (f32[8,1024]{1,0:T(8,128)S(1)}, f32[8,1024]{1,0:T(8,128)S(1)}, u32[]{:S(2)}, u32[]{:S(2)}) collective-permute-start(f32[8,1024]{1,0:T(8,128)S(1)} %get-tuple-element.32), channel_id=1, source_target_pairs={{0,1},{3,2},{5,3},{30,0},{4,5},{7,6},{9,7},{2,4},{8,9},{11,10},{13... | collective-permute-start | bytes 98312 | tf_op jit(solution)/shard_map/ppermute | solution.py:200
  33.6 0.0 collective-permute-done.5.part_ref
  33.6 0.0 collective-permute-start.3
  33.6 0.0 collective-permute-done.4.part_ref
  33.6 2.5 %collective-permute-start.9 = (f32[8,512]{1,0:T(8,128)S(1)}, f32[8,512]{1,0:T(8,128)S(1)}, u32[]{:S(2)}, u32[]{:S(2)}) collective-permute-start(f32[8,512]{1,0:T(8,128)S(1)} %get-tuple-element.45), channel_id=1, source_target_pairs={{0,31},{3,4},{1,3},{2,0},{7,5},{4,6},{5,1},{6,2},{8,7},{11,12},{9,... | collective-permute-start | bytes 49160 | tf_op jit(solution)/shard_map/ppermute | solution.py:200
  36.1 0.0 collective-permute-done.7.part_ref
  36.1 0.9 %shard_map.23 = (f32[8,512]{1,0:T(8,128)S(1)}, f32[8,512]{1,0:T(8,128)S(1)}) custom-call(s32[1]{0:T(128)} %bitcast.role_ref, bf16[256,1024]{1,0:T(8,128)(2,1)S(1)} %collective-permute-done.7.part_ref, bf16[1024,1024]{1,0:T(8,128)(2,1)S(1)} %get-tuple-element.40.far_ref), custom_call_target="tpu_custom_call" | custom-call | tf_op jit(solution)/shard_map/pallas_call | solution.py:160
  37.0 0.8 %collective-permute-done.6.part_ref = bf16[256,1024]{1,0:T(8,128)(2,1)S(1)} collective-permute-done((bf16[256,1024]{1,0:T(8,128)(2,1)S(1)}, bf16[256,1024]{1,0:T(8,128)(2,1)S(1)}, u32[]{:S(2)}, u32[]{:S(2)}) %collective-permute-start.6) | collective-permute-done | bytes 524320 | tf_op jit(solution)/shard_map/ppermute | solution.py:200
  37.8 0.9 %shard_map.24 = (f32[8,512]{1,0:T(8,128)S(1)}, f32[8,512]{1,0:T(8,128)S(1)}) custom-call(s32[1]{0:T(128)} %bitcast.role_ref, bf16[256,1024]{1,0:T(8,128)(2,1)S(1)} %collective-permute-done.6.part_ref, bf16[1024,1024]{1,0:T(8,128)(2,1)S(1)} %get-tuple-element.40.far_ref, f32[8,512]{1,0:T(8,128)S(1)} %get-tuple-element.42.refs_0_, ...), custom_call_target="tpu_custom_call" | custom-call | tf_op jit(solution)/shard_map/pallas_call | solution.py:160
  38.7 10.3 %collective-permute-start.10 = (f32[8,512]{1,0:T(8,128)S(1)}, f32[8,512]{1,0:T(8,128)S(1)}, u32[]{:S(2)}, u32[]{:S(2)}) collective-permute-start(f32[8,512]{1,0:T(8,128)S(1)} %get-tuple-element.46), channel_id=1, source_target_pairs={{3,1},{0,2},{1,5},{2,6},{5,3},{6,8},{4,4},{7,7},{11,9},{8,10},{9,1... | collective-permute-start | bytes 49160 | tf_op jit(solution)/shard_map/ppermute | solution.py:200
  49.0 1.3 %collective-permute-start.8 = (f32[8,512]{1,0:T(8,128)S(1)}, f32[8,512]{1,0:T(8,128)S(1)}, u32[]{:S(2)}, u32[]{:S(2)}) collective-permute-start(f32[8,512]{1,0:T(8,128)S(1)} %get-tuple-element.44), channel_id=1, source_target_pairs={{5,4},{6,7},{13,12},{14,15},{21,20},{22,23},{29,28},{30,31}} | collective-permute-start | bytes 49160 | tf_op jit(solution)/shard_map/ppermute | solution.py:200
  50.3 2.4 %shard_map.19.own_partner_ref = f32[8,1024]{1,0:T(8,128)S(1)} custom-call(bf16[1024,1024]{1,0:T(8,128)(2,1)S(1)} %get-tuple-element.29.unit_ref, bf16[1024,1024]{1,0:T(8,128)(2,1)S(1)} %get-tuple-element.30.partner_ref), custom_call_target="tpu_custom_call" | custom-call | tf_op jit(solution)/shard_map/pallas_call | solution.py:160
  52.7 0.0 collective-permute-done.9.cross_ref
  52.7 0.0 collective-permute-done.2.far_ref
  52.7 0.0 collective-permute-done.3.beside_ref
  52.7 0.0 collective-permute-done.10.ends_ref
  52.7 0.0 collective-permute-done.8.rows_ref
  52.8 0.7 %shard_map.25 = f32[40,1024]{1,0:T(8,128)} custom-call(s32[1]{0:T(128)} %bitcast.role_ref, f32[8,1024]{1,0:T(8,128)S(1)} %get-tuple-element.28.own_ref, f32[8,1024]{1,0:T(8,128)S(1)} %shard_map.19.own_partner_ref, f32[8,1024]{1,0:T(8,128)S(1)} %get-tuple-element.31.own_far_ref, f32[8,1024]{1,0:T(8,128)S(1)} %collective-permute-done.2.far_ref, ...), custom_call_target="tpu_custom_call" | custom-call | tf_op jit(solution)/shard_map/pallas_call | solution.py:160
  (2 shorter events, 0.0 us)
Async XLA Ops:
  0.0 7.9 %collective-permute-start = (bf16[1024,1024]{1,0:T(8,128)(2,1)}, bf16[1024,1024]{1,0:T(8,128)(2,1)S(1)}, u32[]{:S(2)}, u32[]{:S(2)}) collective-permute-start(bf16[1024,1024]{1,0:T(8,128)(2,1)} %rows_ref), channel_id=1, source_target_pairs={{0,2},{2,0},{1,3},{3,1},{4,6},{6,4},{5,7},{7,5},{8,10},{10,8},{9,1... | collective-permute-start | bytes 6291464 | tf_op jit(solution)/shard_map/ppermute | solution.py:200
  0.7 26.6 %collective-permute-start.1 = (bf16[1024,1024]{1,0:T(8,128)(2,1)}, bf16[1024,1024]{1,0:T(8,128)(2,1)S(1)}, u32[]{:S(2)}, u32[]{:S(2)}) collective-permute-start(bf16[1024,1024]{1,0:T(8,128)(2,1)} %rows_ref), channel_id=1, source_target_pairs={{1,0},{2,3},{3,5},{0,30},{5,4},{6,7},{7,9},{4,2},{9,8},{10,11},{11... | collective-permute-start | bytes 6291464 | tf_op jit(solution)/shard_map/ppermute | solution.py:200
  1.9 1.6 %copy-start = (bf16[1024,1024]{1,0:T(8,128)(2,1)S(1)}, bf16[1024,1024]{1,0:T(8,128)(2,1)}, u32[]{:S(2)}) copy-start(bf16[1024,1024]{1,0:T(8,128)(2,1)} %rows_ref) | copy-start | bytes 6291460
  6.5 27.1 %collective-permute-start.5 = (bf16[256,1024]{1,0:T(8,128)(2,1)S(1)}, bf16[256,1024]{1,0:T(8,128)(2,1)S(1)}, u32[]{:S(2)}, u32[]{:S(2)}) collective-permute-start(bf16[256,1024]{1,0:T(8,128)(2,1)S(1)} %get-tuple-element.35), channel_id=1, source_target_pairs={{7,8},{4,3},{15,16},{12,11},{23,24},{20,19},{31,0},{28,27}} | collective-permute-start | bytes 1572872 | tf_op jit(solution)/shard_map/ppermute | solution.py:200
  7.2 26.4 %collective-permute-start.4 = (bf16[256,1024]{1,0:T(8,128)(2,1)S(1)}, bf16[256,1024]{1,0:T(8,128)(2,1)S(1)}, u32[]{:S(2)}, u32[]{:S(2)}) collective-permute-start(bf16[256,1024]{1,0:T(8,128)(2,1)S(1)} %get-tuple-element.34), channel_id=1, source_target_pairs={{7,8},{4,3},{15,16},{12,11},{23,24},{20,19},{31,0},{28,27}} | collective-permute-start | bytes 1572872 | tf_op jit(solution)/shard_map/ppermute | solution.py:200
  8.6 27.5 %collective-permute-start.7 = (bf16[256,1024]{1,0:T(8,128)(2,1)S(1)}, bf16[256,1024]{1,0:T(8,128)(2,1)S(1)}, u32[]{:S(2)}, u32[]{:S(2)}) collective-permute-start(bf16[256,1024]{1,0:T(8,128)(2,1)S(1)} %get-tuple-element.41), channel_id=1, source_target_pairs={{5,6},{6,5},{13,14},{14,13},{21,22},{22,21},{29,30},{30,29}} | collective-permute-start | bytes 1572872 | tf_op jit(solution)/shard_map/ppermute | solution.py:200
  10.9 26.9 %collective-permute-start.6 = (bf16[256,1024]{1,0:T(8,128)(2,1)S(1)}, bf16[256,1024]{1,0:T(8,128)(2,1)S(1)}, u32[]{:S(2)}, u32[]{:S(2)}) collective-permute-start(bf16[256,1024]{1,0:T(8,128)(2,1)S(1)} %get-tuple-element.39), channel_id=1, source_target_pairs={{5,6},{6,5},{13,14},{14,13},{21,22},{22,21},{29,30},{30,29}} | collective-permute-start | bytes 1572872 | tf_op jit(solution)/shard_map/ppermute | solution.py:200
  30.3 22.4 %collective-permute-start.2 = (f32[8,1024]{1,0:T(8,128)S(1)}, f32[8,1024]{1,0:T(8,128)S(1)}, u32[]{:S(2)}, u32[]{:S(2)}) collective-permute-start(f32[8,1024]{1,0:T(8,128)S(1)} %get-tuple-element.32), channel_id=1, source_target_pairs={{0,1},{3,2},{5,3},{30,0},{4,5},{7,6},{9,7},{2,4},{8,9},{11,10},{13... | collective-permute-start | bytes 98312 | tf_op jit(solution)/shard_map/ppermute | solution.py:200
  33.6 19.2 %collective-permute-start.3 = (f32[8,1024]{1,0:T(8,128)S(1)}, f32[8,1024]{1,0:T(8,128)S(1)}, u32[]{:S(2)}, u32[]{:S(2)}) collective-permute-start(f32[8,1024]{1,0:T(8,128)S(1)} %get-tuple-element.33), channel_id=1, source_target_pairs={{0,2},{2,0},{1,3},{3,1},{4,6},{6,4},{5,7},{7,5},{8,10},{10,8},{9,1... | collective-permute-start | bytes 98312 | tf_op jit(solution)/shard_map/ppermute | solution.py:200
  33.6 19.1 %collective-permute-start.9 = (f32[8,512]{1,0:T(8,128)S(1)}, f32[8,512]{1,0:T(8,128)S(1)}, u32[]{:S(2)}, u32[]{:S(2)}) collective-permute-start(f32[8,512]{1,0:T(8,128)S(1)} %get-tuple-element.45), channel_id=1, source_target_pairs={{0,31},{3,4},{1,3},{2,0},{7,5},{4,6},{5,1},{6,2},{8,7},{11,12},{9,... | collective-permute-start | bytes 49160 | tf_op jit(solution)/shard_map/ppermute | solution.py:200
  38.7 14.0 %collective-permute-start.10 = (f32[8,512]{1,0:T(8,128)S(1)}, f32[8,512]{1,0:T(8,128)S(1)}, u32[]{:S(2)}, u32[]{:S(2)}) collective-permute-start(f32[8,512]{1,0:T(8,128)S(1)} %get-tuple-element.46), channel_id=1, source_target_pairs={{3,1},{0,2},{1,5},{2,6},{5,3},{6,8},{4,4},{7,7},{11,9},{8,10},{9,1... | collective-permute-start | bytes 49160 | tf_op jit(solution)/shard_map/ppermute | solution.py:200
  49.0 3.7 %collective-permute-start.8 = (f32[8,512]{1,0:T(8,128)S(1)}, f32[8,512]{1,0:T(8,128)S(1)}, u32[]{:S(2)}, u32[]{:S(2)}) collective-permute-start(f32[8,512]{1,0:T(8,128)S(1)} %get-tuple-element.44), channel_id=1, source_target_pairs={{5,4},{6,7},{13,12},{14,15},{21,20},{22,23},{29,28},{30,31}} | collective-permute-start | bytes 49160 | tf_op jit(solution)/shard_map/ppermute | solution.py:200

commit v10 on v9

--- a/solution.py
+++ b/solution.py
@@ -117,38 +117,47 @@
         best(scale, part_ref, unit_ref, tiles_ref, right_at=at, left_ref=cross_ref, left_from=first)
 
 
-def join_kernel(
-    role_ref, own_ref, own_partner_ref, own_far_ref, far_ref, beside_ref, tiles_ref, rows_ref, cross_ref,
-    ends_ref, out_ref
-):
+def slot_of(turn, slots):
+    slot = slots[0]
+    for i in range(1, 4):
+        slot = jnp.where(turn == i, slots[i], slot)
+    return slot
+
+
+def join_kernel(role_ref, own_ref, own_partner_ref, own_far_ref, far_ref, beside_ref, out_ref):
+    turn, _, _ = place(role_ref)
+    tiles = own_ref.shape[0]
+
+    def put(slots, value):
+        out_ref[pl.ds(pl.multiple_of(slot_of(turn, slots) * tiles, tiles), tiles), :] = value
+
+    put((2, 2, 2, 2), own_ref[...])
+    put((4, 4, 0, 0), own_partner_ref[...])
+    put((3, 0, 4, 1), own_far_ref[...])
+    put((0, 1, 3, 4), far_ref[...])
+    put((1, 3, 1, 3), beside_ref[...])
+
+
+def late_kernel(role_ref, tiles_ref, rows_ref, cross_ref, ends_ref, joined_ref, out_ref, late_ref, sem):
     turn, step, middle = place(role_ref)
-    tiles, _ = own_ref.shape
+    tiles = late_ref.shape[0]
     across = tiles // 2
 
-    def put(slots, *values):
-        slot = slots[0]
-        for i in range(1, 4):
-            slot = jnp.where(turn == i, slots[i], slot)
-        at = pl.multiple_of(slot * tiles, tiles)
-        out_ref[pl.ds(at, tiles), :] = jnp.concatenate(values[1:], axis=values[0])
-
-    put((2, 2, 2, 2), 0, own_ref[...])
-    put((4, 4, 0, 0), 0, own_partner_ref[...])
-    put((3, 0, 4, 1), 0, own_far_ref[...])
-    put((0, 1, 3, 4), 0, far_ref[...])
-
-    @pl.when(middle)
-    def _():
-        put((0, 3, 1, 0), 0, beside_ref[...])
-
-    @pl.when(jnp.logical_and(jnp.logical_not(middle), step == 0))
-    def _():
-        put((1, 1, 1, 3), 1, rows_ref[...], cross_ref[...])
-
-    @pl.when(jnp.logical_and(jnp.logical_not(middle), step == 1))
-    def _():
-        low = jnp.concatenate([ends_ref[:across, :], ends_ref[across:, :]], axis=1)
-        put((1, 1, 1, 3), 0, low, tiles_ref[...])
+    @pl.when(jnp.logical_not(middle))
+    def _():
+        @pl.when(step == 0)
+        def _():
+            late_ref[...] = jnp.concatenate([rows_ref[...], cross_ref[...]], axis=1)
+
+        @pl.when(step == 1)
+        def _():
+            low = jnp.concatenate([ends_ref[:across, :], ends_ref[across:, :]], axis=1)
+            late_ref[...] = jnp.concatenate([low, tiles_ref[...]], axis=0)
+
+        at = pl.multiple_of(slot_of(turn, (1, 1, 1, 3)) * tiles, tiles)
+        copy = pltpu.make_async_copy(late_ref, out_ref.at[pl.ds(at, tiles), :], sem)
+        copy.start()
+        copy.wait()
 
 
 def call(kernel, outs, *operands, last=False):
@@ -187,7 +196,7 @@
             odd += [(at(q, 3), at(q + 1, 0)), (at(q, 0), at(q - 1, 3))]
             rows += [(at(q, 1), at(q, 0)), (at(q, 2), at(q, 3))]
             ends += [(at(q, 1), at(q - 1, 3)), (at(q, 2), at(q + 1, 0))]
-            ends += [(at(q, 0), at(q, 0)), (at(q, 3), at(q, 3))]
+            ends += [(at(q, 0), at(q ^ 2, 0)), (at(q, 3), at(q ^ 2, 3))]
             cross += [(at(q, 3), at(q, 1)), (at(q, 0), at(q, 2))]
             cross += [(at(q, 1), at(beside, 1)), (at(q, 2), at(beside, 2))]
         else:
@@ -237,21 +246,21 @@
         )
     cross_max, half_tiles = done
     cross_max = send(cross_max, cross)
-    (out,) = call(
-        join_kernel,
-        [((OFFSETS * tiles, count), F32)],
-        role,
-        own,
-        own_partner,
-        own_far,
-        far_max,
-        beside_max,
-        half_tiles,
-        rows_max,
-        cross_max,
-        ends_max,
-        last=True,
-    )
+    (joined,) = call(
+        join_kernel, [((OFFSETS * tiles, count), F32)], role, own, own_partner, own_far, far_max, beside_max, last=True
+    )
+    near = [pltpu.with_memory_space_constraint(v, pltpu.VMEM) for v in (half_tiles, rows_max, cross_max, ends_max)]
+    out = pl.pallas_call(
+        late_kernel,
+        out_shape=jax.ShapeDtypeStruct(joined.shape, F32),
+        in_specs=[pl.BlockSpec(memory_space=pltpu.SMEM)]
+        + [pl.BlockSpec(memory_space=pltpu.VMEM)] * 4
+        + [pl.BlockSpec(memory_space=pltpu.HBM)],
+        out_specs=pl.BlockSpec(memory_space=pltpu.HBM),
+        scratch_shapes=[pltpu.VMEM((tiles, count), F32), pltpu.SemaphoreType.DMA],
+        input_output_aliases={5: 0},
+        compiler_params=pltpu.CompilerParams(vmem_limit_bytes=VMEM_LIMIT),
+    )(role, *near, joined)
     return jnp.transpose(out)
 
 

time: 53.7 us -> 52.5 us (0.978)
  the two profiles are of different devices: /device:TPU:3 before, /device:TPU:1 now
where the time goes in v10:
time: 52.5 us; the launch traced here: 52.3 us
  starting transfers between devices  24.6 us (47%)
  waiting for transfers between devices  16.1 us (31%)
  Pallas kernels  9.7 us (18%)
  local copies, waits for them, and re-layouts  1.62 us (3%)
    ppermute x11, starting transfers between devices, send(): return lax.ppermute(value, AXES, pairs)  24.6 us
    ppermute x11, waiting for transfers between devices, send(): return lax.ppermute(value, AXES, pairs)  16.1 us
    pallas_call x9, Pallas kernels, call(): pl.pallas_call(kernel, out_shape=[jax.ShapeDtypeStruct(*o) if last else p...  9.68 us
    unnamed x2, local copies, waits for them, and re-layouts  1.62 us
  transfers between devices with their start and end apart: 11, of which 1 were waited for; matrix products, arithmetic and copies ran while one was open for 0% of the time, Pallas kernels for 19%

profile of v10, /device:TPU:1, one launch (start us, length us, event | category | flops | bytes accessed | tf_op | source)
XLA Modules:
  0.0 52.3 jit_solution(14970858602599551038)
XLA Ops:
  0.0 0.0 collective-permute-start.2
  0.0 2.7 %collective-permute-start.4 = (bf16[1024,1024]{1,0:T(8,128)(2,1)}, bf16[1024,1024]{1,0:T(8,128)(2,1)S(1)}, u32[]{:S(2)}, u32[]{:S(2)}) collective-permute-start(bf16[1024,1024]{1,0:T(8,128)(2,1)} %rows_ref), channel_id=1, source_target_pairs={{1,0},{2,3},{3,5},{0,30},{5,4},{6,7},{7,9},{4,2},{9,8},{10,11},{11... | collective-permute-start | bytes 6291464 | tf_op jit(solution)/shard_map/ppermute | solution.py:209
  2.7 0.0 copy-start
  2.7 1.6 %copy-done = bf16[1024,1024]{1,0:T(8,128)(2,1)S(1)} copy-done((bf16[1024,1024]{1,0:T(8,128)(2,1)S(1)}, bf16[1024,1024]{1,0:T(8,128)(2,1)}, u32[]{:S(2)}) %copy-start) | copy-done | bytes 2097176
  4.4 2.9 %shard_map.17 = (bf16[1024,1024]{1,0:T(8,128)(2,1)S(1)}, f32[8,1024]{1,0:T(8,128)S(1)}, bf16[256,1024]{1,0:T(8,128)(2,1)S(1)}, bf16[256,1024]{1,0:T(8,128)(2,1)S(1)}) custom-call(bf16[1024,1024]{1,0:T(8,128)(2,1)S(1)} %copy-done), custom_call_target="tpu_custom_call" | custom-call | tf_op jit(solution)/shard_map/pallas_call | solution.py:169
  7.3 0.7 %collective-permute-start.1 = (bf16[256,1024]{1,0:T(8,128)(2,1)S(1)}, bf16[256,1024]{1,0:T(8,128)(2,1)S(1)}, u32[]{:S(2)}, u32[]{:S(2)}) collective-permute-start(bf16[256,1024]{1,0:T(8,128)(2,1)S(1)} %get-tuple-element.30), channel_id=1, source_target_pairs={{7,8},{4,3},{15,16},{12,11},{23,24},{20,19},{31,0},{28,27}} | collective-permute-start | bytes 1572872 | tf_op jit(solution)/shard_map/ppermute | solution.py:209
  8.0 0.7 %collective-permute-start = (bf16[256,1024]{1,0:T(8,128)(2,1)S(1)}, bf16[256,1024]{1,0:T(8,128)(2,1)S(1)}, u32[]{:S(2)}, u32[]{:S(2)}) collective-permute-start(bf16[256,1024]{1,0:T(8,128)(2,1)S(1)} %get-tuple-element.28), channel_id=1, source_target_pairs={{7,8},{4,3},{15,16},{12,11},{23,24},{20,19},{31,0},{28,27}} | collective-permute-start | bytes 1572872 | tf_op jit(solution)/shard_map/ppermute | solution.py:209
  8.7 0.0 collective-permute-done.2.rows_ref
  8.7 0.7 %shard_map.20 = (bf16[1024,1024]{1,0:T(8,128)(2,1)S(1)}, bf16[256,1024]{1,0:T(8,128)(2,1)S(1)}, bf16[256,1024]{1,0:T(8,128)(2,1)S(1)}) custom-call(bf16[1024,1024]{1,0:T(8,128)(2,1)S(1)} %collective-permute-done.2.rows_ref), custom_call_target="tpu_custom_call" | custom-call | tf_op jit(solution)/shard_map/pallas_call | solution.py:169
  9.4 0.7 %collective-permute-start.5 = (bf16[256,1024]{1,0:T(8,128)(2,1)S(1)}, bf16[256,1024]{1,0:T(8,128)(2,1)S(1)}, u32[]{:S(2)}, u32[]{:S(2)}) collective-permute-start(bf16[256,1024]{1,0:T(8,128)(2,1)S(1)} %get-tuple-element.37), channel_id=1, source_target_pairs={{5,6},{6,5},{13,14},{14,13},{21,22},{22,21},{29,30},{30,29}} | collective-permute-start | bytes 1572872 | tf_op jit(solution)/shard_map/ppermute | solution.py:209
  10.1 0.7 %collective-permute-start.3 = (bf16[256,1024]{1,0:T(8,128)(2,1)S(1)}, bf16[256,1024]{1,0:T(8,128)(2,1)S(1)}, u32[]{:S(2)}, u32[]{:S(2)}) collective-permute-start(bf16[256,1024]{1,0:T(8,128)(2,1)S(1)} %get-tuple-element.34), channel_id=1, source_target_pairs={{5,6},{6,5},{13,14},{14,13},{21,22},{22,21},{29,30},{30,29}} | collective-permute-start | bytes 1572872 | tf_op jit(solution)/shard_map/ppermute | solution.py:209
  10.8 16.0 %collective-permute-done.4.rows_ref = bf16[1024,1024]{1,0:T(8,128)(2,1)S(1)} collective-permute-done((bf16[1024,1024]{1,0:T(8,128)(2,1)}, bf16[1024,1024]{1,0:T(8,128)(2,1)S(1)}, u32[]{:S(2)}, u32[]{:S(2)}) %collective-permute-start.4) | collective-permute-done | bytes 2097184 | tf_op jit(solution)/shard_map/ppermute | solution.py:209
  26.8 3.0 %shard_map.21 = (bf16[1024,1024]{1,0:T(8,128)(2,1)S(1)}, f32[8,1024]{1,0:T(8,128)S(1)}, f32[8,1024]{1,0:T(8,128)S(1)}, f32[8,1024]{1,0:T(8,128)S(1)}) custom-call(s32[1]{0:T(128)} %bitcast.role_ref, bf16[1024,1024]{1,0:T(8,128)(2,1)S(1)} %collective-permute-done.4.rows_ref, bf16[1024,1024]{1,0:T(8,128)(2,1)S(1)} %get-tuple-element.29.unit_ref, ...), custom_call_target="tpu_custom_call" | custom-call | tf_op jit(solution)/shard_map/pallas_call | solution.py:169
  29.9 4.5 %collective-permute-start.9 = (f32[8,1024]{1,0:T(8,128)S(1)}, f32[8,1024]{1,0:T(8,128)S(1)}, u32[]{:S(2)}, u32[]{:S(2)}) collective-permute-start(f32[8,1024]{1,0:T(8,128)S(1)} %get-tuple-element.45), channel_id=1, source_target_pairs={{0,1},{3,2},{5,3},{30,0},{4,5},{7,6},{9,7},{2,4},{8,9},{11,10},{13... | collective-permute-start | bytes 98312 | tf_op jit(solution)/shard_map/ppermute | solution.py:209
  34.3 0.0 collective-permute-done.1.part_ref
  34.3 2.3 %collective-permute-start.10 = (f32[8,1024]{1,0:T(8,128)S(1)}, f32[8,1024]{1,0:T(8,128)S(1)}, u32[]{:S(2)}, u32[]{:S(2)}) collective-permute-start(f32[8,1024]{1,0:T(8,128)S(1)} %get-tuple-element.46), channel_id=1, source_target_pairs={{0,2},{2,0},{1,3},{3,1},{4,6},{6,4},{5,7},{7,5},{8,10},{10,8},{9,1... | collective-permute-start | bytes 98312 | tf_op jit(solution)/shard_map/ppermute | solution.py:209
  36.6 0.0 collective-permute-done.part_ref
  36.6 6.6 %collective-permute-start.7 = (f32[8,512]{1,0:T(8,128)S(1)}, f32[8,512]{1,0:T(8,128)S(1)}, u32[]{:S(2)}, u32[]{:S(2)}) collective-permute-start(f32[8,512]{1,0:T(8,128)S(1)} %get-tuple-element.41), channel_id=1, source_target_pairs={{0,31},{3,4},{1,3},{2,0},{7,5},{4,6},{5,1},{6,2},{8,7},{11,12},{9,... | collective-permute-start | bytes 49160 | tf_op jit(solution)/shard_map/ppermute | solution.py:209
  43.2 0.0 collective-permute-done.5.part_ref
  43.2 0.0 collective-permute-done.3.part_ref
  43.2 0.7 %collective-permute-start.6 = (f32[8,512]{1,0:T(8,128)S(1)}, f32[8,512]{1,0:T(8,128)S(1)}, u32[]{:S(2)}, u32[]{:S(2)}) collective-permute-start(f32[8,512]{1,0:T(8,128)S(1)} %get-tuple-element.40), channel_id=1, source_target_pairs={{5,4},{6,7},{13,12},{14,15},{21,20},{22,23},{29,28},{30,31}} | collective-permute-start | bytes 49160 | tf_op jit(solution)/shard_map/ppermute | solution.py:209
  43.9 5.1 %collective-permute-start.8 = (f32[8,512]{1,0:T(8,128)S(1)}, f32[8,512]{1,0:T(8,128)S(1)}, u32[]{:S(2)}, u32[]{:S(2)}) collective-permute-start(f32[8,512]{1,0:T(8,128)S(1)} %get-tuple-element.42), channel_id=1, source_target_pairs={{3,1},{0,2},{1,5},{2,6},{5,3},{6,8},{4,12},{7,15},{11,9},{8,10},{9... | collective-permute-start | bytes 49160 | tf_op jit(solution)/shard_map/ppermute | solution.py:209
  49.0 2.4 %shard_map.24.own_partner_ref = f32[8,1024]{1,0:T(8,128)S(1)} custom-call(bf16[1024,1024]{1,0:T(8,128)(2,1)S(1)} %get-tuple-element.29.unit_ref, bf16[1024,1024]{1,0:T(8,128)(2,1)S(1)} %get-tuple-element.35.partner_ref), custom_call_target="tpu_custom_call" | custom-call | tf_op jit(solution)/shard_map/pallas_call | solution.py:169
  51.4 0.0 collective-permute-done.9.far_ref
  51.4 0.0 collective-permute-done.10.beside_ref
  51.4 0.7 %shard_map.25.joined_ref = f32[40,1024]{1,0:T(8,128)} custom-call(s32[1]{0:T(128)} %bitcast.role_ref, f32[8,1024]{1,0:T(8,128)S(1)} %get-tuple-element.43.own_ref, f32[8,1024]{1,0:T(8,128)S(1)} %shard_map.24.own_partner_ref, f32[8,1024]{1,0:T(8,128)S(1)} %get-tuple-element.44.own_far_ref, f32[8,1024]{1,0:T(8,128)S(1)} %collective-permute-done.9.far_ref, ...), custom_call_target="tpu_custom_call" | custom-call | tf_op jit(solution)/shard_map/pallas_call | solution.py:169
  52.1 0.0 collective-permute-done.7.cross_ref
  52.1 0.0 collective-permute-done.6.rows_ref
  52.1 0.0 collective-permute-done.8.ends_ref
  (5 shorter events, 0.0 us)
Async XLA Ops:
  0.0 8.7 %collective-permute-start.2 = (bf16[1024,1024]{1,0:T(8,128)(2,1)}, bf16[1024,1024]{1,0:T(8,128)(2,1)S(1)}, u32[]{:S(2)}, u32[]{:S(2)}) collective-permute-start(bf16[1024,1024]{1,0:T(8,128)(2,1)} %rows_ref), channel_id=1, source_target_pairs={{0,2},{2,0},{1,3},{3,1},{4,6},{6,4},{5,7},{7,5},{8,10},{10,8},{9,1... | collective-permute-start | bytes 6291464 | tf_op jit(solution)/shard_map/ppermute | solution.py:209
  0.0 26.8 %collective-permute-start.4 = (bf16[1024,1024]{1,0:T(8,128)(2,1)}, bf16[1024,1024]{1,0:T(8,128)(2,1)S(1)}, u32[]{:S(2)}, u32[]{:S(2)}) collective-permute-start(bf16[1024,1024]{1,0:T(8,128)(2,1)} %rows_ref), channel_id=1, source_target_pairs={{1,0},{2,3},{3,5},{0,30},{5,4},{6,7},{7,9},{4,2},{9,8},{10,11},{11... | collective-permute-start | bytes 6291464 | tf_op jit(solution)/shard_map/ppermute | solution.py:209
  2.7 1.6 %copy-start = (bf16[1024,1024]{1,0:T(8,128)(2,1)S(1)}, bf16[1024,1024]{1,0:T(8,128)(2,1)}, u32[]{:S(2)}) copy-start(bf16[1024,1024]{1,0:T(8,128)(2,1)} %rows_ref) | copy-start | bytes 6291460
  7.3 27.0 %collective-permute-start.1 = (bf16[256,1024]{1,0:T(8,128)(2,1)S(1)}, bf16[256,1024]{1,0:T(8,128)(2,1)S(1)}, u32[]{:S(2)}, u32[]{:S(2)}) collective-permute-start(bf16[256,1024]{1,0:T(8,128)(2,1)S(1)} %get-tuple-element.30), channel_id=1, source_target_pairs={{7,8},{4,3},{15,16},{12,11},{23,24},{20,19},{31,0},{28,27}} | collective-permute-start | bytes 1572872 | tf_op jit(solution)/shard_map/ppermute | solution.py:209
  8.0 28.7 %collective-permute-start = (bf16[256,1024]{1,0:T(8,128)(2,1)S(1)}, bf16[256,1024]{1,0:T(8,128)(2,1)S(1)}, u32[]{:S(2)}, u32[]{:S(2)}) collective-permute-start(bf16[256,1024]{1,0:T(8,128)(2,1)S(1)} %get-tuple-element.28), channel_id=1, source_target_pairs={{7,8},{4,3},{15,16},{12,11},{23,24},{20,19},{31,0},{28,27}} | collective-permute-start | bytes 1572872 | tf_op jit(solution)/shard_map/ppermute | solution.py:209
  9.4 33.9 %collective-permute-start.5 = (bf16[256,1024]{1,0:T(8,128)(2,1)S(1)}, bf16[256,1024]{1,0:T(8,128)(2,1)S(1)}, u32[]{:S(2)}, u32[]{:S(2)}) collective-permute-start(bf16[256,1024]{1,0:T(8,128)(2,1)S(1)} %get-tuple-element.37), channel_id=1, source_target_pairs={{5,6},{6,5},{13,14},{14,13},{21,22},{22,21},{29,30},{30,29}} | collective-permute-start | bytes 1572872 | tf_op jit(solution)/shard_map/ppermute | solution.py:209
  10.1 33.2 %collective-permute-start.3 = (bf16[256,1024]{1,0:T(8,128)(2,1)S(1)}, bf16[256,1024]{1,0:T(8,128)(2,1)S(1)}, u32[]{:S(2)}, u32[]{:S(2)}) collective-permute-start(bf16[256,1024]{1,0:T(8,128)(2,1)S(1)} %get-tuple-element.34), channel_id=1, source_target_pairs={{5,6},{6,5},{13,14},{14,13},{21,22},{22,21},{29,30},{30,29}} | collective-permute-start | bytes 1572872 | tf_op jit(solution)/shard_map/ppermute | solution.py:209
  29.9 21.5 %collective-permute-start.9 = (f32[8,1024]{1,0:T(8,128)S(1)}, f32[8,1024]{1,0:T(8,128)S(1)}, u32[]{:S(2)}, u32[]{:S(2)}) collective-permute-start(f32[8,1024]{1,0:T(8,128)S(1)} %get-tuple-element.45), channel_id=1, source_target_pairs={{0,1},{3,2},{5,3},{30,0},{4,5},{7,6},{9,7},{2,4},{8,9},{11,10},{13... | collective-permute-start | bytes 98312 | tf_op jit(solution)/shard_map/ppermute | solution.py:209
  34.3 17.1 %collective-permute-start.10 = (f32[8,1024]{1,0:T(8,128)S(1)}, f32[8,1024]{1,0:T(8,128)S(1)}, u32[]{:S(2)}, u32[]{:S(2)}) collective-permute-start(f32[8,1024]{1,0:T(8,128)S(1)} %get-tuple-element.46), channel_id=1, source_target_pairs={{0,2},{2,0},{1,3},{3,1},{4,6},{6,4},{5,7},{7,5},{8,10},{10,8},{9,1... | collective-permute-start | bytes 98312 | tf_op jit(solution)/shard_map/ppermute | solution.py:209
  36.6 15.5 %collective-permute-start.7 = (f32[8,512]{1,0:T(8,128)S(1)}, f32[8,512]{1,0:T(8,128)S(1)}, u32[]{:S(2)}, u32[]{:S(2)}) collective-permute-start(f32[8,512]{1,0:T(8,128)S(1)} %get-tuple-element.41), channel_id=1, source_target_pairs={{0,31},{3,4},{1,3},{2,0},{7,5},{4,6},{5,1},{6,2},{8,7},{11,12},{9,... | collective-permute-start | bytes 49160 | tf_op jit(solution)/shard_map/ppermute | solution.py:209
  43.2 8.9 %collective-permute-start.6 = (f32[8,512]{1,0:T(8,128)S(1)}, f32[8,512]{1,0:T(8,128)S(1)}, u32[]{:S(2)}, u32[]{:S(2)}) collective-permute-start(f32[8,512]{1,0:T(8,128)S(1)} %get-tuple-element.40), channel_id=1, source_target_pairs={{5,4},{6,7},{13,12},{14,15},{21,20},{22,23},{29,28},{30,31}} | collective-permute-start | bytes 49160 | tf_op jit(solution)/shard_map/ppermute | solution.py:209
  43.9 8.2 %collective-permute-start.8 = (f32[8,512]{1,0:T(8,128)S(1)}, f32[8,512]{1,0:T(8,128)S(1)}, u32[]{:S(2)}, u32[]{:S(2)}) collective-permute-start(f32[8,512]{1,0:T(8,128)S(1)} %get-tuple-element.42), channel_id=1, source_target_pairs={{3,1},{0,2},{1,5},{2,6},{5,3},{6,8},{4,12},{7,15},{11,9},{8,10},{9... | collective-permute-start | bytes 49160 | tf_op jit(solution)/shard_map/ppermute | solution.py:209

commit v11 on v9

--- a/solution.py
+++ b/solution.py
@@ -73,21 +73,29 @@
     best(scale, partner_ref, unit_ref, max_ref)
 
 
-def far_kernel(scale, role_ref, rows_ref, unit_ref, partner_ref, far_ref, own_far_ref, far_max_ref, beside_ref):
+def far_kernel(scale, role_ref, rows_ref, unit_ref, partner_ref, far_ref, own_far_ref, far_max_ref, first_ref):
     middle = place(role_ref)[2]
     far_ref[...] = unit_of(rows_ref[...])
     best(scale, far_ref, unit_ref, own_far_ref, left_ref=far_max_ref)
 
     @pl.when(jnp.logical_not(middle))
     def _():
-        best(scale, far_ref, partner_ref, beside_ref)
-
-
-def even_kernel(first, scale, role_ref, part_ref, far_ref, *refs):
+        best(scale, far_ref, partner_ref, first_ref)
+
+    @pl.when(middle)
+    def _():
+        first_ref[...] = far_max_ref[...]
+
+
+def even_kernel(first, scale, role_ref, part_ref, far_ref, far_max_ref, *refs):
     _, step, middle = place(role_ref)
     rows_ref, ends_ref = refs[-2:]
     half = far_ref.shape[0] // 2
     at, across = first // TILE, half // TILE
+
+    @pl.when(jnp.logical_not(middle))
+    def _():
+        rows_ref[...] = far_max_ref[...]
 
     @pl.when(jnp.logical_and(step == 0, middle))
     def _():
@@ -118,11 +126,11 @@
 
 
 def join_kernel(
-    role_ref, own_ref, own_partner_ref, own_far_ref, far_ref, beside_ref, tiles_ref, rows_ref, cross_ref,
+    role_ref, own_ref, own_partner_ref, own_far_ref, first_ref, tiles_ref, rows_ref, cross_ref,
     ends_ref, out_ref
 ):
     turn, step, middle = place(role_ref)
-    tiles, _ = own_ref.shape
+    tiles, count = own_ref.shape
     across = tiles // 2
 
     def put(slots, *values):
@@ -135,15 +143,15 @@
     put((2, 2, 2, 2), 0, own_ref[...])
     put((4, 4, 0, 0), 0, own_partner_ref[...])
     put((3, 0, 4, 1), 0, own_far_ref[...])
-    put((0, 1, 3, 4), 0, far_ref[...])
+    put((0, 3, 1, 4), 0, first_ref[...])
 
     @pl.when(middle)
     def _():
-        put((0, 3, 1, 0), 0, beside_ref[...])
+        put((0, 1, 3, 0), 0, rows_ref[...])
 
     @pl.when(jnp.logical_and(jnp.logical_not(middle), step == 0))
     def _():
-        put((1, 1, 1, 3), 1, rows_ref[...], cross_ref[...])
+        put((1, 1, 1, 3), 1, rows_ref[:, : count // 2], cross_ref[...])
 
     @pl.when(jnp.logical_and(jnp.logical_not(middle), step == 1))
     def _():
@@ -176,22 +184,25 @@
     assert blocks % 8 == 0 and size % STEP == 0
 
     at = lambda column, turn: column % columns * 4 + turn
-    far, swap, even, odd, rows, cross, ends = [], [], [], [], [], [], []
+    far, first, swap, even, odd, rows, cross, ends = [], [], [], [], [], [], [], []
     for q in range(columns):
         far += [(at(q, 1), at(q, 0)), (at(q, 2), at(q, 3))]
         far += [(at(q, 3), at(q + 1, 1)), (at(q, 0), at(q - 1, 2))]
         swap += [(at(q, 0), at(q, 2)), (at(q, 2), at(q, 0)), (at(q, 1), at(q, 3)), (at(q, 3), at(q, 1))]
         beside = q ^ 1
+        rows += [(at(q, 0), at(q, 1)), (at(q, 3), at(q, 2))]
+        first += [(at(q, 1), at(q - 1, 3)), (at(q, 2), at(q + 1, 0)), (at(q, 0), at(q, 2)), (at(q, 3), at(q, 1))]
         if q % 2 == 1:
             even += [(at(q, 1), at(q, 2)), (at(q, 2), at(q, 1))]
             odd += [(at(q, 3), at(q + 1, 0)), (at(q, 0), at(q - 1, 3))]
+            ends += [(at(q, 1), at(q - 1, 3)), (at(q, 2), at(q + 1, 0))]
             rows += [(at(q, 1), at(q, 0)), (at(q, 2), at(q, 3))]
-            ends += [(at(q, 1), at(q - 1, 3)), (at(q, 2), at(q + 1, 0))]
-            ends += [(at(q, 0), at(q, 0)), (at(q, 3), at(q, 3))]
+            ends += [(at(q, 0), at(q, 3)), (at(q, 3), at(q, 0))]
             cross += [(at(q, 3), at(q, 1)), (at(q, 0), at(q, 2))]
             cross += [(at(q, 1), at(beside, 1)), (at(q, 2), at(beside, 2))]
         else:
             cross += [(at(q, 0), at(q - 1, 3)), (at(q, 3), at(q + 1, 0))]
+            rows += [(at(q, 1), at(q, 3)), (at(q, 2), at(q, 0))]
             cross += [(at(q, 1), at(q, 3)), (at(q, 2), at(q, 0))]
             ends += [(at(q, 3), at(q, 1)), (at(q, 0), at(q, 2))]
             ends += [(at(q, 1), at(beside, 1)), (at(q, 2), at(beside, 2))]
@@ -213,7 +224,7 @@
     partner, *even_parts = call(partner_kernel, [((count, width), BF16)] + [piece] * PARTS, partner_rows)
     even_parts = [send(part, even) for part in even_parts]
     (own_partner,) = call(functools.partial(pair_kernel, scale), [((tiles, count), F32)], unit, partner)
-    far_unit, own_far, far_max, beside_max = call(
+    far_unit, own_far, far_max, first_max = call(
         functools.partial(far_kernel, scale),
         [((count, width), BF16)] + [((tiles, count), F32)] * 3,
         role,
@@ -221,15 +232,16 @@
         unit,
         partner,
     )
-    far_max = send(far_max, [(b, a) for a, b in far])
-    beside_max = send(beside_max, swap)
+    first_max = send(first_max, first)
     column = ((tiles, half), F32)
     done = []
     for i, part in enumerate(even_parts):
-        done = call(functools.partial(even_kernel, i * size, scale), [column, column], role, part, far_unit, *done)
+        done = call(
+            functools.partial(even_kernel, i * size, scale), [((tiles, count), F32), column],
+            role, part, far_unit, far_max, *done
+        )
     rows_max, ends_max = done
     ends_max = send(ends_max, ends)
-    rows_max = send(rows_max, rows)
     done = []
     for i, part in enumerate(odd_parts):
         done = call(
@@ -237,6 +249,7 @@
         )
     cross_max, half_tiles = done
     cross_max = send(cross_max, cross)
+    rows_max = send(rows_max, rows)
     (out,) = call(
         join_kernel,
         [((OFFSETS * tiles, count), F32)],
@@ -244,8 +257,7 @@
         own,
         own_partner,
         own_far,
-        far_max,
-        beside_max,
+        first_max,
         half_tiles,
         rows_max,
         cross_max,

time: 53.7 us -> 51.9 us (0.966)
  the two profiles are of different devices: /device:TPU:3 before, /device:TPU:0 now
where the time goes in v11:
time: 51.9 us; the launch traced here: 51.8 us
  waiting for transfers between devices  22.7 us (44%)
  starting transfers between devices  15 us (29%)
  Pallas kernels  13.9 us (27%)
    ppermute x10, waiting for transfers between devices, send(): return lax.ppermute(value, AXES, pairs)  22.7 us
    ppermute x10, starting transfers between devices, send(): return lax.ppermute(value, AXES, pairs)  15 us
    pallas_call x9, Pallas kernels, call(): pl.pallas_call(kernel, out_shape=[jax.ShapeDtypeStruct(*o) if last else p...  13.9 us
  transfers between devices with their start and end apart: 10, of which 3 were waited for; matrix products, arithmetic and copies ran while one was open for 0% of the time, Pallas kernels for 25%

profile of v11, /device:TPU:0, one launch (start us, length us, event | category | flops | bytes accessed | tf_op | source)
XLA Modules:
  0.0 51.8 jit_solution(6360622696141583558)
XLA Ops:
  0.0 0.0 copy-start
  0.0 0.5 collective-permute-start
  0.5 5.6 %collective-permute-start.1 = (bf16[1024,1024]{1,0:T(8,128)(2,1)}, bf16[1024,1024]{1,0:T(8,128)(2,1)S(1)}, u32[]{:S(2)}, u32[]{:S(2)}) collective-permute-start(bf16[1024,1024]{1,0:T(8,128)(2,1)} %rows_ref), channel_id=1, source_target_pairs={{1,0},{2,3},{3,5},{0,30},{5,4},{6,7},{7,9},{4,2},{9,8},{10,11},{11... | collective-permute-start | bytes 6291464 | tf_op jit(solution)/shard_map/ppermute | solution.py:211
  6.1 0.0 collective-permute-done.rows_ref
  6.1 0.7 %shard_map.18 = (bf16[1024,1024]{1,0:T(8,128)(2,1)S(1)}, bf16[256,1024]{1,0:T(8,128)(2,1)S(1)}, bf16[256,1024]{1,0:T(8,128)(2,1)S(1)}) custom-call(bf16[1024,1024]{1,0:T(8,128)(2,1)S(1)} %collective-permute-done.rows_ref), custom_call_target="tpu_custom_call" | custom-call | tf_op jit(solution)/shard_map/pallas_call | solution.py:168
  6.8 0.7 %collective-permute-start.6 = (bf16[256,1024]{1,0:T(8,128)(2,1)S(1)}, bf16[256,1024]{1,0:T(8,128)(2,1)S(1)}, u32[]{:S(2)}, u32[]{:S(2)}) collective-permute-start(bf16[256,1024]{1,0:T(8,128)(2,1)S(1)} %get-tuple-element.41), channel_id=1, source_target_pairs={{5,6},{6,5},{13,14},{14,13},{21,22},{22,21},{29,30},{30,29}} | collective-permute-start | bytes 1572872 | tf_op jit(solution)/shard_map/ppermute | solution.py:211
  7.5 0.7 %collective-permute-start.5 = (bf16[256,1024]{1,0:T(8,128)(2,1)S(1)}, bf16[256,1024]{1,0:T(8,128)(2,1)S(1)}, u32[]{:S(2)}, u32[]{:S(2)}) collective-permute-start(bf16[256,1024]{1,0:T(8,128)(2,1)S(1)} %get-tuple-element.38), channel_id=1, source_target_pairs={{5,6},{6,5},{13,14},{14,13},{21,22},{22,21},{29,30},{30,29}} | collective-permute-start | bytes 1572872 | tf_op jit(solution)/shard_map/ppermute | solution.py:211
  8.2 0.0 copy-done
  8.2 2.9 %shard_map.17 = (bf16[1024,1024]{1,0:T(8,128)(2,1)S(1)}, f32[8,1024]{1,0:T(8,128)S(1)}, bf16[256,1024]{1,0:T(8,128)(2,1)S(1)}, bf16[256,1024]{1,0:T(8,128)(2,1)S(1)}) custom-call(bf16[1024,1024]{1,0:T(8,128)(2,1)S(1)} %copy-done), custom_call_target="tpu_custom_call" | custom-call | tf_op jit(solution)/shard_map/pallas_call | solution.py:168
  11.1 1.3 %collective-permute-start.4 = (bf16[256,1024]{1,0:T(8,128)(2,1)S(1)}, bf16[256,1024]{1,0:T(8,128)(2,1)S(1)}, u32[]{:S(2)}, u32[]{:S(2)}) collective-permute-start(bf16[256,1024]{1,0:T(8,128)(2,1)S(1)} %get-tuple-element.34), channel_id=1, source_target_pairs={{7,8},{4,3},{15,16},{12,11},{23,24},{20,19},{31,0},{28,27}} | collective-permute-start | bytes 1572872 | tf_op jit(solution)/shard_map/ppermute | solution.py:211
  12.4 1.3 %collective-permute-start.3 = (bf16[256,1024]{1,0:T(8,128)(2,1)S(1)}, bf16[256,1024]{1,0:T(8,128)(2,1)S(1)}, u32[]{:S(2)}, u32[]{:S(2)}) collective-permute-start(bf16[256,1024]{1,0:T(8,128)(2,1)S(1)} %get-tuple-element.33), channel_id=1, source_target_pairs={{7,8},{4,3},{15,16},{12,11},{23,24},{20,19},{31,0},{28,27}} | collective-permute-start | bytes 1572872 | tf_op jit(solution)/shard_map/ppermute | solution.py:211
  13.7 16.3 %collective-permute-done.1.rows_ref = bf16[1024,1024]{1,0:T(8,128)(2,1)S(1)} collective-permute-done((bf16[1024,1024]{1,0:T(8,128)(2,1)}, bf16[1024,1024]{1,0:T(8,128)(2,1)S(1)}, u32[]{:S(2)}, u32[]{:S(2)}) %collective-permute-start.1) | collective-permute-done | bytes 2097184 | tf_op jit(solution)/shard_map/ppermute | solution.py:211
  30.0 5.4 %shard_map.20 = (bf16[1024,1024]{1,0:T(8,128)(2,1)S(1)}, f32[8,1024]{1,0:T(8,128)S(1)}, f32[8,1024]{1,0:T(8,128)S(1)}, f32[8,1024]{1,0:T(8,128)S(1)}) custom-call(s32[1]{0:T(128)} %bitcast.role_ref, bf16[1024,1024]{1,0:T(8,128)(2,1)S(1)} %collective-permute-done.1.rows_ref, bf16[1024,1024]{1,0:T(8,128)(2,1)S(1)} %get-tuple-element.29.unit_ref, ...), custom_call_target="tpu_custom_call" | custom-call | tf_op jit(solution)/shard_map/pallas_call | solution.py:168
  35.4 0.1 collective-permute-start.2
  35.5 0.0 collective-permute-done.6.part_ref
  35.5 0.0 collective-permute-done.5.part_ref
  35.6 3.0 %collective-permute-start.7 = (f32[8,1024]{1,0:T(8,128)S(1)}, f32[8,1024]{1,0:T(8,128)S(1)}, u32[]{:S(2)}, u32[]{:S(2)}) collective-permute-start(f32[8,1024]{1,0:T(8,128)S(1)} %get-tuple-element.44), channel_id=1, source_target_pairs={{0,1},{3,2},{1,3},{2,0},{4,5},{7,6},{5,4},{6,7},{8,9},{11,10},{9,1... | collective-permute-start | bytes 98312 | tf_op jit(solution)/shard_map/ppermute | solution.py:211
  38.5 0.0 collective-permute-done.4.part_ref
  38.5 0.9 %shard_map.21 = (f32[8,512]{1,0:T(8,128)S(1)}, f32[4,1024]{1,0:T(4,128)S(1)}) custom-call(s32[1]{0:T(128)} %bitcast.role_ref, bf16[256,1024]{1,0:T(8,128)(2,1)S(1)} %collective-permute-done.4.part_ref, bf16[1024,1024]{1,0:T(8,128)(2,1)S(1)} %get-tuple-element.29.unit_ref), custom_call_target="tpu_custom_call" | custom-call | tf_op jit(solution)/shard_map/pallas_call | solution.py:168
  39.4 3.0 %collective-permute-done.3.part_ref = bf16[256,1024]{1,0:T(8,128)(2,1)S(1)} collective-permute-done((bf16[256,1024]{1,0:T(8,128)(2,1)S(1)}, bf16[256,1024]{1,0:T(8,128)(2,1)S(1)}, u32[]{:S(2)}, u32[]{:S(2)}) %collective-permute-start.3) | collective-permute-done | bytes 524320 | tf_op jit(solution)/shard_map/ppermute | solution.py:211
  42.4 0.9 %shard_map.22 = (f32[8,512]{1,0:T(8,128)S(1)}, f32[4,1024]{1,0:T(4,128)S(1)}) custom-call(s32[1]{0:T(128)} %bitcast.role_ref, bf16[256,1024]{1,0:T(8,128)(2,1)S(1)} %collective-permute-done.3.part_ref, bf16[1024,1024]{1,0:T(8,128)(2,1)S(1)} %get-tuple-element.29.unit_ref, f32[8,512]{1,0:T(8,128)S(1)} %get-tuple-element.35.refs_0_, ...), custom_call_target="tpu_custom_call" | custom-call | tf_op jit(solution)/shard_map/pallas_call | solution.py:168
  43.3 1.9 %collective-permute-start.8 = (f32[8,512]{1,0:T(8,128)S(1)}, f32[8,512]{1,0:T(8,128)S(1)}, u32[]{:S(2)}, u32[]{:S(2)}) collective-permute-start(f32[8,512]{1,0:T(8,128)S(1)} %get-tuple-element.45), channel_id=1, source_target_pairs={{0,31},{3,4},{1,3},{2,0},{7,5},{4,6},{5,1},{6,2},{8,7},{11,12},{9,... | collective-permute-start | bytes 49160 | tf_op jit(solution)/shard_map/ppermute | solution.py:211
  45.2 0.0 collective-permute-start.9
  45.2 2.4 %shard_map.19.own_partner_ref = f32[8,1024]{1,0:T(8,128)S(1)} custom-call(bf16[1024,1024]{1,0:T(8,128)(2,1)S(1)} %get-tuple-element.29.unit_ref, bf16[1024,1024]{1,0:T(8,128)(2,1)S(1)} %get-tuple-element.30.partner_ref), custom_call_target="tpu_custom_call" | custom-call | tf_op jit(solution)/shard_map/pallas_call | solution.py:168
  47.6 0.0 collective-permute-done.8.cross_ref
  47.6 0.0 collective-permute-done.2.first_ref
  47.6 3.5 %collective-permute-done.9.ends_ref = f32[8,512]{1,0:T(8,128)S(1)} collective-permute-done((f32[8,512]{1,0:T(8,128)S(1)}, f32[8,512]{1,0:T(8,128)S(1)}, u32[]{:S(2)}, u32[]{:S(2)}) %collective-permute-start.9) | collective-permute-done | bytes 16416 | tf_op jit(solution)/shard_map/ppermute | solution.py:211
  51.1 0.0 collective-permute-done.7.rows_ref
  51.1 0.7 %shard_map.25 = f32[40,1024]{1,0:T(8,128)} custom-call(s32[1]{0:T(128)} %bitcast.role_ref, f32[8,1024]{1,0:T(8,128)S(1)} %get-tuple-element.28.own_ref, f32[8,1024]{1,0:T(8,128)S(1)} %shard_map.19.own_partner_ref, f32[8,1024]{1,0:T(8,128)S(1)} %get-tuple-element.31.own_far_ref, f32[8,1024]{1,0:T(8,128)S(1)} %collective-permute-done.2.first_ref, ...), custom_call_target="tpu_custom_call" | custom-call | tf_op jit(solution)/shard_map/pallas_call | solution.py:168
  (2 shorter events, 0.0 us)
Async XLA Ops:
  0.0 8.2 %copy-start = (bf16[1024,1024]{1,0:T(8,128)(2,1)S(1)}, bf16[1024,1024]{1,0:T(8,128)(2,1)}, u32[]{:S(2)}) copy-start(bf16[1024,1024]{1,0:T(8,128)(2,1)} %rows_ref) | copy-start | bytes 6291460
  0.0 6.1 %collective-permute-start = (bf16[1024,1024]{1,0:T(8,128)(2,1)}, bf16[1024,1024]{1,0:T(8,128)(2,1)S(1)}, u32[]{:S(2)}, u32[]{:S(2)}) collective-permute-start(bf16[1024,1024]{1,0:T(8,128)(2,1)} %rows_ref), channel_id=1, source_target_pairs={{0,2},{2,0},{1,3},{3,1},{4,6},{6,4},{5,7},{7,5},{8,10},{10,8},{9,1... | collective-permute-start | bytes 6291464 | tf_op jit(solution)/shard_map/ppermute | solution.py:211
  0.5 29.5 %collective-permute-start.1 = (bf16[1024,1024]{1,0:T(8,128)(2,1)}, bf16[1024,1024]{1,0:T(8,128)(2,1)S(1)}, u32[]{:S(2)}, u32[]{:S(2)}) collective-permute-start(bf16[1024,1024]{1,0:T(8,128)(2,1)} %rows_ref), channel_id=1, source_target_pairs={{1,0},{2,3},{3,5},{0,30},{5,4},{6,7},{7,9},{4,2},{9,8},{10,11},{11... | collective-permute-start | bytes 6291464 | tf_op jit(solution)/shard_map/ppermute | solution.py:211
  6.8 28.7 %collective-permute-start.6 = (bf16[256,1024]{1,0:T(8,128)(2,1)S(1)}, bf16[256,1024]{1,0:T(8,128)(2,1)S(1)}, u32[]{:S(2)}, u32[]{:S(2)}) collective-permute-start(bf16[256,1024]{1,0:T(8,128)(2,1)S(1)} %get-tuple-element.41), channel_id=1, source_target_pairs={{5,6},{6,5},{13,14},{14,13},{21,22},{22,21},{29,30},{30,29}} | collective-permute-start | bytes 1572872 | tf_op jit(solution)/shard_map/ppermute | solution.py:211
  7.5 28.0 %collective-permute-start.5 = (bf16[256,1024]{1,0:T(8,128)(2,1)S(1)}, bf16[256,1024]{1,0:T(8,128)(2,1)S(1)}, u32[]{:S(2)}, u32[]{:S(2)}) collective-permute-start(bf16[256,1024]{1,0:T(8,128)(2,1)S(1)} %get-tuple-element.38), channel_id=1, source_target_pairs={{5,6},{6,5},{13,14},{14,13},{21,22},{22,21},{29,30},{30,29}} | collective-permute-start | bytes 1572872 | tf_op jit(solution)/shard_map/ppermute | solution.py:211
  11.1 27.4 %collective-permute-start.4 = (bf16[256,1024]{1,0:T(8,128)(2,1)S(1)}, bf16[256,1024]{1,0:T(8,128)(2,1)S(1)}, u32[]{:S(2)}, u32[]{:S(2)}) collective-permute-start(bf16[256,1024]{1,0:T(8,128)(2,1)S(1)} %get-tuple-element.34), channel_id=1, source_target_pairs={{7,8},{4,3},{15,16},{12,11},{23,24},{20,19},{31,0},{28,27}} | collective-permute-start | bytes 1572872 | tf_op jit(solution)/shard_map/ppermute | solution.py:211
  12.4 30.0 %collective-permute-start.3 = (bf16[256,1024]{1,0:T(8,128)(2,1)S(1)}, bf16[256,1024]{1,0:T(8,128)(2,1)S(1)}, u32[]{:S(2)}, u32[]{:S(2)}) collective-permute-start(bf16[256,1024]{1,0:T(8,128)(2,1)S(1)} %get-tuple-element.33), channel_id=1, source_target_pairs={{7,8},{4,3},{15,16},{12,11},{23,24},{20,19},{31,0},{28,27}} | collective-permute-start | bytes 1572872 | tf_op jit(solution)/shard_map/ppermute | solution.py:211
  35.4 12.2 %collective-permute-start.2 = (f32[8,1024]{1,0:T(8,128)S(1)}, f32[8,1024]{1,0:T(8,128)S(1)}, u32[]{:S(2)}, u32[]{:S(2)}) collective-permute-start(f32[8,1024]{1,0:T(8,128)S(1)} %get-tuple-element.32), channel_id=1, source_target_pairs={{1,31},{2,4},{0,2},{3,1},{5,3},{6,8},{4,6},{7,5},{9,7},{10,12},{8,... | collective-permute-start | bytes 98312 | tf_op jit(solution)/shard_map/ppermute | solution.py:211
  35.6 15.5 %collective-permute-start.7 = (f32[8,1024]{1,0:T(8,128)S(1)}, f32[8,1024]{1,0:T(8,128)S(1)}, u32[]{:S(2)}, u32[]{:S(2)}) collective-permute-start(f32[8,1024]{1,0:T(8,128)S(1)} %get-tuple-element.44), channel_id=1, source_target_pairs={{0,1},{3,2},{1,3},{2,0},{4,5},{7,6},{5,4},{6,7},{8,9},{11,10},{9,1... | collective-permute-start | bytes 98312 | tf_op jit(solution)/shard_map/ppermute | solution.py:211
  43.3 4.3 %collective-permute-start.8 = (f32[8,512]{1,0:T(8,128)S(1)}, f32[8,512]{1,0:T(8,128)S(1)}, u32[]{:S(2)}, u32[]{:S(2)}) collective-permute-start(f32[8,512]{1,0:T(8,128)S(1)} %get-tuple-element.45), channel_id=1, source_target_pairs={{0,31},{3,4},{1,3},{2,0},{7,5},{4,6},{5,1},{6,2},{8,7},{11,12},{9,... | collective-permute-start | bytes 49160 | tf_op jit(solution)/shard_map/ppermute | solution.py:211
  45.2 5.9 %collective-permute-start.9 = (f32[8,512]{1,0:T(8,128)S(1)}, f32[8,512]{1,0:T(8,128)S(1)}, u32[]{:S(2)}, u32[]{:S(2)}) collective-permute-start(f32[8,512]{1,0:T(8,128)S(1)} %get-tuple-element.46), channel_id=1, source_target_pairs={{3,1},{0,2},{1,5},{2,6},{5,3},{6,8},{4,7},{7,4},{11,9},{8,10},{9,1... | collective-permute-start | bytes 49160 | tf_op jit(solution)/shard_map/ppermute | solution.py:211
